TPU v7x, 128 devices: a whole 4x4x4 slice. The times are simulated.
128 devices in a mesh: lat: 8 (over x, core), lon: 4 (over y), lev: 4 (over z).
Axes of the slice: x: 4, y: 4, z: 4, core: 2. Of those that a mesh axis runs over, the one named last changes fastest.
Arguments:
- initial_state: float32 [32, 384, 128, 128], P('lat', 'lon', 'lev'), may hold values from 0.5 to 2
- scaled_wind_north: float32 [32, 384, 128, 128], P('lat', 'lon', 'lev'), may hold values from -0.3 to 0.3
- scaled_wind_east: float32 [32, 384, 128, 128], P('lat', 'lon', 'lev'), may hold values from -0.3 to 0.3
- scaled_wind_upward: float32 [32, 384, 128, 128], P('lat', 'lon', 'lev'), may hold values from -0.3 to 0.3
Outputs:
- normalised_state: float32 [32, 384, 128, 128], P('lat', 'lon', 'lev')
- temperature_end: float32 [32, 384, 128, 128], P('lat', 'lon', 'lev')
All inputs are finite; a program needn't handle non-finite values.
Results may differ from a plain program's by a relative error of at most 0.00002.
Values sent between devices are 32-bit elements; how exact they have to be, the bound alone decides.
No kernel may reach another device: no remote copies, remote signals or barrier semaphores. Data moves between devices by JAX's collectives and lax.ppermute only.
A program may use at most 128 MiB of HBM per device.

v0:
```python
import jax
import jax.numpy as jnp
from jax import lax
from jax.sharding import PartitionSpec as P

STEPS = 4


def padded(array, sides, width):
    edges = {}
    for axis, dim in sides:
        count, length = (lax.axis_size(axis), array.shape[dim])
        up = [(i, (i + 1) % count) for i in range(count - 1)]
        last = lax.slice_in_dim(array, length - width, length, axis=dim)
        initial = lax.slice_in_dim(array, 0, width, axis=dim)
        edges[dim] = (
            lax.ppermute(last, axis, up),
            lax.ppermute(initial, axis, [(b, a) for a, b in up]),
        )
    done = []
    for _, dim in sides:
        low, high = edges[dim]
        around = [(width, width) if d in done else (0, 0) for d in range(array.ndim)]
        array = jnp.concatenate([jnp.pad(low, around), array, jnp.pad(high, around)], axis=dim)
        done.append(dim)
    return array


def copy_for_each(array, axis):
    copies = jnp.broadcast_to(array, (lax.axis_size(axis), *array.shape))
    return lax.all_to_all(copies, axis, split_axis=0, concat_axis=0, tiled=True)


def over_copies(array, axis):
    return copy_for_each(array, axis).sum(axis=0)


def together(arrays, axis):
    ends = [0]
    for a in arrays:
        ends.append(ends[-1] + a.size)
    subtotal = over_copies(jnp.concatenate([a.ravel() for a in arrays]), axis)
    return tuple((subtotal[b:e].reshape(a.shape) for a, b, e in zip(arrays, ends, ends[1:])))


def strip_edges(values, dims):
    for dim in dims:
        values = lax.slice_in_dim(values, 1, values.shape[dim] - 1, axis=dim)
    return values


def neighbour(values, dim, start, dims):
    others = [other for other in dims if other != dim]
    values = strip_edges(values, others)
    return lax.slice_in_dim(values, start, start + values.shape[dim] - 2, axis=dim)


def march_one_step(padded_state, scaled_wind_north, scaled_wind_east, scaled_wind_upward):
    middle = strip_edges(padded_state, (0, 1, 2))
    lower = [neighbour(padded_state, dim, 0, (0, 1, 2)) for dim in (0, 1, 2)]
    upper = [neighbour(padded_state, dim, 2, (0, 1, 2)) for dim in (0, 1, 2)]
    slopes = [above - below for above, below in zip(upper, lower)]
    smooth_rate = 0.05
    spread = lower[0] + upper[0] + lower[1] + upper[1] + lower[2] + upper[2] - 6.0 * middle
    return (
        middle
        - scaled_wind_north * slopes[0]
        - scaled_wind_east * slopes[1]
        - scaled_wind_upward * slopes[2]
        + smooth_rate * spread
    )


def shards(initial_state, scaled_wind_north, scaled_wind_east, scaled_wind_upward):
    for step in range(STEPS):
        padded_state = padded(initial_state, (("lat", 0), ("lon", 1), ("lev", 2)), 1)
        initial_state = march_one_step(
            padded_state, scaled_wind_north, scaled_wind_east, scaled_wind_upward
        )
    number_of_values = initial_state.shape[1] * lax.axis_size("lon")
    guess = 1.0
    moved = initial_state - guess
    totals, squares = together(
        (jnp.sum(moved, axis=1, keepdims=True), jnp.sum(moved * moved, axis=1, keepdims=True)),
        "lon",
    )
    vertical_mean = guess + totals / number_of_values
    symmetric_slope = initial_state - vertical_mean
    line_variance = squares / number_of_values - totals / number_of_values * (
        totals / number_of_values
    )
    normalised_state = symmetric_slope * lax.rsqrt(line_variance + 0.0001)
    return (normalised_state, initial_state)


def solution(mesh):
    return jax.shard_map(
        shards,
        mesh=mesh,
        in_specs=(
            P("lat", "lon", "lev", None),
            P("lat", "lon", "lev", None),
            P("lat", "lon", "lev", None),
            P("lat", "lon", "lev", None),
        ),
        out_specs=(P("lat", "lon", "lev", None), P("lat", "lon", "lev", None)),
        check_vma=False,
    )
```

profile of v0, /device:TPU:14, one launch (start us, length us, event | category | flops | bytes accessed | tf_op | source)
XLA Modules:
  0.0 268.8 jit_solution(3711400979713692046)
XLA Ops:
  0.6 6.4 %copy.61 = f32[4,96,32,128]{3,1,2,0:T(8,128)S(1)} copy(f32[4,96,32,128]{3,2,1,0:T(8,128)} %param.4) | data formatting | bytes 12582912 | tf_op args[0]
  7.1 1.3 fusion.23
  8.4 2.3 collective-permute-start.1
  10.7 3.6 %collective-permute-start = (f32[1,96,32,128]{3,1,2,0:T(8,128)}, f32[1,96,32,128]{3,1,2,0:T(8,128)}, u32[]{:S(2)}, u32[]{:S(2)}) collective-permute-start(f32[1,96,32,128]{3,1,2,0:T(8,128)} %get-tuple-element.33), channel_id=1, source_target_pairs={{16,0},{32,16},{48,32},{64,48},{80,64},{96,80},{112,96},{17,1},{33... | collective-permute-start | bytes 4718600 | tf_op jit(solution)/shard_map/ppermute | solution.py:18
  14.4 2.4 collective-permute-start.2
  16.8 3.5 %collective-permute-start.3 = (f32[4,1,32,128]{3,1,2,0:T(1,128)S(1)}, f32[4,1,32,128]{3,1,2,0:T(1,128)S(1)}, u32[]{:S(2)}, u32[]{:S(2)}) collective-permute-start(f32[4,1,32,128]{3,1,2,0:T(1,128)S(1)} %bitcast.14), channel_id=1, source_target_pairs={{0,4},{4,8},{8,12},{1,5},{5,9},{9,13},{2,6},{6,10},{10,14},{3,7},{... | collective-permute-start | bytes 196616 | tf_op jit(solution)/shard_map/ppermute | solution.py:17
  20.3 0.8 fusion.21
  21.1 1.3 collective-permute-start.4
  22.4 5.4 %collective-permute-start.5 = (f32[4,96,1,128]{3,1,2,0:T(8,128)}, f32[4,96,1,128]{3,1,2,0:T(8,128)}, u32[]{:S(2)}, u32[]{:S(2)}) collective-permute-start(f32[4,96,1,128]{3,1,2,0:T(8,128)} %get-tuple-element.29), channel_id=1, source_target_pairs={{0,1},{1,2},{2,3},{4,5},{5,6},{6,7},{8,9},{9,10},{10,11},{12,13},{... | collective-permute-start | bytes 589832 | tf_op jit(solution)/shard_map/ppermute | solution.py:17
  27.8 0.1 pad.50
  27.8 0.1 pad.51
  27.9 2.7 collective-permute-done.1
  30.6 1.2 copy-done.3
  31.8 1.3 constant_dynamic-update-slice_fusion.2
  33.1 6.8 %constant_dynamic-update-slice_fusion.1 = f32[6,96,32,128]{3,1,2,0:T(8,128)} fusion(f32[6,96,32,128]{3,1,2,0:T(8,128)} %constant_dynamic-update-slice_fusion.2, f32[4,96,32,128]{3,2,1,0:T(8,128)S(1)} %copy-done.2), kind=kLoop, calls=%fused_computation.89 | loop fusion | bytes 12582912
  39.9 2.9 %constant_dynamic-update-slice_fusion = f32[6,96,32,128]{3,1,2,0:T(8,128)} fusion(f32[6,96,32,128]{3,1,2,0:T(8,128)} %constant_dynamic-update-slice_fusion.1, f32[1,96,32,128]{3,1,2,0:T(8,128)} %collective-permute-done), kind=kLoop, calls=%fused_computation.88 | loop fusion | bytes 3145728 | tf_op jit(solution)/shard_map/concatenate | solution.py:24
  42.8 29.4 %multiply_add_fusion.3 = f32[4,96,32,128]{3,1,2,0:T(8,128)} fusion(f32[4,96,32,128]{3,1,2,0:T(8,128)} %copy-done.1, f32[4,96,1,128]{3,1,2,0:T(8,128)S(1)} %collective-permute-done.4, f32[6,1,32,128]{3,1,2,0:T(1,128)S(1)} %pad.50, f32[6,96,32,128]{3,1,2,0:T(8,128)} %constant_dynamic-update-slice_fusion, f32[6,1,32,128]{3,1,2,0:T(1,128)S(1)} %pad.51, ...), kind=kLoop, calls=%fused_computation.79 | loop fusion | flops 53477376 | bytes 44630016 | tf_op jit(solution)/shard_map/add | solution.py:66
  72.2 2.1 fusion.20
  74.3 1.9 collective-permute-start.6
  76.2 3.6 %collective-permute-start.7 = (f32[1,96,32,128]{3,1,2,0:T(8,128)S(1)}, f32[1,96,32,128]{3,1,2,0:T(8,128)}, u32[]{:S(2)}, u32[]{:S(2)}) collective-permute-start(f32[1,96,32,128]{3,1,2,0:T(8,128)S(1)} %get-tuple-element.27), channel_id=1, source_target_pairs={{0,16},{16,32},{32,48},{48,64},{64,80},{80,96},{96,112},{1,17},{17... | collective-permute-start | bytes 4718600 | tf_op jit(solution)/shard_map/ppermute | solution.py:17
  79.8 1.1 fusion.18
  80.9 1.3 collective-permute-start.10
  82.2 4.6 %collective-permute-start.11 = (f32[4,96,1,128]{3,1,2,0:T(8,128)S(1)}, f32[4,96,1,128]{3,1,2,0:T(8,128)S(1)}, u32[]{:S(2)}, u32[]{:S(2)}) collective-permute-start(f32[4,96,1,128]{3,1,2,0:T(8,128)S(1)} %get-tuple-element.23), channel_id=1, source_target_pairs={{0,1},{1,2},{2,3},{4,5},{5,6},{6,7},{8,9},{9,10},{10,11},{12,13},{... | collective-permute-start | bytes 589832 | tf_op jit(solution)/shard_map/ppermute | solution.py:17
  86.7 1.3 fusion.19
  88.0 2.4 collective-permute-start.8
  90.4 3.8 %collective-permute-done.8 = f32[4,1,32,128]{3,1,2,0:T(1,128)S(1)} collective-permute-done((f32[4,1,32,128]{3,1,2,0:T(1,128)S(1)}, f32[4,1,32,128]{3,1,2,0:T(1,128)S(1)}, u32[]{:S(2)}, u32[]{:S(2)}) %collective-permute-start.8) | collective-permute-done | bytes 65568 | tf_op jit(solution)/shard_map/ppermute | solution.py:18
  94.2 3.7 %collective-permute-start.9 = (f32[4,1,32,128]{3,1,2,0:T(1,128)S(1)}, f32[4,1,32,128]{3,1,2,0:T(1,128)S(1)}, u32[]{:S(2)}, u32[]{:S(2)}) collective-permute-start(f32[4,1,32,128]{3,1,2,0:T(1,128)S(1)} %get-tuple-element.25), channel_id=1, source_target_pairs={{0,4},{4,8},{8,12},{1,5},{5,9},{9,13},{2,6},{6,10},{10,14},{3,7},{... | collective-permute-start | bytes 196616 | tf_op jit(solution)/shard_map/ppermute | solution.py:17
  97.9 0.1 pad.54
  98.0 2.4 collective-permute-done.9
  100.5 0.7 copy-done.6
  101.1 26.5 %multiply_add_fusion.2 = f32[4,96,32,128]{3,1,2,0:T(8,128)} fusion(f32[4,96,32,128]{3,1,2,0:T(8,128)} %multiply_add_fusion.3, f32[4,96,1,128]{3,1,2,0:T(8,128)S(1)} %collective-permute-done.10, f32[6,1,32,128]{3,1,2,0:T(1,128)S(1)} %pad.54, f32[1,96,32,128]{3,1,2,0:T(8,128)} %collective-permute-done.6, f32[1,96,32,128]{3,1,2,0:T(8,128)} %collective-permute-done.7, ...), kind=kLoop, calls=%fused_computation.78 | loop fusion | flops 66060288 | bytes 35192832 | tf_op jit(solution)/shard_map/add | solution.py:66
  127.6 2.1 fusion.17
  129.7 1.9 collective-permute-start.12
  131.6 3.6 %collective-permute-start.13 = (f32[1,96,32,128]{3,1,2,0:T(8,128)S(1)}, f32[1,96,32,128]{3,1,2,0:T(8,128)}, u32[]{:S(2)}, u32[]{:S(2)}) collective-permute-start(f32[1,96,32,128]{3,1,2,0:T(8,128)S(1)} %get-tuple-element.21), channel_id=1, source_target_pairs={{0,16},{16,32},{32,48},{48,64},{64,80},{80,96},{96,112},{1,17},{17... | collective-permute-start | bytes 4718600 | tf_op jit(solution)/shard_map/ppermute | solution.py:17
  135.2 1.1 fusion.15
  136.2 1.3 collective-permute-start.16
  137.5 4.6 %collective-permute-start.17 = (f32[4,96,1,128]{3,1,2,0:T(8,128)S(1)}, f32[4,96,1,128]{3,1,2,0:T(8,128)S(1)}, u32[]{:S(2)}, u32[]{:S(2)}) collective-permute-start(f32[4,96,1,128]{3,1,2,0:T(8,128)S(1)} %get-tuple-element.17), channel_id=1, source_target_pairs={{0,1},{1,2},{2,3},{4,5},{5,6},{6,7},{8,9},{9,10},{10,11},{12,13},{... | collective-permute-start | bytes 589832 | tf_op jit(solution)/shard_map/ppermute | solution.py:17
  142.1 1.3 fusion.16
  143.4 1.9 collective-permute-start.14
  145.3 4.2 %collective-permute-done.14 = f32[4,1,32,128]{3,1,2,0:T(1,128)S(1)} collective-permute-done((f32[4,1,32,128]{3,1,2,0:T(1,128)S(1)}, f32[4,1,32,128]{3,1,2,0:T(1,128)S(1)}, u32[]{:S(2)}, u32[]{:S(2)}) %collective-permute-start.14) | collective-permute-done | bytes 65568 | tf_op jit(solution)/shard_map/ppermute | solution.py:18
  149.6 3.5 %collective-permute-start.15 = (f32[4,1,32,128]{3,1,2,0:T(1,128)S(1)}, f32[4,1,32,128]{3,1,2,0:T(1,128)S(1)}, u32[]{:S(2)}, u32[]{:S(2)}) collective-permute-start(f32[4,1,32,128]{3,1,2,0:T(1,128)S(1)} %get-tuple-element.19), channel_id=1, source_target_pairs={{0,4},{4,8},{8,12},{1,5},{5,9},{9,13},{2,6},{6,10},{10,14},{3,7},{... | collective-permute-start | bytes 196616 | tf_op jit(solution)/shard_map/ppermute | solution.py:17
  153.1 0.1 pad.58
  153.1 2.6 collective-permute-done.15
  155.8 0.7 copy-done.7
  156.5 25.8 %multiply_add_fusion.1 = f32[4,96,32,128]{3,1,2,0:T(8,128)} fusion(f32[4,96,32,128]{3,1,2,0:T(8,128)} %multiply_add_fusion.2, f32[4,96,1,128]{3,1,2,0:T(8,128)S(1)} %collective-permute-done.16, f32[6,1,32,128]{3,1,2,0:T(1,128)S(1)} %pad.58, f32[1,96,32,128]{3,1,2,0:T(8,128)} %collective-permute-done.12, f32[1,96,32,128]{3,1,2,0:T(8,128)} %collective-permute-done.13, ...), kind=kLoop, calls=%fused_computation.77 | loop fusion | flops 66060288 | bytes 35192832 | tf_op jit(solution)/shard_map/add | solution.py:66
  182.3 2.1 fusion.14
  184.4 1.9 collective-permute-start.18
  186.3 3.6 %collective-permute-start.19 = (f32[1,96,32,128]{3,1,2,0:T(8,128)S(1)}, f32[1,96,32,128]{3,1,2,0:T(8,128)}, u32[]{:S(2)}, u32[]{:S(2)}) collective-permute-start(f32[1,96,32,128]{3,1,2,0:T(8,128)S(1)} %get-tuple-element.15), channel_id=1, source_target_pairs={{0,16},{16,32},{32,48},{48,64},{64,80},{80,96},{96,112},{1,17},{17... | collective-permute-start | bytes 4718600 | tf_op jit(solution)/shard_map/ppermute | solution.py:17
  189.9 1.1 fusion.12
  190.9 1.3 collective-permute-start.22
  192.2 4.6 %collective-permute-start.23 = (f32[4,96,1,128]{3,1,2,0:T(8,128)S(1)}, f32[4,96,1,128]{3,1,2,0:T(8,128)S(1)}, u32[]{:S(2)}, u32[]{:S(2)}) collective-permute-start(f32[4,96,1,128]{3,1,2,0:T(8,128)S(1)} %get-tuple-element.12), channel_id=1, source_target_pairs={{0,1},{1,2},{2,3},{4,5},{5,6},{6,7},{8,9},{9,10},{10,11},{12,13},{... | collective-permute-start | bytes 589832 | tf_op jit(solution)/shard_map/ppermute | solution.py:17
  196.8 1.3 fusion.13
  198.1 1.9 collective-permute-start.20
  200.0 4.2 %collective-permute-done.20 = f32[4,1,32,128]{3,1,2,0:T(1,128)S(1)} collective-permute-done((f32[4,1,32,128]{3,1,2,0:T(1,128)S(1)}, f32[4,1,32,128]{3,1,2,0:T(1,128)S(1)}, u32[]{:S(2)}, u32[]{:S(2)}) %collective-permute-start.20) | collective-permute-done | bytes 65568 | tf_op jit(solution)/shard_map/ppermute | solution.py:18
  204.3 3.7 %collective-permute-start.21 = (f32[4,1,32,128]{3,1,2,0:T(1,128)S(1)}, f32[4,1,32,128]{3,1,2,0:T(1,128)S(1)}, u32[]{:S(2)}, u32[]{:S(2)}) collective-permute-start(f32[4,1,32,128]{3,1,2,0:T(1,128)S(1)} %get-tuple-element.13), channel_id=1, source_target_pairs={{0,4},{4,8},{8,12},{1,5},{5,9},{9,13},{2,6},{6,10},{10,14},{3,7},{... | collective-permute-start | bytes 196616 | tf_op jit(solution)/shard_map/ppermute | solution.py:17
  208.1 2.3 collective-permute-done.21
  210.5 0.6 copy-done.4
  211.2 31.1 %add_reduce_fusion = (f32[4,32,128]{2,1,0:T(8,128)S(1)}, f32[4,32,128]{2,1,0:T(8,128)S(1)}, f32[4,96,32,128]{3,1,2,0:T(8,128)}) fusion(f32[4,96,32,128]{3,1,2,0:T(8,128)} %multiply_add_fusion.1, f32[6,1,32,128]{3,1,2,0:T(1,128)S(1)} %pad.62, f32[1,96,32,128]{3,1,2,0:T(8,128)} %collective-permute-done.18, f32[1,96,32,128]{3,1,2,0:T(8,128)} %collective-permute-done.19, ...), kind=kLoop, calls=%fused_computation.80 | loop fusion | flops 72318976 | bytes 35323904 | tf_op jit(solution)/shard_map/reduce_sum | solution.py:84
  242.4 1.1 broadcast_in_dim.3
  243.4 4.9 %all-to-all-start = ((f32[4,1,32768]{2,1,0:T(1,128)}), f32[4,1,32768]{2,1,0:T(1,128)S(1)}, u32[]{:S(2)}, u32[]{:S(2)}) async-start(f32[4,1,32768]{2,1,0:T(1,128)} %broadcast_in_dim.3), calls=%async_computation | async-start | bytes 1048576 | tf_op jit(solution)/shard_map/all_to_all | solution.py:31
  248.3 9.1 %copy.81 = f32[4,96,32,128]{3,2,1,0:T(8,128)} copy(f32[4,96,32,128]{3,1,2,0:T(8,128)} %get-tuple-element.10) | data formatting | bytes 12582912
  257.5 0.5 reduce_sum.29
  258.0 4.0 %subtract_multiply_fusion = f32[4,96,32,128]{3,1,2,0:T(8,128)S(1)} fusion(f32[4,96,32,128]{3,1,2,0:T(8,128)} %get-tuple-element.10, f32[4,32,128]{2,1,0:T(8,128)S(1)} %bitcast.13, f32[4,32,128]{2,1,0:T(8,128)S(1)} %bitcast.12), kind=kLoop, calls=%fused_computation.74 | loop fusion | flops 3145728 | bytes 12713984 | tf_op jit(solution)/shard_map/mul | solution.py:92
  262.0 6.3 %copy.80 = f32[4,96,32,128]{3,2,1,0:T(8,128)} copy(f32[4,96,32,128]{3,1,2,0:T(8,128)S(1)} %subtract_multiply_fusion) | data formatting | bytes 12582912
  (47 shorter events, 0.4 us)
Async XLA Ops:
  7.1 32.9 %copy-start.1 = (f32[4,96,32,128]{3,1,2,0:T(8,128)}, f32[4,96,32,128]{3,1,2,0:T(8,128)S(1)}, u32[]{:S(2)}) copy-start(f32[4,96,32,128]{3,1,2,0:T(8,128)S(1)} %copy.61) | copy-start | bytes 18874372
  7.1 7.3 %copy-start.2 = (f32[4,96,32,128]{3,2,1,0:T(8,128)S(1)}, f32[4,96,32,128]{3,2,1,0:T(8,128)}, u32[]{:S(2)}) copy-start(f32[4,96,32,128]{3,2,1,0:T(8,128)} %param.4) | copy-start | bytes 18874372
  8.4 22.1 %collective-permute-start.1 = (f32[1,96,32,128]{3,1,2,0:T(8,128)S(1)}, f32[1,96,32,128]{3,1,2,0:T(8,128)S(1)}, u32[]{:S(2)}, u32[]{:S(2)}) collective-permute-start(f32[1,96,32,128]{3,1,2,0:T(8,128)S(1)} %get-tuple-element.34), channel_id=1, source_target_pairs={{0,16},{16,32},{32,48},{48,64},{64,80},{80,96},{96,112},{1,17},{17... | collective-permute-start | bytes 4718600 | tf_op jit(solution)/shard_map/ppermute | solution.py:17
  10.7 29.2 %collective-permute-start = (f32[1,96,32,128]{3,1,2,0:T(8,128)}, f32[1,96,32,128]{3,1,2,0:T(8,128)}, u32[]{:S(2)}, u32[]{:S(2)}) collective-permute-start(f32[1,96,32,128]{3,1,2,0:T(8,128)} %get-tuple-element.33), channel_id=1, source_target_pairs={{16,0},{32,16},{48,32},{64,48},{80,64},{96,80},{112,96},{17,1},{33... | collective-permute-start | bytes 4718600 | tf_op jit(solution)/shard_map/ppermute | solution.py:18
  14.4 7.9 %collective-permute-start.2 = (f32[4,1,32,128]{3,1,2,0:T(1,128)S(1)}, f32[4,1,32,128]{3,1,2,0:T(1,128)S(1)}, u32[]{:S(2)}, u32[]{:S(2)}) collective-permute-start(f32[4,1,32,128]{3,1,2,0:T(1,128)S(1)} %bitcast.15), channel_id=1, source_target_pairs={{4,0},{8,4},{12,8},{5,1},{9,5},{13,9},{6,2},{10,6},{14,10},{7,3},{... | collective-permute-start | bytes 196616 | tf_op jit(solution)/shard_map/ppermute | solution.py:18
  16.8 11.0 %collective-permute-start.3 = (f32[4,1,32,128]{3,1,2,0:T(1,128)S(1)}, f32[4,1,32,128]{3,1,2,0:T(1,128)S(1)}, u32[]{:S(2)}, u32[]{:S(2)}) collective-permute-start(f32[4,1,32,128]{3,1,2,0:T(1,128)S(1)} %bitcast.14), channel_id=1, source_target_pairs={{0,4},{4,8},{8,12},{1,5},{5,9},{9,13},{2,6},{6,10},{10,14},{3,7},{... | collective-permute-start | bytes 196616 | tf_op jit(solution)/shard_map/ppermute | solution.py:17
  21.1 21.7 %collective-permute-start.4 = (f32[4,96,1,128]{3,1,2,0:T(8,128)}, f32[4,96,1,128]{3,1,2,0:T(8,128)S(1)}, u32[]{:S(2)}, u32[]{:S(2)}) collective-permute-start(f32[4,96,1,128]{3,1,2,0:T(8,128)} %get-tuple-element.30), channel_id=1, source_target_pairs={{1,0},{2,1},{3,2},{5,4},{6,5},{7,6},{9,8},{10,9},{11,10},{13,12},{... | collective-permute-start | bytes 589832 | tf_op jit(solution)/shard_map/ppermute | solution.py:18
  22.4 20.4 %collective-permute-start.5 = (f32[4,96,1,128]{3,1,2,0:T(8,128)}, f32[4,96,1,128]{3,1,2,0:T(8,128)}, u32[]{:S(2)}, u32[]{:S(2)}) collective-permute-start(f32[4,96,1,128]{3,1,2,0:T(8,128)} %get-tuple-element.29), channel_id=1, source_target_pairs={{0,1},{1,2},{2,3},{4,5},{5,6},{6,7},{8,9},{9,10},{10,11},{12,13},{... | collective-permute-start | bytes 589832 | tf_op jit(solution)/shard_map/ppermute | solution.py:17
  30.5 1.2 copy-start.3
  31.8 11.0 %slice-start = ((s8[6291456]{0:T(1024)(128)(4,1)}), s8[4194304]{0:T(1024)(128)(4,1)S(1)}, s32[]{:S(2)}) async-start(s8[6291456]{0:T(1024)(128)(4,1)} %bitcast.6), calls=%async_computation.1 | async-start | bytes 8388608
  31.8 11.0 %slice-start.2 = ((s8[6291456]{0:T(1024)(128)(4,1)}), s8[4194304]{0:T(1024)(128)(4,1)S(1)}, s32[]{:S(2)}) async-start(s8[6291456]{0:T(1024)(128)(4,1)} %bitcast.8), calls=%async_computation.3 | async-start | bytes 8388608
  33.1 9.7 %slice-start.1 = ((s8[6291456]{0:T(1024)(128)(4,1)}), s8[2097152]{0:T(1024)(128)(4,1)S(1)}, s32[]{:S(2)}) async-start(s8[6291456]{0:T(1024)(128)(4,1)} %bitcast.6), calls=%async_computation.2 | async-start | bytes 4194304
  33.1 9.7 %slice-start.3 = ((s8[6291456]{0:T(1024)(128)(4,1)}), s8[2097152]{0:T(1024)(128)(4,1)S(1)}, s32[]{:S(2)}) async-start(s8[6291456]{0:T(1024)(128)(4,1)} %bitcast.8), calls=%async_computation.4 | async-start | bytes 4194304
  33.1 9.7 %copy-start = (f32[4,96,32,128]{3,2,1,0:T(8,128)S(1)}, f32[4,96,32,128]{3,2,1,0:T(8,128)}, u32[]{:S(2)}) copy-start(f32[4,96,32,128]{3,2,1,0:T(8,128)} %param.5) | copy-start | bytes 18874372
  74.3 26.1 %collective-permute-start.6 = (f32[1,96,32,128]{3,1,2,0:T(8,128)S(1)}, f32[1,96,32,128]{3,1,2,0:T(8,128)}, u32[]{:S(2)}, u32[]{:S(2)}) collective-permute-start(f32[1,96,32,128]{3,1,2,0:T(8,128)S(1)} %get-tuple-element.28), channel_id=1, source_target_pairs={{16,0},{32,16},{48,32},{64,48},{80,64},{96,80},{112,96},{17,1},{33... | collective-permute-start | bytes 4718600 | tf_op jit(solution)/shard_map/ppermute | solution.py:18
  76.2 24.9 %collective-permute-start.7 = (f32[1,96,32,128]{3,1,2,0:T(8,128)S(1)}, f32[1,96,32,128]{3,1,2,0:T(8,128)}, u32[]{:S(2)}, u32[]{:S(2)}) collective-permute-start(f32[1,96,32,128]{3,1,2,0:T(8,128)S(1)} %get-tuple-element.27), channel_id=1, source_target_pairs={{0,16},{16,32},{32,48},{48,64},{64,80},{80,96},{96,112},{1,17},{17... | collective-permute-start | bytes 4718600 | tf_op jit(solution)/shard_map/ppermute | solution.py:17
  80.9 19.5 %collective-permute-start.10 = (f32[4,96,1,128]{3,1,2,0:T(8,128)S(1)}, f32[4,96,1,128]{3,1,2,0:T(8,128)S(1)}, u32[]{:S(2)}, u32[]{:S(2)}) collective-permute-start(f32[4,96,1,128]{3,1,2,0:T(8,128)S(1)} %get-tuple-element.24), channel_id=1, source_target_pairs={{1,0},{2,1},{3,2},{5,4},{6,5},{7,6},{9,8},{10,9},{11,10},{13,12},{... | collective-permute-start | bytes 589832 | tf_op jit(solution)/shard_map/ppermute | solution.py:18
  82.2 18.3 %collective-permute-start.11 = (f32[4,96,1,128]{3,1,2,0:T(8,128)S(1)}, f32[4,96,1,128]{3,1,2,0:T(8,128)S(1)}, u32[]{:S(2)}, u32[]{:S(2)}) collective-permute-start(f32[4,96,1,128]{3,1,2,0:T(8,128)S(1)} %get-tuple-element.23), channel_id=1, source_target_pairs={{0,1},{1,2},{2,3},{4,5},{5,6},{6,7},{8,9},{9,10},{10,11},{12,13},{... | collective-permute-start | bytes 589832 | tf_op jit(solution)/shard_map/ppermute | solution.py:17
  88.0 6.2 %collective-permute-start.8 = (f32[4,1,32,128]{3,1,2,0:T(1,128)S(1)}, f32[4,1,32,128]{3,1,2,0:T(1,128)S(1)}, u32[]{:S(2)}, u32[]{:S(2)}) collective-permute-start(f32[4,1,32,128]{3,1,2,0:T(1,128)S(1)} %get-tuple-element.26), channel_id=1, source_target_pairs={{4,0},{8,4},{12,8},{5,1},{9,5},{13,9},{6,2},{10,6},{14,10},{7,3},{... | collective-permute-start | bytes 196616 | tf_op jit(solution)/shard_map/ppermute | solution.py:18
  94.2 6.1 %collective-permute-start.9 = (f32[4,1,32,128]{3,1,2,0:T(1,128)S(1)}, f32[4,1,32,128]{3,1,2,0:T(1,128)S(1)}, u32[]{:S(2)}, u32[]{:S(2)}) collective-permute-start(f32[4,1,32,128]{3,1,2,0:T(1,128)S(1)} %get-tuple-element.25), channel_id=1, source_target_pairs={{0,4},{4,8},{8,12},{1,5},{5,9},{9,13},{2,6},{6,10},{10,14},{3,7},{... | collective-permute-start | bytes 196616 | tf_op jit(solution)/shard_map/ppermute | solution.py:17
  100.4 0.7 copy-start.6
  129.7 26.1 %collective-permute-start.12 = (f32[1,96,32,128]{3,1,2,0:T(8,128)S(1)}, f32[1,96,32,128]{3,1,2,0:T(8,128)}, u32[]{:S(2)}, u32[]{:S(2)}) collective-permute-start(f32[1,96,32,128]{3,1,2,0:T(8,128)S(1)} %get-tuple-element.22), channel_id=1, source_target_pairs={{16,0},{32,16},{48,32},{64,48},{80,64},{96,80},{112,96},{17,1},{33... | collective-permute-start | bytes 4718600 | tf_op jit(solution)/shard_map/ppermute | solution.py:18
  131.6 24.9 %collective-permute-start.13 = (f32[1,96,32,128]{3,1,2,0:T(8,128)S(1)}, f32[1,96,32,128]{3,1,2,0:T(8,128)}, u32[]{:S(2)}, u32[]{:S(2)}) collective-permute-start(f32[1,96,32,128]{3,1,2,0:T(8,128)S(1)} %get-tuple-element.21), channel_id=1, source_target_pairs={{0,16},{16,32},{32,48},{48,64},{64,80},{80,96},{96,112},{1,17},{17... | collective-permute-start | bytes 4718600 | tf_op jit(solution)/shard_map/ppermute | solution.py:17
  136.2 19.5 %collective-permute-start.16 = (f32[4,96,1,128]{3,1,2,0:T(8,128)S(1)}, f32[4,96,1,128]{3,1,2,0:T(8,128)S(1)}, u32[]{:S(2)}, u32[]{:S(2)}) collective-permute-start(f32[4,96,1,128]{3,1,2,0:T(8,128)S(1)} %get-tuple-element.18), channel_id=1, source_target_pairs={{1,0},{2,1},{3,2},{5,4},{6,5},{7,6},{9,8},{10,9},{11,10},{13,12},{... | collective-permute-start | bytes 589832 | tf_op jit(solution)/shard_map/ppermute | solution.py:18
  137.5 18.3 %collective-permute-start.17 = (f32[4,96,1,128]{3,1,2,0:T(8,128)S(1)}, f32[4,96,1,128]{3,1,2,0:T(8,128)S(1)}, u32[]{:S(2)}, u32[]{:S(2)}) collective-permute-start(f32[4,96,1,128]{3,1,2,0:T(8,128)S(1)} %get-tuple-element.17), channel_id=1, source_target_pairs={{0,1},{1,2},{2,3},{4,5},{5,6},{6,7},{8,9},{9,10},{10,11},{12,13},{... | collective-permute-start | bytes 589832 | tf_op jit(solution)/shard_map/ppermute | solution.py:17
  143.4 6.2 %collective-permute-start.14 = (f32[4,1,32,128]{3,1,2,0:T(1,128)S(1)}, f32[4,1,32,128]{3,1,2,0:T(1,128)S(1)}, u32[]{:S(2)}, u32[]{:S(2)}) collective-permute-start(f32[4,1,32,128]{3,1,2,0:T(1,128)S(1)} %get-tuple-element.20), channel_id=1, source_target_pairs={{4,0},{8,4},{12,8},{5,1},{9,5},{13,9},{6,2},{10,6},{14,10},{7,3},{... | collective-permute-start | bytes 196616 | tf_op jit(solution)/shard_map/ppermute | solution.py:18
  149.6 6.1 %collective-permute-start.15 = (f32[4,1,32,128]{3,1,2,0:T(1,128)S(1)}, f32[4,1,32,128]{3,1,2,0:T(1,128)S(1)}, u32[]{:S(2)}, u32[]{:S(2)}) collective-permute-start(f32[4,1,32,128]{3,1,2,0:T(1,128)S(1)} %get-tuple-element.19), channel_id=1, source_target_pairs={{0,4},{4,8},{8,12},{1,5},{5,9},{9,13},{2,6},{6,10},{10,14},{3,7},{... | collective-permute-start | bytes 196616 | tf_op jit(solution)/shard_map/ppermute | solution.py:17
  155.8 0.7 copy-start.7
  184.4 26.2 %collective-permute-start.18 = (f32[1,96,32,128]{3,1,2,0:T(8,128)S(1)}, f32[1,96,32,128]{3,1,2,0:T(8,128)}, u32[]{:S(2)}, u32[]{:S(2)}) collective-permute-start(f32[1,96,32,128]{3,1,2,0:T(8,128)S(1)} %get-tuple-element.16), channel_id=1, source_target_pairs={{16,0},{32,16},{48,32},{64,48},{80,64},{96,80},{112,96},{17,1},{33... | collective-permute-start | bytes 4718600 | tf_op jit(solution)/shard_map/ppermute | solution.py:18
  186.3 24.9 %collective-permute-start.19 = (f32[1,96,32,128]{3,1,2,0:T(8,128)S(1)}, f32[1,96,32,128]{3,1,2,0:T(8,128)}, u32[]{:S(2)}, u32[]{:S(2)}) collective-permute-start(f32[1,96,32,128]{3,1,2,0:T(8,128)S(1)} %get-tuple-element.15), channel_id=1, source_target_pairs={{0,16},{16,32},{32,48},{48,64},{64,80},{80,96},{96,112},{1,17},{17... | collective-permute-start | bytes 4718600 | tf_op jit(solution)/shard_map/ppermute | solution.py:17
  190.9 19.5 %collective-permute-start.22 = (f32[4,96,1,128]{3,1,2,0:T(8,128)S(1)}, f32[4,96,1,128]{3,1,2,0:T(8,128)S(1)}, u32[]{:S(2)}, u32[]{:S(2)}) collective-permute-start(f32[4,96,1,128]{3,1,2,0:T(8,128)S(1)} %get-tuple-element.11), channel_id=1, source_target_pairs={{1,0},{2,1},{3,2},{5,4},{6,5},{7,6},{9,8},{10,9},{11,10},{13,12},{... | collective-permute-start | bytes 589832 | tf_op jit(solution)/shard_map/ppermute | solution.py:18
  192.2 18.3 %collective-permute-start.23 = (f32[4,96,1,128]{3,1,2,0:T(8,128)S(1)}, f32[4,96,1,128]{3,1,2,0:T(8,128)S(1)}, u32[]{:S(2)}, u32[]{:S(2)}) collective-permute-start(f32[4,96,1,128]{3,1,2,0:T(8,128)S(1)} %get-tuple-element.12), channel_id=1, source_target_pairs={{0,1},{1,2},{2,3},{4,5},{5,6},{6,7},{8,9},{9,10},{10,11},{12,13},{... | collective-permute-start | bytes 589832 | tf_op jit(solution)/shard_map/ppermute | solution.py:17
  198.1 6.2 %collective-permute-start.20 = (f32[4,1,32,128]{3,1,2,0:T(1,128)S(1)}, f32[4,1,32,128]{3,1,2,0:T(1,128)S(1)}, u32[]{:S(2)}, u32[]{:S(2)}) collective-permute-start(f32[4,1,32,128]{3,1,2,0:T(1,128)S(1)} %get-tuple-element.14), channel_id=1, source_target_pairs={{4,0},{8,4},{12,8},{5,1},{9,5},{13,9},{6,2},{10,6},{14,10},{7,3},{... | collective-permute-start | bytes 196616 | tf_op jit(solution)/shard_map/ppermute | solution.py:18
  204.3 6.1 %collective-permute-start.21 = (f32[4,1,32,128]{3,1,2,0:T(1,128)S(1)}, f32[4,1,32,128]{3,1,2,0:T(1,128)S(1)}, u32[]{:S(2)}, u32[]{:S(2)}) collective-permute-start(f32[4,1,32,128]{3,1,2,0:T(1,128)S(1)} %get-tuple-element.13), channel_id=1, source_target_pairs={{0,4},{4,8},{8,12},{1,5},{5,9},{9,13},{2,6},{6,10},{10,14},{3,7},{... | collective-permute-start | bytes 196616 | tf_op jit(solution)/shard_map/ppermute | solution.py:17
  210.5 0.7 copy-start.4
  210.5 0.7 copy-start.5
  243.4 14.0 %all-to-all-start = ((f32[4,1,32768]{2,1,0:T(1,128)}), f32[4,1,32768]{2,1,0:T(1,128)S(1)}, u32[]{:S(2)}, u32[]{:S(2)}) async-start(f32[4,1,32768]{2,1,0:T(1,128)} %broadcast_in_dim.3), calls=%async_computation | async-start | bytes 1048576 | tf_op jit(solution)/shard_map/all_to_all | solution.py:31
where the time goes:
time: 274 us; the launch traced here: 269 us
  other arithmetic  117 us (43%)
  starting transfers between devices  74.5 us (27%)
  local copies, waits for them, and re-layouts  53.2 us (19%)
  waiting for transfers between devices  22.3 us (8%)
    add x3, other arithmetic, march_one_step(): middle - scaled_wind_north * slopes[0] - scaled_wind_east * slopes[1]  81.6 us
    ppermute x12, starting transfers between devices, padded(): lax.ppermute(last, axis, up)  46.4 us
    unnamed x29, local copies, waits for them, and re-layouts  33.3 us
    reduce_sum x1, other arithmetic, shards(): jnp.sum(moved, axis=1, keepdims=True)  31.1 us
    ppermute x12, starting transfers between devices, padded(): lax.ppermute(initial, axis, [(b, a) for a, b in up])  23.1 us
    slice x10, local copies, waits for them, and re-layouts, padded(): last = lax.slice_in_dim(array, length - width, length, axis=dim)  13.1 us
    ppermute x12, waiting for transfers between devices, padded(): lax.ppermute(initial, axis, [(b, a) for a, b in up])  12.3 us
    ppermute x12, waiting for transfers between devices, padded(): lax.ppermute(last, axis, up)  10 us
  transfers between devices with their start and end apart: 25, of which 7 were waited for; matrix products, arithmetic and copies ran while one was open for 11% of the time, Pallas kernels for 0%

commit v1 on v0

v1 whole, which is shorter than its diff:
```python
import functools

import jax
import jax.numpy as jnp
from jax import lax
from jax.experimental import pallas as pl
from jax.experimental.pallas import tpu as pltpu
from jax.sharding import PartitionSpec as P


STEPS = 4
RATE = 0.05
GRID = P("lat", "lon", "lev", None)


def roles(odd):
    first = 3 * odd
    turn = 1 - 2 * odd
    sign = jnp.where(odd == 0, 1.0, -1.0).astype(jnp.float32)
    return [first + turn * k for k in range(4)], sign


def either(flag, a, b):
    return jnp.where(flag, a, b)


def take_outer(place, source, outer, sem):
    rows, _ = roles(place[0])
    copy = pltpu.make_async_copy(source.at[rows[0]], outer, sem)
    copy.start()
    copy.wait()


def take_others(place, source, outer, *refs):
    others, ends, sems = refs[:3], refs[3:7], refs[7]
    rows, _ = roles(place[0])
    even_lev, even_lon = place[1] == 0, place[2] == 0
    copies = [
        pltpu.make_async_copy(source.at[rows[k + 1]], others[k], sems.at[k]) for k in range(3)
    ]
    for copy in copies:
        copy.start()
    for k in range(4):
        if k > 0:
            copies[k - 1].wait()
        row = outer if k == 0 else others[k - 1]
        send_ends(k, row, ends, even_lev, even_lon)


def send_ends(k, row, ends, even_lev, even_lon):
    length, levels, _ = row.shape

    def body(x, carry):
        low, high = row[x, 0:1], row[x, levels - 1 : levels]
        ends[0][k, pl.ds(x, 1)] = either(even_lev, high, low)
        ends[1][k, pl.ds(x, 1)] = either(even_lev, low, high)
        return carry

    lax.fori_loop(0, length, body, 0, unroll=4)
    low, high = row[0], row[length - 1]
    ends[2][k] = either(even_lon, high, low)
    ends[3][k] = either(even_lon, low, high)


def spread_step(last, place, *refs):
    state, refs = refs[:4], refs[4:]
    core_row, near_lev, far_lev, near_lon, far_lon, north, east, upward = refs[:8]
    new = refs[8:12]
    extra = refs[12:]
    rows, sign = roles(place[0])
    length, levels, members = new[0].shape
    even_lev, even_lon = place[1] == 0, place[2] == 0
    level = lax.broadcasted_iota(jnp.int32, (levels, members), 0)
    for k in range(4):
        row = rows[k]
        inward = core_row if k == 3 else state[k + 1]
        outward = None if k == 0 else state[k - 1]

        def cell(x, before, here, after):
            lower = either(even_lev, far_lev[k, pl.ds(x, 1)], near_lev[k, pl.ds(x, 1)])
            upper = either(even_lev, near_lev[k, pl.ds(x, 1)], far_lev[k, pl.ds(x, 1)])
            down = jnp.where(level == 0, lower, pltpu.roll(here, 1, 0))
            up = jnp.where(level == levels - 1, upper, pltpu.roll(here, levels - 1, 0))
            inner = inward[x]
            total = (before + after) + (down + up)
            if outward is None:
                total += inner
                slope = inner
            else:
                outer = outward[x]
                total += inner + outer
                slope = inner - outer
            value = (
                (1.0 - 6.0 * RATE) * here
                + RATE * total
                - (sign * north[row, x]) * slope
                - east[row, x] * (after - before)
                - upward[row, x] * (up - down)
            )
            new[k][x] = value
            if not last and k > 0:
                low, high = value[0:1], value[levels - 1 : levels]
                extra[0][k, pl.ds(x, 1)] = either(even_lev, high, low)
                extra[1][k, pl.ds(x, 1)] = either(even_lev, low, high)
            return value

        start = either(even_lon, far_lon[k], near_lon[k])
        stop = either(even_lon, near_lon[k], far_lon[k])

        def body(x, carry):
            before, here, total = carry
            after = state[k][x + 1]
            value = cell(x, before, here, after)
            return here, after, (total + value if last else total)

        zero = jnp.zeros((levels, members), jnp.float32)
        before, here, total = lax.fori_loop(
            0, length - 1, body, (start, state[k][0], zero), unroll=5
        )
        value = cell(length - 1, before, here, stop)
        if not last and k > 0:
            low, high = new[k][0], value
            extra[2][k] = either(even_lon, high, low)
            extra[3][k] = either(even_lon, low, high)
        if last and k > 0:
            line_statistics(new[k], total + value, extra[0], 2 * (k - 1))


def line_statistics(row, total, out, at):
    length = row.shape[0]
    mean = total * (1.0 / length)

    def body(x, carry):
        away = row[x] - mean
        return carry + away * away

    out[at] = mean
    out[at + 1] = lax.fori_loop(0, length, body, jnp.zeros_like(mean), unroll=4)


def finish_row(last, place, *refs):
    part, north, halo = refs[:3]
    rows, sign = roles(place[0])
    row = rows[0]
    length, levels, members = part.shape
    if last:
        out, stats = refs[3:]
    else:
        out, ends = refs[7], refs[8:]
        for old, end in zip(refs[3:7], ends):
            end[1:] = old[1:]
    even_lev, even_lon = place[1] == 0, place[2] == 0

    def body(x, total):
        value = part[x] + (RATE + sign * north[row, x]) * halo[x]
        out[x] = value
        if last:
            return total + value
        low, high = value[0:1], value[levels - 1 : levels]
        ends[0][0, pl.ds(x, 1)] = either(even_lev, high, low)
        ends[1][0, pl.ds(x, 1)] = either(even_lev, low, high)
        return total

    total = lax.fori_loop(0, length, body, jnp.zeros((levels, members), jnp.float32), unroll=4)
    if last:
        line_statistics(out, total, stats, 0)
    else:
        low, high = out[0], out[length - 1]
        ends[2][0] = either(even_lon, high, low)
        ends[3][0] = either(even_lon, low, high)


def normalise(count, place, *refs):
    state, stats = refs[:count], refs[count : count + 4]
    begin = count + 4 + (2 if count == 1 else 0)
    normal_out, end_out, work, sems = refs[begin:]
    rows, _ = roles(place[0])
    length = state[0].shape[0]
    offset = 1 if count > 1 else 0
    copies = []
    for k in range(count):
        copy = pltpu.make_async_copy(state[k], end_out.at[rows[k + offset]], sems.at[2 * k])
        copy.start()
        copies.append(copy)
    for k in range(count):
        means = [s[2 * k] for s in stats]
        mean = 0.25 * ((means[0] + means[1]) + (means[2] + means[3]))
        square = (stats[0][2 * k + 1] + stats[1][2 * k + 1]) + (
            stats[2][2 * k + 1] + stats[3][2 * k + 1]
        )
        for part in means:
            square += length * ((part - mean) * (part - mean))
        scale = lax.rsqrt(square * (1.0 / (4 * length)) + 0.0001)

        def body(x, carry):
            work[k, x] = (state[k][x] - mean) * scale
            return carry

        lax.fori_loop(0, length, body, 0, unroll=4)
        copy = pltpu.make_async_copy(work.at[k], normal_out.at[rows[k + offset]], sems.at[2 * k + 1])
        copy.start()
        copies.append(copy)
    for copy in copies:
        copy.wait()


def shards(initial_state, north, east, upward):
    rows_here, length, levels, members = initial_state.shape
    row_type = jax.ShapeDtypeStruct((length, levels, members), jnp.float32)
    lev_type = jax.ShapeDtypeStruct((rows_here, length, members), jnp.float32)
    lon_type = jax.ShapeDtypeStruct((rows_here, levels, members), jnp.float32)
    whole = jax.ShapeDtypeStruct(initial_state.shape, jnp.float32)
    vmem = pl.BlockSpec(memory_space=pltpu.VMEM)
    smem = pl.BlockSpec(memory_space=pltpu.SMEM)
    anywhere = pl.BlockSpec(memory_space=pl.ANY)
    place = jnp.stack([lax.rem(lax.axis_index(a), 2) for a in ("lat", "lev", "lon")])

    def call(kernel, args, outs, flops, aliases={}, in_specs=None, out_specs=None, scratch=()):
        return pl.pallas_call(
            kernel,
            out_shape=outs,
            in_specs=[smem] + (in_specs or [vmem] * len(args)),
            out_specs=out_specs or [vmem] * len(outs),
            scratch_shapes=list(scratch),
            input_output_aliases=aliases,
            compiler_params=pltpu.CompilerParams(vmem_limit_bytes=VMEM_LIMIT),
            cost_estimate=pl.CostEstimate(flops=flops, bytes_accessed=0, transcendentals=0),
        )(place, *args)

    lats, lons = lax.axis_size("lat"), lax.axis_size("lon")

    def pairs(count, start):
        out = []
        for i in range(start, count - 1, 2):
            out += [(i, i + 1), (i + 1, i)]
        return out

    def across(array):
        return lax.ppermute(array, "lat", pairs(lats, 1))

    def beside(array):
        return lax.ppermute(array, "lat", pairs(lats, 0))

    def swap(array, axis, start):
        return lax.ppermute(array, axis, pairs(lax.axis_size(axis), start))

    def ends_of(near_lev, far_lev, near_lon, far_lon):
        return [
            swap(near_lev, "lev", 0),
            swap(far_lev, "lev", 1),
            swap(near_lon, "lon", 0),
            swap(far_lon, "lon", 1),
        ]

    def from_others(array):
        return [lax.ppermute(array, "lon", [(i, i ^ d) for i in range(lons)]) for d in (1, 2, 3)]

    end_types = [lev_type, lev_type, lon_type, lon_type]
    source = pltpu.with_memory_space_constraint(initial_state, pltpu.HBM)
    winds = [pltpu.with_memory_space_constraint(w, pltpu.VMEM) for w in (north, east, upward)]
    for step in range(STEPS):
        last = step == STEPS - 1
        if step == 0:
            (outer,) = call(
                take_outer,
                [source],
                [row_type],
                10**6,
                in_specs=[anywhere],
                scratch=[pltpu.SemaphoreType.DMA],
            )
            halo = across(outer)
            *inner_rows, near, far, close, distant = call(
                take_others,
                [source, outer],
                [row_type] * 3 + end_types,
                10**9,
                in_specs=[anywhere, vmem],
                scratch=[pltpu.SemaphoreType.DMA((3,))],
            )
            core_row = beside(inner_rows[2])
            ends = ends_of(near, far, close, distant)
        else:
            outer, *sent = call(
                functools.partial(finish_row, False),
                [part, winds[0], halo, *extra],
                [row_type, *end_types],
                10**9,
            )
            halo = across(outer)
            ends = ends_of(*sent)
        part, *made = call(
            functools.partial(spread_step, last),
            [outer, *inner_rows, core_row, *ends, *winds],
            [row_type] * 4
            + ([jax.ShapeDtypeStruct((6, levels, members), jnp.float32)] if last else end_types),
            SPREAD_FLOPS,
        )
        inner_rows, extra = made[:3], made[3:]
        if not last:
            core_row = beside(inner_rows[2])
        else:
            stats = extra[0]
            shared = from_others(stats)
            results = call(
                functools.partial(normalise, 3),
                [*inner_rows, stats, *shared],
                [whole, whole],
                SPREAD_FLOPS,
                out_specs=[anywhere, anywhere],
                scratch=[
                    pltpu.VMEM((3, length, levels, members), jnp.float32),
                    pltpu.SemaphoreType.DMA((6,)),
                ],
            )
    outer, stats = call(
        functools.partial(finish_row, True),
        [part, winds[0], halo],
        [row_type, jax.ShapeDtypeStruct((2, levels, members), jnp.float32)],
        10**9,
    )
    results = call(
        functools.partial(normalise, 1),
        [outer, stats, *from_others(stats), *results],
        [whole, whole],
        10**9,
        aliases={6: 0, 7: 1},
        in_specs=[vmem] * 5 + [anywhere] * 2,
        out_specs=[anywhere, anywhere],
        scratch=[
            pltpu.VMEM((1, length, levels, members), jnp.float32),
            pltpu.SemaphoreType.DMA((2,)),
        ],
    )
    return tuple(results)


VMEM_LIMIT = 12 * 2**20
SPREAD_FLOPS = 2 * 10**10


def solution(mesh):
    return jax.shard_map(
        shards, mesh=mesh, in_specs=(GRID,) * 4, out_specs=(GRID, GRID), check_vma=False
    )
```

time: 274 us -> 142 us (0.52); the launches traced: 269 us -> 141 us
  other arithmetic: 117 us -> 0.08 us
  local copies, waits for them, and re-layouts: 53.2 us -> 2.8 us
  Pallas kernels: 0 us -> 44 us
  starting transfers between devices: 74.5 us -> 48.4 us
  waiting for transfers between devices: 22.3 us -> 44.7 us
    add x4 -> x0, other arithmetic: 81.6 us -> none  [the longest x3 81.6 us: march_one_step(): middle - scaled_wind_north * slopes[0] - scaled_wind_east * slopes[1]]
    pallas_call x0 -> x12, Pallas kernels: none -> 44 us  [call(): pl.pallas_call(kernel, out_shape=outs, in_specs=[smem] + (in_specs or [vm...]
    reduce_sum x2 -> x0, other arithmetic: 31.6 us -> none  [the longest x1 31.1 us: shards(): jnp.sum(moved, axis=1, keepdims=True)]
    unnamed x29 -> x10, local copies, waits for them, and re-layouts: 33.3 us -> 2.8 us
    ppermute x24 -> x30, waiting for transfers between devices: 22.3 us -> 44.7 us  [the longest x4 42.4 us: across(): return lax.ppermute(array, 'lat', pairs(lats, 1))]
    ppermute x24 -> x30, starting transfers between devices: 69.6 us -> 48.4 us  [the longest x16 32.1 us: swap(): return lax.ppermute(array, axis, pairs(lax.axis_size(axis), start))]
    slice x12 -> x0, local copies, waits for them, and re-layouts: 15.5 us -> none  [the longest x10 13.1 us: padded(): last = lax.slice_in_dim(array, length - width, length, axis=dim)]
    all_to_all x1 -> x0, starting transfers between devices: 4.91 us -> none  [copy_for_each(): return lax.all_to_all(copies, axis, split_axis=0, concat_axis=0, tiled=True)]
  transfers between devices with their start and end apart: 25 -> 30, of which waited for: 7 -> 8; matrix products, arithmetic and copies ran while one was open for 11% -> 0% of each run, Pallas kernels for 0% -> 25%
where the time goes in v1:
time: 142 us; the launch traced here: 141 us
  starting transfers between devices  48.4 us (34%)
  waiting for transfers between devices  44.7 us (31%)
  Pallas kernels  44 us (31%)
  local copies, waits for them, and re-layouts  2.8 us (2%)
    pallas_call x12, Pallas kernels, call(): pl.pallas_call(kernel, out_shape=outs, in_specs=[smem] + (in_specs or [vm...  44 us
    ppermute x4, waiting for transfers between devices, across(): return lax.ppermute(array, 'lat', pairs(lats, 1))  42.4 us
    ppermute x16, starting transfers between devices, swap(): return lax.ppermute(array, axis, pairs(lax.axis_size(axis), start))  32.1 us
    ppermute x6, starting transfers between devices, from_others(): lax.ppermute(array, 'lon', [(i, i ^ d) for i in range(lons)])  8.35 us
    ppermute x4, starting transfers between devices, across(): return lax.ppermute(array, 'lat', pairs(lats, 1))  7.65 us
  transfers between devices with their start and end apart: 30, of which 8 were waited for; matrix products, arithmetic and copies ran while one was open for 0% of the time, Pallas kernels for 25%

profile of v1, /device:TPU:14, one launch (start us, length us, event | category | flops | bytes accessed | tf_op | source)
XLA Modules:
  0.0 141.0 jit_solution(1548687601441968262)
XLA Ops:
  0.6 0.1 pad_add_fusion.place
  0.7 2.2 %shard_map.59.outer.refs_0_ = f32[96,32,128]{2,1,0:T(8,128)S(1)} custom-call(s32[3]{0:T(128)S(1)} %pad_add_fusion.place, f32[4,96,32,128]{3,2,1,0:T(8,128)} %source.3), custom_call_target="tpu_custom_call" | custom-call | flops 1000000 | tf_op jit(solution)/shard_map/pallas_call | solution.py:219
  3.0 0.0 slice-start.1
  3.0 3.9 %shard_map.60 = (f32[96,32,128]{2,1,0:T(8,128)S(1)}, f32[96,32,128]{2,1,0:T(8,128)S(1)}, f32[96,32,128]{2,1,0:T(8,128)S(1)}, f32[4,96,128]{2,1,0:T(8,128)S(1)}, ...) custom-call(s32[3]{0:T(128)S(1)} %pad_add_fusion.place, ...), custom_call_target="tpu_custom_call" | custom-call | flops 1000000000 | tf_op jit(solution)/shard_map/pallas_call | solution.py:219
  6.9 0.1 collective-permute-start
  6.9 2.0 %collective-permute-start.1 = (f32[4,96,128]{2,1,0:T(8,128)S(1)}, f32[4,96,128]{2,1,0:T(8,128)S(1)}, u32[]{:S(2)}, u32[]{:S(2)}) collective-permute-start(f32[4,96,128]{2,1,0:T(8,128)S(1)} %get-tuple-element.60), channel_id=1, source_target_pairs={{0,1},{1,0},{2,3},{3,2},{4,5},{5,4},{6,7},{7,6},{8,9},{9,8},{10,11... | collective-permute-start | bytes 589832 | tf_op jit(solution)/shard_map/ppermute | solution.py:245
  8.9 0.7 collective-permute-start.2
  9.6 0.5 collective-permute-start.3
  10.1 4.3 %collective-permute-start.4 = (f32[4,32,128]{2,1,0:T(8,128)S(1)}, f32[4,32,128]{2,1,0:T(8,128)S(1)}, u32[]{:S(2)}, u32[]{:S(2)}) collective-permute-start(f32[4,32,128]{2,1,0:T(8,128)S(1)} %get-tuple-element.63), channel_id=1, source_target_pairs={{4,8},{8,4},{5,9},{9,5},{6,10},{10,6},{7,11},{11,7},{20,24},{24,20... | collective-permute-start | bytes 196616 | tf_op jit(solution)/shard_map/ppermute | solution.py:245
  14.5 0.0 collective-permute-done.3.refs_7_
  14.5 1.9 %collective-permute-start.5 = (f32[96,32,128]{2,1,0:T(8,128)S(1)}, f32[96,32,128]{2,1,0:T(8,128)S(1)}, u32[]{:S(2)}, u32[]{:S(2)}) collective-permute-start(f32[96,32,128]{2,1,0:T(8,128)S(1)} %shard_map.59.outer.refs_0_), channel_id=1, source_target_pairs={{16,32},{32,16},{48,64},{64,48},{80,96},{96,80},{17,33},{33,17},{4... | collective-permute-start | bytes 4718600 | tf_op jit(solution)/shard_map/ppermute | solution.py:239
  16.4 0.3 collective-permute-done.4.refs_8_
  16.7 0.0 collective-permute-done.1.refs_5_
  16.7 0.0 collective-permute-done.2.refs_6_
  16.7 0.0 copy-start.1
  16.7 2.8 %copy-done.1 = f32[4,96,32,128]{3,2,1,0:T(8,128)S(1)} copy-done((f32[4,96,32,128]{3,2,1,0:T(8,128)S(1)}, f32[4,96,32,128]{3,2,1,0:T(8,128)}, u32[]{:S(2)}) %copy-start.1) | copy-done | bytes 6291480
  19.5 6.6 %shard_map.61 = (f32[96,32,128]{2,1,0:T(8,128)S(1)}, f32[96,32,128]{2,1,0:T(8,128)S(1)}, f32[96,32,128]{2,1,0:T(8,128)S(1)}, f32[96,32,128]{2,1,0:T(8,128)S(1)},...) custom-call(s32[3]{0:T(128)S(1)} %pad_add_fusion.place, ...), custom_call_target="tpu_custom_call" | custom-call | flops 20000000000 | tf_op jit(solution)/shard_map/pallas_call | solution.py:219
  26.1 0.1 collective-permute-start.6
  26.2 10.0 %collective-permute-done.5.refs_2_ = f32[96,32,128]{2,1,0:T(8,128)S(1)} collective-permute-done((f32[96,32,128]{2,1,0:T(8,128)S(1)}, f32[96,32,128]{2,1,0:T(8,128)S(1)}, u32[]{:S(2)}, u32[]{:S(2)}) %collective-permute-start.5) | collective-permute-done | bytes 1572896 | tf_op jit(solution)/shard_map/ppermute | solution.py:239
  36.2 1.0 shard_map.62
  37.2 4.9 %collective-permute-start.7 = (f32[4,96,128]{2,1,0:T(8,128)S(1)}, f32[4,96,128]{2,1,0:T(8,128)S(1)}, u32[]{:S(2)}, u32[]{:S(2)}) collective-permute-start(f32[4,96,128]{2,1,0:T(8,128)S(1)} %get-tuple-element.73), channel_id=1, source_target_pairs={{0,1},{1,0},{2,3},{3,2},{4,5},{5,4},{6,7},{7,6},{8,9},{9,8},{10,11... | collective-permute-start | bytes 589832 | tf_op jit(solution)/shard_map/ppermute | solution.py:245
  42.0 0.7 collective-permute-start.8
  42.7 0.1 collective-permute-start.9
  42.8 4.2 %collective-permute-start.10 = (f32[4,32,128]{2,1,0:T(8,128)S(1)}, f32[4,32,128]{2,1,0:T(8,128)S(1)}, u32[]{:S(2)}, u32[]{:S(2)}) collective-permute-start(f32[4,32,128]{2,1,0:T(8,128)S(1)} %get-tuple-element.76), channel_id=1, source_target_pairs={{4,8},{8,4},{5,9},{9,5},{6,10},{10,6},{7,11},{11,7},{20,24},{24,20... | collective-permute-start | bytes 196616 | tf_op jit(solution)/shard_map/ppermute | solution.py:245
  47.0 0.0 collective-permute-done.9.refs_7_
  47.1 1.9 %collective-permute-start.11 = (f32[96,32,128]{2,1,0:T(8,128)S(1)}, f32[96,32,128]{2,1,0:T(8,128)S(1)}, u32[]{:S(2)}, u32[]{:S(2)}) collective-permute-start(f32[96,32,128]{2,1,0:T(8,128)S(1)} %get-tuple-element.69.refs_0_), channel_id=1, source_target_pairs={{16,32},{32,16},{48,64},{64,48},{80,96},{96,80},{17,33},{33,17},{4... | collective-permute-start | bytes 4718600 | tf_op jit(solution)/shard_map/ppermute | solution.py:239
  49.0 0.3 collective-permute-done.10.refs_8_
  49.3 0.0 collective-permute-done.7.refs_5_
  49.3 0.0 collective-permute-done.8.refs_6_
  49.3 6.6 %shard_map.63 = (f32[96,32,128]{2,1,0:T(8,128)S(1)}, f32[96,32,128]{2,1,0:T(8,128)S(1)}, f32[96,32,128]{2,1,0:T(8,128)S(1)}, f32[96,32,128]{2,1,0:T(8,128)S(1)},...) custom-call(s32[3]{0:T(128)S(1)} %pad_add_fusion.place, ...), custom_call_target="tpu_custom_call" | custom-call | flops 20000000000 | tf_op jit(solution)/shard_map/pallas_call | solution.py:219
  55.9 0.1 collective-permute-start.12
  56.0 12.8 %collective-permute-done.11.refs_2_ = f32[96,32,128]{2,1,0:T(8,128)S(1)} collective-permute-done((f32[96,32,128]{2,1,0:T(8,128)S(1)}, f32[96,32,128]{2,1,0:T(8,128)S(1)}, u32[]{:S(2)}, u32[]{:S(2)}) %collective-permute-start.11) | collective-permute-done | bytes 1572896 | tf_op jit(solution)/shard_map/ppermute | solution.py:239
  68.8 1.0 shard_map.64
  69.8 1.5 %collective-permute-start.13 = (f32[4,96,128]{2,1,0:T(8,128)S(1)}, f32[4,96,128]{2,1,0:T(8,128)S(1)}, u32[]{:S(2)}, u32[]{:S(2)}) collective-permute-start(f32[4,96,128]{2,1,0:T(8,128)S(1)} %get-tuple-element.86), channel_id=1, source_target_pairs={{0,1},{1,0},{2,3},{3,2},{4,5},{5,4},{6,7},{7,6},{8,9},{9,8},{10,11... | collective-permute-start | bytes 589832 | tf_op jit(solution)/shard_map/ppermute | solution.py:245
  71.3 0.7 collective-permute-start.14
  71.9 0.1 collective-permute-start.15
  72.0 4.2 %collective-permute-start.16 = (f32[4,32,128]{2,1,0:T(8,128)S(1)}, f32[4,32,128]{2,1,0:T(8,128)S(1)}, u32[]{:S(2)}, u32[]{:S(2)}) collective-permute-start(f32[4,32,128]{2,1,0:T(8,128)S(1)} %get-tuple-element.89), channel_id=1, source_target_pairs={{4,8},{8,4},{5,9},{9,5},{6,10},{10,6},{7,11},{11,7},{20,24},{24,20... | collective-permute-start | bytes 196616 | tf_op jit(solution)/shard_map/ppermute | solution.py:245
  76.2 0.0 collective-permute-done.15.refs_7_
  76.3 1.9 %collective-permute-start.17 = (f32[96,32,128]{2,1,0:T(8,128)S(1)}, f32[96,32,128]{2,1,0:T(8,128)S(1)}, u32[]{:S(2)}, u32[]{:S(2)}) collective-permute-start(f32[96,32,128]{2,1,0:T(8,128)S(1)} %get-tuple-element.82.refs_0_), channel_id=1, source_target_pairs={{16,32},{32,16},{48,64},{64,48},{80,96},{96,80},{17,33},{33,17},{4... | collective-permute-start | bytes 4718600 | tf_op jit(solution)/shard_map/ppermute | solution.py:239
  78.2 0.3 collective-permute-done.16.refs_8_
  78.5 0.0 collective-permute-done.13.refs_5_
  78.5 0.0 collective-permute-done.14.refs_6_
  78.5 6.6 %shard_map.65 = (f32[96,32,128]{2,1,0:T(8,128)S(1)}, f32[96,32,128]{2,1,0:T(8,128)S(1)}, f32[96,32,128]{2,1,0:T(8,128)S(1)}, f32[96,32,128]{2,1,0:T(8,128)S(1)},...) custom-call(s32[3]{0:T(128)S(1)} %pad_add_fusion.place, ...), custom_call_target="tpu_custom_call" | custom-call | flops 20000000000 | tf_op jit(solution)/shard_map/pallas_call | solution.py:219
  85.1 0.1 collective-permute-start.18
  85.2 12.8 %collective-permute-done.17.refs_2_ = f32[96,32,128]{2,1,0:T(8,128)S(1)} collective-permute-done((f32[96,32,128]{2,1,0:T(8,128)S(1)}, f32[96,32,128]{2,1,0:T(8,128)S(1)}, u32[]{:S(2)}, u32[]{:S(2)}) %collective-permute-start.17) | collective-permute-done | bytes 1572896 | tf_op jit(solution)/shard_map/ppermute | solution.py:239
  98.0 1.0 shard_map.66
  99.0 3.4 %collective-permute-start.19 = (f32[4,96,128]{2,1,0:T(8,128)S(1)}, f32[4,96,128]{2,1,0:T(8,128)S(1)}, u32[]{:S(2)}, u32[]{:S(2)}) collective-permute-start(f32[4,96,128]{2,1,0:T(8,128)S(1)} %get-tuple-element.99), channel_id=1, source_target_pairs={{0,1},{1,0},{2,3},{3,2},{4,5},{5,4},{6,7},{7,6},{8,9},{9,8},{10,11... | collective-permute-start | bytes 589832 | tf_op jit(solution)/shard_map/ppermute | solution.py:245
  102.3 0.7 collective-permute-start.20
  103.0 0.1 collective-permute-start.21
  103.1 4.2 %collective-permute-start.22 = (f32[4,32,128]{2,1,0:T(8,128)S(1)}, f32[4,32,128]{2,1,0:T(8,128)S(1)}, u32[]{:S(2)}, u32[]{:S(2)}) collective-permute-start(f32[4,32,128]{2,1,0:T(8,128)S(1)} %get-tuple-element.102), channel_id=1, source_target_pairs={{4,8},{8,4},{5,9},{9,5},{6,10},{10,6},{7,11},{11,7},{20,24},{24,20... | collective-permute-start | bytes 196616 | tf_op jit(solution)/shard_map/ppermute | solution.py:245
  107.3 0.0 collective-permute-done.21.refs_7_
  107.3 1.9 %collective-permute-start.23 = (f32[96,32,128]{2,1,0:T(8,128)S(1)}, f32[96,32,128]{2,1,0:T(8,128)S(1)}, u32[]{:S(2)}, u32[]{:S(2)}) collective-permute-start(f32[96,32,128]{2,1,0:T(8,128)S(1)} %get-tuple-element.95.refs_0_), channel_id=1, source_target_pairs={{16,32},{32,16},{48,64},{64,48},{80,96},{96,80},{17,33},{33,17},{4... | collective-permute-start | bytes 4718600 | tf_op jit(solution)/shard_map/ppermute | solution.py:239
  109.3 1.3 collective-permute-done.22.refs_8_
  110.6 7.4 %shard_map.67 = (f32[96,32,128]{2,1,0:T(8,128)S(1)}, f32[96,32,128]{2,1,0:T(8,128)S(1)}, f32[96,32,128]{2,1,0:T(8,128)S(1)}, f32[96,32,128]{2,1,0:T(8,128)S(1)}, f32[6,32,128]{2,1,0:T(8,128)S(1)}) custom-call(s32[3]{0:T(128)S(1)} %pad_add_fusion.place, f32[96,32,128]{2,1,0:T(8,128)S(1)} %get-tuple-element.95.refs_0_, ...), custom_call_target="tpu_custom_call" | custom-call | flops 20000000000 | tf_op jit(solution)/shard_map/pallas_call | solution.py:219
  118.1 1.0 collective-permute-start.29
  119.1 0.3 collective-permute-start.28
  119.4 2.8 %collective-permute-start.27 = (f32[6,32,128]{2,1,0:T(8,128)S(1)}, f32[6,32,128]{2,1,0:T(8,128)S(1)}, u32[]{:S(2)}, u32[]{:S(2)}) collective-permute-start(f32[6,32,128]{2,1,0:T(8,128)S(1)} %get-tuple-element.109.refs_3_), channel_id=1, source_target_pairs={{0,4},{4,0},{8,12},{12,8},{1,5},{5,1},{9,13},{13,9},{2,6},{6,2},{1... | collective-permute-start | bytes 294920 | tf_op jit(solution)/shard_map/ppermute | solution.py:256
  122.2 6.8 %collective-permute-done.23.refs_2_ = f32[96,32,128]{2,1,0:T(8,128)S(1)} collective-permute-done((f32[96,32,128]{2,1,0:T(8,128)S(1)}, f32[96,32,128]{2,1,0:T(8,128)S(1)}, u32[]{:S(2)}, u32[]{:S(2)}) %collective-permute-start.23) | collective-permute-done | bytes 1572896 | tf_op jit(solution)/shard_map/ppermute | solution.py:239
  129.1 1.2 shard_map.68
  130.3 1.1 collective-permute-start.26
  131.4 1.5 %collective-permute-start.25 = (f32[2,32,128]{2,1,0:T(8,128)S(1)}, f32[2,32,128]{2,1,0:T(8,128)S(1)}, u32[]{:S(2)}, u32[]{:S(2)}) collective-permute-start(f32[2,32,128]{2,1,0:T(8,128)S(1)} %get-tuple-element.105.refs_1_), channel_id=1, source_target_pairs={{0,8},{4,12},{8,0},{12,4},{1,9},{5,13},{9,1},{13,5},{2,10},{6,14},... | collective-permute-start | bytes 98312 | tf_op jit(solution)/shard_map/ppermute | solution.py:256
  132.9 1.5 %collective-permute-start.24 = (f32[2,32,128]{2,1,0:T(8,128)S(1)}, f32[2,32,128]{2,1,0:T(8,128)S(1)}, u32[]{:S(2)}, u32[]{:S(2)}) collective-permute-start(f32[2,32,128]{2,1,0:T(8,128)S(1)} %get-tuple-element.105.refs_1_), channel_id=1, source_target_pairs={{0,4},{4,0},{8,12},{12,8},{1,5},{5,1},{9,13},{13,9},{2,6},{6,2},{1... | collective-permute-start | bytes 98312 | tf_op jit(solution)/shard_map/ppermute | solution.py:256
  134.5 4.2 %shard_map.69 = (f32[4,96,32,128]{3,2,1,0:T(8,128)}, f32[4,96,32,128]{3,2,1,0:T(8,128)}) custom-call(s32[3]{0:T(128)S(1)} %pad_add_fusion.place, f32[96,32,128]{2,1,0:T(8,128)S(1)} %get-tuple-element.106.refs_0_, f32[96,32,128]{2,1,0:T(8,128)S(1)} %get-tuple-element.107.refs_1_, f32[96,32,128]{2,1,0:T(8,128)S(1)} %get-tuple-element.108.refs_2_, ...), custom_call_target="tpu_custom_call" | custom-call | flops 20000000000 | tf_op jit(solution)/shard_map/pallas_call | solution.py:219
  138.8 2.2 %shard_map.70 = (f32[4,96,32,128]{3,2,1,0:T(8,128)}, f32[4,96,32,128]{3,2,1,0:T(8,128)}) custom-call(s32[3]{0:T(128)S(1)} %pad_add_fusion.place, f32[96,32,128]{2,1,0:T(8,128)S(1)} %get-tuple-element.104.refs_0_, f32[2,32,128]{2,1,0:T(8,128)S(1)} %get-tuple-element.105.refs_1_, ...), custom_call_target="tpu_custom_call", output_to_operand_aliasing={{0}: (6, {}), {1}: (7, {})} | custom-call | flops 1000000000 | tf_op jit(solution)/shard_map/pallas_call | solution.py:219
  (20 shorter events, 0.0 us)
Async XLA Ops:
  0.7 16.0 %slice-start = ((s8[6291456]{0:T(1024)(128)(4,1)}), s8[4194304]{0:T(1024)(128)(4,1)S(1)}, s32[]{:S(2)}) async-start(s8[6291456]{0:T(1024)(128)(4,1)} %bitcast.3), calls=%async_computation | async-start | bytes 8388608
  0.7 16.0 %copy-start = (f32[4,96,32,128]{3,2,1,0:T(8,128)S(1)}, f32[4,96,32,128]{3,2,1,0:T(8,128)}, u32[]{:S(2)}) copy-start(f32[4,96,32,128]{3,2,1,0:T(8,128)} %refs_10_.7) | copy-start | bytes 18874372
  3.0 13.8 %slice-start.1 = ((s8[6291456]{0:T(1024)(128)(4,1)}), s8[2097152]{0:T(1024)(128)(4,1)S(1)}, s32[]{:S(2)}) async-start(s8[6291456]{0:T(1024)(128)(4,1)} %bitcast.3), calls=%async_computation.1 | async-start | bytes 4194304
  6.9 9.8 %collective-permute-start = (f32[96,32,128]{2,1,0:T(8,128)S(1)}, f32[96,32,128]{2,1,0:T(8,128)S(1)}, u32[]{:S(2)}, u32[]{:S(2)}) collective-permute-start(f32[96,32,128]{2,1,0:T(8,128)S(1)} %get-tuple-element.59.refs_3_), channel_id=1, source_target_pairs={{0,16},{16,0},{32,48},{48,32},{64,80},{80,64},{96,112},{112,96},{1... | collective-permute-start | bytes 4718600 | tf_op jit(solution)/shard_map/ppermute | solution.py:242
  6.9 9.7 %collective-permute-start.1 = (f32[4,96,128]{2,1,0:T(8,128)S(1)}, f32[4,96,128]{2,1,0:T(8,128)S(1)}, u32[]{:S(2)}, u32[]{:S(2)}) collective-permute-start(f32[4,96,128]{2,1,0:T(8,128)S(1)} %get-tuple-element.60), channel_id=1, source_target_pairs={{0,1},{1,0},{2,3},{3,2},{4,5},{5,4},{6,7},{7,6},{8,9},{9,8},{10,11... | collective-permute-start | bytes 589832 | tf_op jit(solution)/shard_map/ppermute | solution.py:245
  8.9 7.7 %collective-permute-start.2 = (f32[4,96,128]{2,1,0:T(8,128)S(1)}, f32[4,96,128]{2,1,0:T(8,128)S(1)}, u32[]{:S(2)}, u32[]{:S(2)}) collective-permute-start(f32[4,96,128]{2,1,0:T(8,128)S(1)} %get-tuple-element.61), channel_id=1, source_target_pairs={{1,2},{2,1},{5,6},{6,5},{9,10},{10,9},{13,14},{14,13},{17,18},{18,... | collective-permute-start | bytes 589832 | tf_op jit(solution)/shard_map/ppermute | solution.py:245
  9.6 4.8 %collective-permute-start.3 = (f32[4,32,128]{2,1,0:T(8,128)S(1)}, f32[4,32,128]{2,1,0:T(8,128)S(1)}, u32[]{:S(2)}, u32[]{:S(2)}) collective-permute-start(f32[4,32,128]{2,1,0:T(8,128)S(1)} %get-tuple-element.62), channel_id=1, source_target_pairs={{0,4},{4,0},{8,12},{12,8},{1,5},{5,1},{9,13},{13,9},{2,6},{6,2},{1... | collective-permute-start | bytes 196616 | tf_op jit(solution)/shard_map/ppermute | solution.py:245
  10.1 6.5 %collective-permute-start.4 = (f32[4,32,128]{2,1,0:T(8,128)S(1)}, f32[4,32,128]{2,1,0:T(8,128)S(1)}, u32[]{:S(2)}, u32[]{:S(2)}) collective-permute-start(f32[4,32,128]{2,1,0:T(8,128)S(1)} %get-tuple-element.63), channel_id=1, source_target_pairs={{4,8},{8,4},{5,9},{9,5},{6,10},{10,6},{7,11},{11,7},{20,24},{24,20... | collective-permute-start | bytes 196616 | tf_op jit(solution)/shard_map/ppermute | solution.py:245
  14.5 21.7 %collective-permute-start.5 = (f32[96,32,128]{2,1,0:T(8,128)S(1)}, f32[96,32,128]{2,1,0:T(8,128)S(1)}, u32[]{:S(2)}, u32[]{:S(2)}) collective-permute-start(f32[96,32,128]{2,1,0:T(8,128)S(1)} %shard_map.59.outer.refs_0_), channel_id=1, source_target_pairs={{16,32},{32,16},{48,64},{64,48},{80,96},{96,80},{17,33},{33,17},{4... | collective-permute-start | bytes 4718600 | tf_op jit(solution)/shard_map/ppermute | solution.py:239
  16.7 2.8 %copy-start.1 = (f32[4,96,32,128]{3,2,1,0:T(8,128)S(1)}, f32[4,96,32,128]{3,2,1,0:T(8,128)}, u32[]{:S(2)}) copy-start(f32[4,96,32,128]{3,2,1,0:T(8,128)} %refs_11_.7) | copy-start | bytes 18874372
  26.1 23.2 %collective-permute-start.6 = (f32[96,32,128]{2,1,0:T(8,128)S(1)}, f32[96,32,128]{2,1,0:T(8,128)S(1)}, u32[]{:S(2)}, u32[]{:S(2)}) collective-permute-start(f32[96,32,128]{2,1,0:T(8,128)S(1)} %get-tuple-element.72.refs_3_), channel_id=1, source_target_pairs={{0,16},{16,0},{32,48},{48,32},{64,80},{80,64},{96,112},{112,96},{1... | collective-permute-start | bytes 4718600 | tf_op jit(solution)/shard_map/ppermute | solution.py:242
  36.2 13.1 %copy-start.2 = (f32[4,96,32,128]{3,2,1,0:T(8,128)S(1)}, f32[4,96,32,128]{3,2,1,0:T(8,128)}, u32[]{:S(2)}) copy-start(f32[4,96,32,128]{3,2,1,0:T(8,128)} %refs_11_.7) | copy-start | bytes 18874372
  37.2 12.1 %collective-permute-start.7 = (f32[4,96,128]{2,1,0:T(8,128)S(1)}, f32[4,96,128]{2,1,0:T(8,128)S(1)}, u32[]{:S(2)}, u32[]{:S(2)}) collective-permute-start(f32[4,96,128]{2,1,0:T(8,128)S(1)} %get-tuple-element.73), channel_id=1, source_target_pairs={{0,1},{1,0},{2,3},{3,2},{4,5},{5,4},{6,7},{7,6},{8,9},{9,8},{10,11... | collective-permute-start | bytes 589832 | tf_op jit(solution)/shard_map/ppermute | solution.py:245
  42.0 7.2 %collective-permute-start.8 = (f32[4,96,128]{2,1,0:T(8,128)S(1)}, f32[4,96,128]{2,1,0:T(8,128)S(1)}, u32[]{:S(2)}, u32[]{:S(2)}) collective-permute-start(f32[4,96,128]{2,1,0:T(8,128)S(1)} %get-tuple-element.74), channel_id=1, source_target_pairs={{1,2},{2,1},{5,6},{6,5},{9,10},{10,9},{13,14},{14,13},{17,18},{18,... | collective-permute-start | bytes 589832 | tf_op jit(solution)/shard_map/ppermute | solution.py:245
  42.7 4.3 %collective-permute-start.9 = (f32[4,32,128]{2,1,0:T(8,128)S(1)}, f32[4,32,128]{2,1,0:T(8,128)S(1)}, u32[]{:S(2)}, u32[]{:S(2)}) collective-permute-start(f32[4,32,128]{2,1,0:T(8,128)S(1)} %get-tuple-element.75), channel_id=1, source_target_pairs={{0,4},{4,0},{8,12},{12,8},{1,5},{5,1},{9,13},{13,9},{2,6},{6,2},{1... | collective-permute-start | bytes 196616 | tf_op jit(solution)/shard_map/ppermute | solution.py:245
  42.8 6.5 %collective-permute-start.10 = (f32[4,32,128]{2,1,0:T(8,128)S(1)}, f32[4,32,128]{2,1,0:T(8,128)S(1)}, u32[]{:S(2)}, u32[]{:S(2)}) collective-permute-start(f32[4,32,128]{2,1,0:T(8,128)S(1)} %get-tuple-element.76), channel_id=1, source_target_pairs={{4,8},{8,4},{5,9},{9,5},{6,10},{10,6},{7,11},{11,7},{20,24},{24,20... | collective-permute-start | bytes 196616 | tf_op jit(solution)/shard_map/ppermute | solution.py:245
  47.1 21.7 %collective-permute-start.11 = (f32[96,32,128]{2,1,0:T(8,128)S(1)}, f32[96,32,128]{2,1,0:T(8,128)S(1)}, u32[]{:S(2)}, u32[]{:S(2)}) collective-permute-start(f32[96,32,128]{2,1,0:T(8,128)S(1)} %get-tuple-element.69.refs_0_), channel_id=1, source_target_pairs={{16,32},{32,16},{48,64},{64,48},{80,96},{96,80},{17,33},{33,17},{4... | collective-permute-start | bytes 4718600 | tf_op jit(solution)/shard_map/ppermute | solution.py:239
  55.9 22.6 %collective-permute-start.12 = (f32[96,32,128]{2,1,0:T(8,128)S(1)}, f32[96,32,128]{2,1,0:T(8,128)S(1)}, u32[]{:S(2)}, u32[]{:S(2)}) collective-permute-start(f32[96,32,128]{2,1,0:T(8,128)S(1)} %get-tuple-element.85.refs_3_), channel_id=1, source_target_pairs={{0,16},{16,0},{32,48},{48,32},{64,80},{80,64},{96,112},{112,96},{1... | collective-permute-start | bytes 4718600 | tf_op jit(solution)/shard_map/ppermute | solution.py:242
  69.8 8.7 %collective-permute-start.13 = (f32[4,96,128]{2,1,0:T(8,128)S(1)}, f32[4,96,128]{2,1,0:T(8,128)S(1)}, u32[]{:S(2)}, u32[]{:S(2)}) collective-permute-start(f32[4,96,128]{2,1,0:T(8,128)S(1)} %get-tuple-element.86), channel_id=1, source_target_pairs={{0,1},{1,0},{2,3},{3,2},{4,5},{5,4},{6,7},{7,6},{8,9},{9,8},{10,11... | collective-permute-start | bytes 589832 | tf_op jit(solution)/shard_map/ppermute | solution.py:245
  71.3 7.2 %collective-permute-start.14 = (f32[4,96,128]{2,1,0:T(8,128)S(1)}, f32[4,96,128]{2,1,0:T(8,128)S(1)}, u32[]{:S(2)}, u32[]{:S(2)}) collective-permute-start(f32[4,96,128]{2,1,0:T(8,128)S(1)} %get-tuple-element.87), channel_id=1, source_target_pairs={{1,2},{2,1},{5,6},{6,5},{9,10},{10,9},{13,14},{14,13},{17,18},{18,... | collective-permute-start | bytes 589832 | tf_op jit(solution)/shard_map/ppermute | solution.py:245
  71.9 4.3 %collective-permute-start.15 = (f32[4,32,128]{2,1,0:T(8,128)S(1)}, f32[4,32,128]{2,1,0:T(8,128)S(1)}, u32[]{:S(2)}, u32[]{:S(2)}) collective-permute-start(f32[4,32,128]{2,1,0:T(8,128)S(1)} %get-tuple-element.88), channel_id=1, source_target_pairs={{0,4},{4,0},{8,12},{12,8},{1,5},{5,1},{9,13},{13,9},{2,6},{6,2},{1... | collective-permute-start | bytes 196616 | tf_op jit(solution)/shard_map/ppermute | solution.py:245
  72.0 6.5 %collective-permute-start.16 = (f32[4,32,128]{2,1,0:T(8,128)S(1)}, f32[4,32,128]{2,1,0:T(8,128)S(1)}, u32[]{:S(2)}, u32[]{:S(2)}) collective-permute-start(f32[4,32,128]{2,1,0:T(8,128)S(1)} %get-tuple-element.89), channel_id=1, source_target_pairs={{4,8},{8,4},{5,9},{9,5},{6,10},{10,6},{7,11},{11,7},{20,24},{24,20... | collective-permute-start | bytes 196616 | tf_op jit(solution)/shard_map/ppermute | solution.py:245
  76.3 21.7 %collective-permute-start.17 = (f32[96,32,128]{2,1,0:T(8,128)S(1)}, f32[96,32,128]{2,1,0:T(8,128)S(1)}, u32[]{:S(2)}, u32[]{:S(2)}) collective-permute-start(f32[96,32,128]{2,1,0:T(8,128)S(1)} %get-tuple-element.82.refs_0_), channel_id=1, source_target_pairs={{16,32},{32,16},{48,64},{64,48},{80,96},{96,80},{17,33},{33,17},{4... | collective-permute-start | bytes 4718600 | tf_op jit(solution)/shard_map/ppermute | solution.py:239
  85.1 25.5 %collective-permute-start.18 = (f32[96,32,128]{2,1,0:T(8,128)S(1)}, f32[96,32,128]{2,1,0:T(8,128)S(1)}, u32[]{:S(2)}, u32[]{:S(2)}) collective-permute-start(f32[96,32,128]{2,1,0:T(8,128)S(1)} %get-tuple-element.98.refs_3_), channel_id=1, source_target_pairs={{0,16},{16,0},{32,48},{48,32},{64,80},{80,64},{96,112},{112,96},{1... | collective-permute-start | bytes 4718600 | tf_op jit(solution)/shard_map/ppermute | solution.py:242
  99.0 11.6 %collective-permute-start.19 = (f32[4,96,128]{2,1,0:T(8,128)S(1)}, f32[4,96,128]{2,1,0:T(8,128)S(1)}, u32[]{:S(2)}, u32[]{:S(2)}) collective-permute-start(f32[4,96,128]{2,1,0:T(8,128)S(1)} %get-tuple-element.99), channel_id=1, source_target_pairs={{0,1},{1,0},{2,3},{3,2},{4,5},{5,4},{6,7},{7,6},{8,9},{9,8},{10,11... | collective-permute-start | bytes 589832 | tf_op jit(solution)/shard_map/ppermute | solution.py:245
  102.3 8.3 %collective-permute-start.20 = (f32[4,96,128]{2,1,0:T(8,128)S(1)}, f32[4,96,128]{2,1,0:T(8,128)S(1)}, u32[]{:S(2)}, u32[]{:S(2)}) collective-permute-start(f32[4,96,128]{2,1,0:T(8,128)S(1)} %get-tuple-element.100), channel_id=1, source_target_pairs={{1,2},{2,1},{5,6},{6,5},{9,10},{10,9},{13,14},{14,13},{17,18},{18,... | collective-permute-start | bytes 589832 | tf_op jit(solution)/shard_map/ppermute | solution.py:245
  103.0 4.3 %collective-permute-start.21 = (f32[4,32,128]{2,1,0:T(8,128)S(1)}, f32[4,32,128]{2,1,0:T(8,128)S(1)}, u32[]{:S(2)}, u32[]{:S(2)}) collective-permute-start(f32[4,32,128]{2,1,0:T(8,128)S(1)} %get-tuple-element.101), channel_id=1, source_target_pairs={{0,4},{4,0},{8,12},{12,8},{1,5},{5,1},{9,13},{13,9},{2,6},{6,2},{1... | collective-permute-start | bytes 196616 | tf_op jit(solution)/shard_map/ppermute | solution.py:245
  103.1 7.5 %collective-permute-start.22 = (f32[4,32,128]{2,1,0:T(8,128)S(1)}, f32[4,32,128]{2,1,0:T(8,128)S(1)}, u32[]{:S(2)}, u32[]{:S(2)}) collective-permute-start(f32[4,32,128]{2,1,0:T(8,128)S(1)} %get-tuple-element.102), channel_id=1, source_target_pairs={{4,8},{8,4},{5,9},{9,5},{6,10},{10,6},{7,11},{11,7},{20,24},{24,20... | collective-permute-start | bytes 196616 | tf_op jit(solution)/shard_map/ppermute | solution.py:245
  107.3 21.7 %collective-permute-start.23 = (f32[96,32,128]{2,1,0:T(8,128)S(1)}, f32[96,32,128]{2,1,0:T(8,128)S(1)}, u32[]{:S(2)}, u32[]{:S(2)}) collective-permute-start(f32[96,32,128]{2,1,0:T(8,128)S(1)} %get-tuple-element.95.refs_0_), channel_id=1, source_target_pairs={{16,32},{32,16},{48,64},{64,48},{80,96},{96,80},{17,33},{33,17},{4... | collective-permute-start | bytes 4718600 | tf_op jit(solution)/shard_map/ppermute | solution.py:239
  118.1 14.9 %collective-permute-start.29 = (f32[6,32,128]{2,1,0:T(8,128)S(1)}, f32[6,32,128]{2,1,0:T(8,128)S(1)}, u32[]{:S(2)}, u32[]{:S(2)}) collective-permute-start(f32[6,32,128]{2,1,0:T(8,128)S(1)} %get-tuple-element.109.refs_3_), channel_id=1, source_target_pairs={{0,12},{4,8},{8,4},{12,0},{1,13},{5,9},{9,5},{13,1},{2,14},{6,10},... | collective-permute-start | bytes 294920 | tf_op jit(solution)/shard_map/ppermute | solution.py:256
  119.1 15.4 %collective-permute-start.28 = (f32[6,32,128]{2,1,0:T(8,128)S(1)}, f32[6,32,128]{2,1,0:T(8,128)S(1)}, u32[]{:S(2)}, u32[]{:S(2)}) collective-permute-start(f32[6,32,128]{2,1,0:T(8,128)S(1)} %get-tuple-element.109.refs_3_), channel_id=1, source_target_pairs={{0,8},{4,12},{8,0},{12,4},{1,9},{5,13},{9,1},{13,5},{2,10},{6,14},... | collective-permute-start | bytes 294920 | tf_op jit(solution)/shard_map/ppermute | solution.py:256
  119.4 15.1 %collective-permute-start.27 = (f32[6,32,128]{2,1,0:T(8,128)S(1)}, f32[6,32,128]{2,1,0:T(8,128)S(1)}, u32[]{:S(2)}, u32[]{:S(2)}) collective-permute-start(f32[6,32,128]{2,1,0:T(8,128)S(1)} %get-tuple-element.109.refs_3_), channel_id=1, source_target_pairs={{0,4},{4,0},{8,12},{12,8},{1,5},{5,1},{9,13},{13,9},{2,6},{6,2},{1... | collective-permute-start | bytes 294920 | tf_op jit(solution)/shard_map/ppermute | solution.py:256
  130.3 8.4 %collective-permute-start.26 = (f32[2,32,128]{2,1,0:T(8,128)S(1)}, f32[2,32,128]{2,1,0:T(8,128)S(1)}, u32[]{:S(2)}, u32[]{:S(2)}) collective-permute-start(f32[2,32,128]{2,1,0:T(8,128)S(1)} %get-tuple-element.105.refs_1_), channel_id=1, source_target_pairs={{0,12},{4,8},{8,4},{12,0},{1,13},{5,9},{9,5},{13,1},{2,14},{6,10},... | collective-permute-start | bytes 98312 | tf_op jit(solution)/shard_map/ppermute | solution.py:256
  131.4 7.3 %collective-permute-start.25 = (f32[2,32,128]{2,1,0:T(8,128)S(1)}, f32[2,32,128]{2,1,0:T(8,128)S(1)}, u32[]{:S(2)}, u32[]{:S(2)}) collective-permute-start(f32[2,32,128]{2,1,0:T(8,128)S(1)} %get-tuple-element.105.refs_1_), channel_id=1, source_target_pairs={{0,8},{4,12},{8,0},{12,4},{1,9},{5,13},{9,1},{13,5},{2,10},{6,14},... | collective-permute-start | bytes 98312 | tf_op jit(solution)/shard_map/ppermute | solution.py:256
  132.9 5.8 %collective-permute-start.24 = (f32[2,32,128]{2,1,0:T(8,128)S(1)}, f32[2,32,128]{2,1,0:T(8,128)S(1)}, u32[]{:S(2)}, u32[]{:S(2)}) collective-permute-start(f32[2,32,128]{2,1,0:T(8,128)S(1)} %get-tuple-element.105.refs_1_), channel_id=1, source_target_pairs={{0,4},{4,0},{8,12},{12,8},{1,5},{5,1},{9,13},{13,9},{2,6},{6,2},{1... | collective-permute-start | bytes 98312 | tf_op jit(solution)/shard_map/ppermute | solution.py:256

commit v2 on v1

v2 whole, which is shorter than its diff:
```python
import functools

import jax
import jax.numpy as jnp
from jax import lax
from jax.experimental import pallas as pl
from jax.experimental.pallas import tpu as pltpu
from jax.sharding import PartitionSpec as P


STEPS = 4
TILE = 8
UNROLL = 19
PIECES = 2
RATE = 0.05
GRID = P("lat", "lon", "lev", None)


def here():
    return [lax.rem(lax.axis_index(axis), 2) for axis in ("lat", "lev", "lon")]


def roles(odd):
    first = 3 * odd
    turn = 1 - 2 * odd
    sign = jnp.where(odd == 0, 1.0, -1.0).astype(jnp.float32)
    return [first + turn * k for k in range(4)], sign


def either(flag, a, b):
    return jnp.where(flag, a, b)


def take_outer(source, *refs):
    place = here()
    pieces, sems = refs[:PIECES], refs[PIECES]
    rows, _ = roles(place[0])
    size = pieces[0].shape[0]
    copies = [
        pltpu.make_async_copy(source.at[rows[0], pl.ds(size * p, size)], pieces[p], sems.at[p])
        for p in range(PIECES)
    ]
    for copy in copies:
        copy.start()
    for copy in copies:
        copy.wait()


def take_all(source, *refs):
    place = here()
    taken, ends, sems = refs[:4], refs[4:8], refs[8]
    rows, _ = roles(place[0])
    even_lev, even_lon = place[1] == 0, place[2] == 0
    copies = [pltpu.make_async_copy(source.at[rows[k]], taken[k], sems.at[k]) for k in range(4)]
    for copy in copies:
        copy.start()
    for k in range(4):
        copies[k].wait()
        send_ends(k, taken[k], ends, even_lev, even_lon)


def send_ends(k, row, ends, even_lev, even_lon):
    length, levels, _ = row.shape

    def body(x, carry):
        low, high = row[x, 0:1], row[x, levels - 1 : levels]
        ends[0][k, pl.ds(x, 1)] = either(even_lev, high, low)
        ends[1][k, pl.ds(x, 1)] = either(even_lev, low, high)
        return carry

    lax.fori_loop(0, length, body, 0, unroll=4)
    low, high = row[0], row[length - 1]
    ends[2][k] = either(even_lon, high, low)
    ends[3][k] = either(even_lon, low, high)


def spread_step(last, *refs):
    place = here()
    for odd in (0, 1):
        pl.when(place[0] == odd)(functools.partial(spread_rows, last, odd, place, *refs))


def spread_rows(last, odd, place, *refs):
    state, refs = refs[:4], refs[4:]
    core_row, near_lev, far_lev, near_lon, far_lon, north, east, upward = refs[:8]
    new = refs[8:12]
    extra = refs[12:]
    rows, _ = roles(odd)
    length, levels, members = new[0].shape
    even_lev, even_lon = place[1] == 0, place[2] == 0
    parts = levels // TILE
    spot = lax.broadcasted_iota(jnp.int32, (TILE, members), 0)
    at_low, at_high = spot == 0, spot == TILE - 1
    for k in range(4):
        row = rows[k]
        inward = core_row if k == 3 else state[k + 1]
        outward = None if k == 0 else state[k - 1]

        def cell(x, before, here, after):
            near, far = near_lev[k, pl.ds(x, 1)], far_lev[k, pl.ds(x, 1)]
            lower, upper = either(even_lev, far, near), either(even_lev, near, far)
            tiles = [here[TILE * j : TILE * (j + 1)] for j in range(parts)]
            from_below = [lower] + [pltpu.roll(t, 1, 0) for t in tiles]
            from_above = [pltpu.roll(t, TILE - 1, 0) for t in tiles] + [upper]
            values = []
            for j in range(parts):
                cut = slice(TILE * j, TILE * (j + 1))
                down = jnp.where(at_low, from_below[j], from_below[j + 1])
                up = jnp.where(at_high, from_above[j + 1], from_above[j])
                inner = inward[x, cut]
                total = (before[cut] + after[cut]) + (down + up)
                if outward is None:
                    total += inner
                    slope = inner
                else:
                    outer = outward[x, cut]
                    total += inner + outer
                    slope = outer - inner if odd else inner - outer
                drift = north[row, x, cut] * slope
                value = (1.0 - 6.0 * RATE) * tiles[j] + RATE * total
                value = value + drift if odd and outward is None else value - drift
                value = (
                    value
                    - east[row, x, cut] * (after[cut] - before[cut])
                    - upward[row, x, cut] * (up - down)
                )
                new[k][x, cut] = value
                values.append(value)
            if not last and k > 0:
                low, high = values[0][0:1], values[-1][TILE - 1 : TILE]
                extra[0][k, pl.ds(x, 1)] = either(even_lev, high, low)
                extra[1][k, pl.ds(x, 1)] = either(even_lev, low, high)
            return jnp.concatenate(values, axis=0)

        start = either(even_lon, far_lon[k], near_lon[k])
        stop = either(even_lon, near_lon[k], far_lon[k])

        def body(x, carry):
            before, here, total = carry
            after = state[k][x + 1]
            value = cell(x, before, here, after)
            return here, after, (total + value if last else total)

        zero = jnp.zeros((levels, members), jnp.float32)
        before, here, total = lax.fori_loop(
            0, length - 1, body, (start, state[k][0], zero), unroll=UNROLL
        )
        value = cell(length - 1, before, here, stop)
        if not last and k > 0:
            low, high = new[k][0], value
            extra[2][k] = either(even_lon, high, low)
            extra[3][k] = either(even_lon, low, high)
        if last and k > 0:
            line_statistics(new[k], total + value, extra[0], 2 * (k - 1))


def line_statistics(row, total, out, at):
    length = row.shape[0]
    mean = total * (1.0 / length)

    def body(x, carry):
        away = row[x] - mean
        return carry + away * away

    out[at] = mean
    out[at + 1] = lax.fori_loop(0, length, body, jnp.zeros_like(mean), unroll=4)


def add_halo(piece, place, part, north, halo, out, inner=None):
    rows, sign = roles(place[0])
    size, levels, members = halo.shape

    def body(x, total):
        at = size * piece + x
        value = part[at] + (RATE + sign * north[rows[0], at]) * halo[x]
        out[x] = value
        if inner is not None:
            inner(at, value)
        return total + value

    zero = jnp.zeros((levels, members), jnp.float32)
    return lax.fori_loop(0, size, body, zero, unroll=4)


def start_row(part, north, halo, out):
    add_halo(0, here(), part, north, halo, out)


def finish_row(last, *refs):
    place = here()
    part, north, halo, done = refs[:4]
    rest = refs[4:]
    size, levels, members = halo.shape
    if last:
        row, stats = rest
    else:
        old, piece, row, ends = rest[:4], rest[4], rest[5], rest[6:]
        for a, b in zip(old, ends):
            b[1:] = a[1:]
    even_lev, even_lon = place[1] == 0, place[2] == 0

    def send(at, value):
        if not last:
            low, high = value[0:1], value[levels - 1 : levels]
            ends[0][0, pl.ds(at, 1)] = either(even_lev, high, low)
            ends[1][0, pl.ds(at, 1)] = either(even_lev, low, high)

    def keep(x, total):
        value = done[x]
        row[x] = value
        send(x, value)
        return total + value

    def both(at, value):
        if not last:
            row[at] = value
        send(at, value)

    zero = jnp.zeros((levels, members), jnp.float32)
    total = lax.fori_loop(0, size, keep, zero, unroll=4)
    if last:
        total += add_halo(1, place, part, north, halo, row.at[pl.ds(size, size)])
        line_statistics(row, total, stats, 0)
    else:
        add_halo(1, place, part, north, halo, piece, both)
        low, high = row[0], row[2 * size - 1]
        ends[2][0] = either(even_lon, high, low)
        ends[3][0] = either(even_lon, low, high)


def normalise(count, *refs):
    state, stats = refs[:count], refs[count : count + 4]
    out, end, work, sems = refs[-4:]
    rows, _ = roles(here()[0])
    offset = 0 if count == 1 else 1
    length = state[0].shape[0]
    copies = [
        pltpu.make_async_copy(state[k], end.at[rows[k + offset]], sems.at[k]) for k in range(count)
    ]
    for copy in copies:
        copy.start()
    for k in range(count):
        means = [s[2 * k] for s in stats]
        mean = 0.25 * ((means[0] + means[1]) + (means[2] + means[3]))
        square = (stats[0][2 * k + 1] + stats[1][2 * k + 1]) + (
            stats[2][2 * k + 1] + stats[3][2 * k + 1]
        )
        for part in means:
            square += length * ((part - mean) * (part - mean))
        scale = lax.rsqrt(square * (1.0 / (4 * length)) + 0.0001)

        def body(x, carry):
            work[k, x] = (state[k][x] - mean) * scale
            return carry

        lax.fori_loop(0, length, body, 0, unroll=4)
        copy = pltpu.make_async_copy(work.at[k], out.at[rows[k + offset]], sems.at[count + k])
        copy.start()
        copies.append(copy)
    for copy in copies:
        copy.wait()


def shards(initial_state, north, east, upward):
    rows_here, length, levels, members = initial_state.shape
    row_type = jax.ShapeDtypeStruct((length, levels, members), jnp.float32)
    piece_type = jax.ShapeDtypeStruct((length // PIECES, levels, members), jnp.float32)
    lev_type = jax.ShapeDtypeStruct((rows_here, length, members), jnp.float32)
    lon_type = jax.ShapeDtypeStruct((rows_here, levels, members), jnp.float32)
    whole = jax.ShapeDtypeStruct(initial_state.shape, jnp.float32)
    vmem = pl.BlockSpec(memory_space=pltpu.VMEM)
    anywhere = pl.BlockSpec(memory_space=pl.ANY)

    def call(kernel, args, outs, flops, aliases={}, in_specs=None, out_specs=None, scratch=(), room=2**20):
        return pl.pallas_call(
            kernel,
            out_shape=outs,
            in_specs=in_specs or [vmem] * len(args),
            out_specs=out_specs or [vmem] * len(outs),
            scratch_shapes=list(scratch),
            input_output_aliases=aliases,
            compiler_params=pltpu.CompilerParams(vmem_limit_bytes=room),
            cost_estimate=pl.CostEstimate(flops=flops, bytes_accessed=0, transcendentals=0),
        )(*args)

    lats, lons = lax.axis_size("lat"), lax.axis_size("lon")

    def pairs(count, start):
        out = []
        for i in range(start, count - 1, 2):
            out += [(i, i + 1), (i + 1, i)]
        return out

    def across(array):
        return lax.ppermute(array, "lat", pairs(lats, 1))

    def beside(array):
        return lax.ppermute(array, "lat", pairs(lats, 0))

    def swap(array, axis, start):
        return lax.ppermute(array, axis, pairs(lax.axis_size(axis), start))

    def ends_of(near_lev, far_lev, near_lon, far_lon):
        return [
            swap(near_lev, "lev", 0),
            swap(far_lev, "lev", 1),
            swap(near_lon, "lon", 0),
            swap(far_lon, "lon", 1),
        ]

    def from_others(array):
        made = []
        for d in (1, 2, 3):
            made.append(lax.ppermute(array, "lon", [(i, i ^ d) for i in range(lons)]))
        return made

    stats_type = jax.ShapeDtypeStruct((2 * rows_here - 2, levels, members), jnp.float32)
    end_types = [lev_type, lev_type, lon_type, lon_type]
    source = pltpu.with_memory_space_constraint(initial_state, pltpu.HBM)
    winds = [pltpu.with_memory_space_constraint(w, pltpu.VMEM) for w in (north, east, upward)]
    for step in range(STEPS):
        last = step == STEPS - 1
        if step == 0:
            pieces = call(
                take_outer,
                [source],
                [piece_type] * PIECES,
                10**6,
                in_specs=[anywhere],
                scratch=[pltpu.SemaphoreType.DMA((PIECES,))],
            )
            halos = [across(piece) for piece in pieces]
            outer, *inner_rows, near, far, close, distant = call(
                take_all,
                [source],
                [row_type] * 4 + end_types,
                10**9,
                in_specs=[anywhere],
                scratch=[pltpu.SemaphoreType.DMA((4,))],
            )
            core_row = beside(inner_rows[2])
            ends = ends_of(near, far, close, distant)
        else:
            (begun,) = call(
                start_row, [part, winds[0], halos[0]], [piece_type], 10**9
            )
            first_halo = across(begun)
            ended, outer, *sent = call(
                functools.partial(finish_row, False),
                [part, winds[0], halos[1], begun, *extra],
                [piece_type, row_type, *end_types],
                10**9,
            )
            halos = [first_halo, across(ended)]
            ends = ends_of(*sent)
        part, *made = call(
            functools.partial(spread_step, last),
            [outer, *inner_rows, core_row, *ends, *winds],
            [row_type] * 4 + ([stats_type] if last else end_types),
            SPREAD_FLOPS,
        )
        inner_rows, extra = made[:3], made[3:]
        if not last:
            core_row = beside(inner_rows[2])

    def normalised(rows_of, stats, others, *results):
        count = len(rows_of)
        return call(
            functools.partial(normalise, count),
            [*rows_of, stats, *others, *results],
            [whole, whole],
            10**9,
            aliases={count + 4 + i: i for i in range(len(results))},
            in_specs=[vmem] * (count + 4) + [anywhere] * len(results),
            out_specs=[anywhere, anywhere],
            scratch=[
                pltpu.VMEM((count, length, levels, members), jnp.float32),
                pltpu.SemaphoreType.DMA((2 * count,)),
            ],
            room=8 * 2**20,
        )

    (begun,) = call(start_row, [part, winds[0], halos[0]], [piece_type], 10**9)
    early = from_others(extra[0])
    outer, stats = call(
        functools.partial(finish_row, True),
        [part, winds[0], halos[1], begun],
        [row_type, jax.ShapeDtypeStruct((2, levels, members), jnp.float32)],
        10**9,
    )
    late = from_others(stats)
    results = normalised(inner_rows, extra[0], early)
    return tuple(normalised([outer], stats, late, *results))


SPREAD_FLOPS = 2 * 10**10


def solution(mesh):
    return jax.shard_map(
        shards, mesh=mesh, in_specs=(GRID,) * 4, out_specs=(GRID, GRID), check_vma=False
    )
```

time: 142 us -> 164 us (1.15)
  waiting for transfers between devices: 44.7 us -> 60.8 us
  starting transfers between devices: 48.4 us -> 62.6 us
  Pallas kernels: 44 us -> 32.3 us
  local copies, waits for them, and re-layouts: 2.8 us -> 5.58 us
    ppermute x4 -> x8, starting transfers between devices: 7.65 us -> 22.4 us  [across(): return lax.ppermute(array, 'lat', pairs(lats, 1))]
    pallas_call x12 -> x16, Pallas kernels: 44 us -> 32.3 us  [call(): pl.pallas_call(kernel, out_shape=outs, in_specs=in_specs or [vmem] * len(...]
    ppermute x4 -> x8, waiting for transfers between devices: 42.4 us -> 53.8 us  [across(): return lax.ppermute(array, 'lat', pairs(lats, 1))]
    ppermute x16, waiting for transfers between devices: 2.3 us -> 7.03 us  [swap(): return lax.ppermute(array, axis, pairs(lax.axis_size(axis), start))]
    unnamed x10 -> x14, local copies, waits for them, and re-layouts: 2.8 us -> 5.58 us
  transfers between devices with their start and end apart: 30 -> 34, of which waited for: 8 -> 13; matrix products, arithmetic and copies ran while one was open for 0% -> 0% of each run, Pallas kernels for 25% -> 8%
where the time goes in v2:
time: 164 us; the launch traced here: 163 us
  starting transfers between devices  62.6 us (38%)
  waiting for transfers between devices  60.8 us (37%)
  Pallas kernels  32.3 us (20%)
  local copies, waits for them, and re-layouts  5.58 us (3%)
    ppermute x8, waiting for transfers between devices, across(): return lax.ppermute(array, 'lat', pairs(lats, 1))  53.8 us
    pallas_call x16, Pallas kernels, call(): pl.pallas_call(kernel, out_shape=outs, in_specs=in_specs or [vmem] * len(...  32.3 us
    ppermute x16, starting transfers between devices, swap(): return lax.ppermute(array, axis, pairs(lax.axis_size(axis), start))  31.3 us
    ppermute x8, starting transfers between devices, across(): return lax.ppermute(array, 'lat', pairs(lats, 1))  22.4 us
    ppermute x6, starting transfers between devices, from_others(): made.append(lax.ppermute(array, 'lon', [(i, i ^ d) for i in range(lons)]))  8.51 us
    ppermute x16, waiting for transfers between devices, swap(): return lax.ppermute(array, axis, pairs(lax.axis_size(axis), start))  7.03 us
    unnamed x14, local copies, waits for them, and re-layouts  5.58 us
  transfers between devices with their start and end apart: 34, of which 13 were waited for; matrix products, arithmetic and copies ran while one was open for 0% of the time, Pallas kernels for 8%

profile of v2, /device:TPU:14, one launch (start us, length us, event | category | flops | bytes accessed | tf_op | source)
XLA Modules:
  0.0 162.6 jit_solution(9705920836704094911)
XLA Ops:
  0.6 3.2 %shard_map.59 = (f32[96,32,128]{2,1,0:T(8,128)S(1)}, f32[96,32,128]{2,1,0:T(8,128)S(1)}, f32[96,32,128]{2,1,0:T(8,128)S(1)}, f32[96,32,128]{2,1,0:T(8,128)S(1)},...) custom-call(f32[4,96,32,128]{3,2,1,0:T(8,128)} %source.3), custom_call_target="tpu_custom_call" | custom-call | flops 1000000000 | tf_op jit(solution)/shard_map/pallas_call | solution.py:275
  3.8 0.1 collective-permute-start
  3.9 2.0 %collective-permute-start.1 = (f32[4,96,128]{2,1,0:T(8,128)S(1)}, f32[4,96,128]{2,1,0:T(8,128)S(1)}, u32[]{:S(2)}, u32[]{:S(2)}) collective-permute-start(f32[4,96,128]{2,1,0:T(8,128)S(1)} %get-tuple-element.67), channel_id=1, source_target_pairs={{0,1},{1,0},{2,3},{3,2},{4,5},{5,4},{6,7},{7,6},{8,9},{9,8},{10,11... | collective-permute-start | bytes 589832 | tf_op jit(solution)/shard_map/ppermute | solution.py:301
  5.9 0.7 collective-permute-start.2
  6.6 0.5 collective-permute-start.3
  7.1 4.3 %collective-permute-start.4 = (f32[4,32,128]{2,1,0:T(8,128)S(1)}, f32[4,32,128]{2,1,0:T(8,128)S(1)}, u32[]{:S(2)}, u32[]{:S(2)}) collective-permute-start(f32[4,32,128]{2,1,0:T(8,128)S(1)} %get-tuple-element.70), channel_id=1, source_target_pairs={{4,8},{8,4},{5,9},{9,5},{6,10},{10,6},{7,11},{11,7},{20,24},{24,20... | collective-permute-start | bytes 196616 | tf_op jit(solution)/shard_map/ppermute | solution.py:301
  11.4 2.2 %collective-permute-done.4.refs_8_ = f32[4,32,128]{2,1,0:T(8,128)S(1)} collective-permute-done((f32[4,32,128]{2,1,0:T(8,128)S(1)}, f32[4,32,128]{2,1,0:T(8,128)S(1)}, u32[]{:S(2)}, u32[]{:S(2)}) %collective-permute-start.4) | collective-permute-done | bytes 65568 | tf_op jit(solution)/shard_map/ppermute | solution.py:301
  13.7 2.8 %copy-done.1 = f32[4,96,32,128]{3,2,1,0:T(8,128)S(1)} copy-done((f32[4,96,32,128]{3,2,1,0:T(8,128)S(1)}, f32[4,96,32,128]{3,2,1,0:T(8,128)}, u32[]{:S(2)}) %copy-start.1) | copy-done | bytes 6291480
  16.5 2.8 %copy-done.2 = f32[4,96,32,128]{3,2,1,0:T(8,128)S(1)} copy-done((f32[4,96,32,128]{3,2,1,0:T(8,128)S(1)}, f32[4,96,32,128]{3,2,1,0:T(8,128)}, u32[]{:S(2)}) %copy-start.2) | copy-done | bytes 6291480
  19.3 4.8 %shard_map.60 = (f32[96,32,128]{2,1,0:T(8,128)S(1)}, f32[96,32,128]{2,1,0:T(8,128)S(1)}, f32[96,32,128]{2,1,0:T(8,128)S(1)}, f32[96,32,128]{2,1,0:T(8,128)S(1)},...) custom-call(f32[96,32,128]{2,1,0:T(8,128)S(1)} %get-tuple-element.63, ...), custom_call_target="tpu_custom_call" | custom-call | flops 20000000000 | tf_op jit(solution)/shard_map/pallas_call | solution.py:275
  24.0 0.1 collective-permute-start.7
  24.1 1.4 shard_map.61
  25.5 2.8 %collective-permute-start.6 = (f32[48,32,128]{2,1,0:T(8,128)S(1)}, f32[48,32,128]{2,1,0:T(8,128)S(1)}, u32[]{:S(2)}, u32[]{:S(2)}) collective-permute-start(f32[48,32,128]{2,1,0:T(8,128)S(1)} %get-tuple-element.73), channel_id=1, source_target_pairs={{16,32},{32,16},{48,64},{64,48},{80,96},{96,80},{17,33},{33,17},{4... | collective-permute-start | bytes 2359304 | tf_op jit(solution)/shard_map/ppermute | solution.py:295
  28.4 2.7 %collective-permute-start.5 = (f32[48,32,128]{2,1,0:T(8,128)S(1)}, f32[48,32,128]{2,1,0:T(8,128)S(1)}, u32[]{:S(2)}, u32[]{:S(2)}) collective-permute-start(f32[48,32,128]{2,1,0:T(8,128)S(1)} %get-tuple-element.72), channel_id=1, source_target_pairs={{16,32},{32,16},{48,64},{64,48},{80,96},{96,80},{17,33},{33,17},{4... | collective-permute-start | bytes 2359304 | tf_op jit(solution)/shard_map/ppermute | solution.py:295
  31.1 7.7 %collective-permute-done.6.halo = f32[48,32,128]{2,1,0:T(8,128)S(1)} collective-permute-done((f32[48,32,128]{2,1,0:T(8,128)S(1)}, f32[48,32,128]{2,1,0:T(8,128)S(1)}, u32[]{:S(2)}, u32[]{:S(2)}) %collective-permute-start.6) | collective-permute-done | bytes 786464 | tf_op jit(solution)/shard_map/ppermute | solution.py:295
  38.8 0.2 shard_map.62.refs_3_
  39.0 8.2 %collective-permute-done.5.refs_2_ = f32[48,32,128]{2,1,0:T(8,128)S(1)} collective-permute-done((f32[48,32,128]{2,1,0:T(8,128)S(1)}, f32[48,32,128]{2,1,0:T(8,128)S(1)}, u32[]{:S(2)}, u32[]{:S(2)}) %collective-permute-start.5) | collective-permute-done | bytes 786464 | tf_op jit(solution)/shard_map/ppermute | solution.py:295
  47.3 0.4 shard_map.63
  47.7 4.9 %collective-permute-start.8 = (f32[4,96,128]{2,1,0:T(8,128)S(1)}, f32[4,96,128]{2,1,0:T(8,128)S(1)}, u32[]{:S(2)}, u32[]{:S(2)}) collective-permute-start(f32[4,96,128]{2,1,0:T(8,128)S(1)} %get-tuple-element.82), channel_id=1, source_target_pairs={{0,1},{1,0},{2,3},{3,2},{4,5},{5,4},{6,7},{7,6},{8,9},{9,8},{10,11... | collective-permute-start | bytes 589832 | tf_op jit(solution)/shard_map/ppermute | solution.py:301
  52.5 0.7 collective-permute-start.9
  53.2 0.1 collective-permute-start.10
  53.3 3.9 %collective-permute-start.11 = (f32[4,32,128]{2,1,0:T(8,128)S(1)}, f32[4,32,128]{2,1,0:T(8,128)S(1)}, u32[]{:S(2)}, u32[]{:S(2)}) collective-permute-start(f32[4,32,128]{2,1,0:T(8,128)S(1)} %get-tuple-element.85), channel_id=1, source_target_pairs={{4,8},{8,4},{5,9},{9,5},{6,10},{10,6},{7,11},{11,7},{20,24},{24,20... | collective-permute-start | bytes 196616 | tf_op jit(solution)/shard_map/ppermute | solution.py:301
  57.2 0.3 collective-permute-done.10.refs_7_
  57.5 1.9 %collective-permute-done.11.refs_8_ = f32[4,32,128]{2,1,0:T(8,128)S(1)} collective-permute-done((f32[4,32,128]{2,1,0:T(8,128)S(1)}, f32[4,32,128]{2,1,0:T(8,128)S(1)}, u32[]{:S(2)}, u32[]{:S(2)}) %collective-permute-start.11) | collective-permute-done | bytes 65568 | tf_op jit(solution)/shard_map/ppermute | solution.py:301
  59.5 4.8 %shard_map.64 = (f32[96,32,128]{2,1,0:T(8,128)S(1)}, f32[96,32,128]{2,1,0:T(8,128)S(1)}, f32[96,32,128]{2,1,0:T(8,128)S(1)}, f32[96,32,128]{2,1,0:T(8,128)S(1)},...) custom-call(f32[96,32,128]{2,1,0:T(8,128)S(1)} %get-tuple-element.78, ...), custom_call_target="tpu_custom_call" | custom-call | flops 20000000000 | tf_op jit(solution)/shard_map/pallas_call | solution.py:275
  64.3 0.1 collective-permute-start.14
  64.4 3.0 %collective-permute-start.13 = (f32[48,32,128]{2,1,0:T(8,128)S(1)}, f32[48,32,128]{2,1,0:T(8,128)S(1)}, u32[]{:S(2)}, u32[]{:S(2)}) collective-permute-start(f32[48,32,128]{2,1,0:T(8,128)S(1)} %shard_map.62.refs_3_), channel_id=1, source_target_pairs={{16,32},{32,16},{48,64},{64,48},{80,96},{96,80},{17,33},{33,17},{4... | collective-permute-start | bytes 2359304 | tf_op jit(solution)/shard_map/ppermute | solution.py:295
  67.4 2.5 %collective-permute-start.12 = (f32[48,32,128]{2,1,0:T(8,128)S(1)}, f32[48,32,128]{2,1,0:T(8,128)S(1)}, u32[]{:S(2)}, u32[]{:S(2)}) collective-permute-start(f32[48,32,128]{2,1,0:T(8,128)S(1)} %get-tuple-element.87), channel_id=1, source_target_pairs={{16,32},{32,16},{48,64},{64,48},{80,96},{96,80},{17,33},{33,17},{4... | collective-permute-start | bytes 2359304 | tf_op jit(solution)/shard_map/ppermute | solution.py:295
  70.0 7.7 %collective-permute-done.13.halo = f32[48,32,128]{2,1,0:T(8,128)S(1)} collective-permute-done((f32[48,32,128]{2,1,0:T(8,128)S(1)}, f32[48,32,128]{2,1,0:T(8,128)S(1)}, u32[]{:S(2)}, u32[]{:S(2)}) %collective-permute-start.13) | collective-permute-done | bytes 786464 | tf_op jit(solution)/shard_map/ppermute | solution.py:295
  77.7 0.2 shard_map.65.refs_3_
  77.9 8.2 %collective-permute-done.12.refs_2_ = f32[48,32,128]{2,1,0:T(8,128)S(1)} collective-permute-done((f32[48,32,128]{2,1,0:T(8,128)S(1)}, f32[48,32,128]{2,1,0:T(8,128)S(1)}, u32[]{:S(2)}, u32[]{:S(2)}) %collective-permute-start.12) | collective-permute-done | bytes 786464 | tf_op jit(solution)/shard_map/ppermute | solution.py:295
  86.1 0.4 shard_map.66
  86.5 2.3 %collective-permute-start.15 = (f32[4,96,128]{2,1,0:T(8,128)S(1)}, f32[4,96,128]{2,1,0:T(8,128)S(1)}, u32[]{:S(2)}, u32[]{:S(2)}) collective-permute-start(f32[4,96,128]{2,1,0:T(8,128)S(1)} %get-tuple-element.96), channel_id=1, source_target_pairs={{0,1},{1,0},{2,3},{3,2},{4,5},{5,4},{6,7},{7,6},{8,9},{9,8},{10,11... | collective-permute-start | bytes 589832 | tf_op jit(solution)/shard_map/ppermute | solution.py:301
  88.8 0.7 collective-permute-start.16
  89.4 0.1 collective-permute-start.17
  89.5 3.9 %collective-permute-start.18 = (f32[4,32,128]{2,1,0:T(8,128)S(1)}, f32[4,32,128]{2,1,0:T(8,128)S(1)}, u32[]{:S(2)}, u32[]{:S(2)}) collective-permute-start(f32[4,32,128]{2,1,0:T(8,128)S(1)} %get-tuple-element.99), channel_id=1, source_target_pairs={{4,8},{8,4},{5,9},{9,5},{6,10},{10,6},{7,11},{11,7},{20,24},{24,20... | collective-permute-start | bytes 196616 | tf_op jit(solution)/shard_map/ppermute | solution.py:301
  93.5 0.3 collective-permute-done.17.refs_7_
  93.8 1.9 %collective-permute-done.18.refs_8_ = f32[4,32,128]{2,1,0:T(8,128)S(1)} collective-permute-done((f32[4,32,128]{2,1,0:T(8,128)S(1)}, f32[4,32,128]{2,1,0:T(8,128)S(1)}, u32[]{:S(2)}, u32[]{:S(2)}) %collective-permute-start.18) | collective-permute-done | bytes 65568 | tf_op jit(solution)/shard_map/ppermute | solution.py:301
  95.7 4.8 %shard_map.67 = (f32[96,32,128]{2,1,0:T(8,128)S(1)}, f32[96,32,128]{2,1,0:T(8,128)S(1)}, f32[96,32,128]{2,1,0:T(8,128)S(1)}, f32[96,32,128]{2,1,0:T(8,128)S(1)},...) custom-call(f32[96,32,128]{2,1,0:T(8,128)S(1)} %get-tuple-element.92, ...), custom_call_target="tpu_custom_call" | custom-call | flops 20000000000 | tf_op jit(solution)/shard_map/pallas_call | solution.py:275
  100.5 0.1 collective-permute-start.21
  100.6 3.4 %collective-permute-start.20 = (f32[48,32,128]{2,1,0:T(8,128)S(1)}, f32[48,32,128]{2,1,0:T(8,128)S(1)}, u32[]{:S(2)}, u32[]{:S(2)}) collective-permute-start(f32[48,32,128]{2,1,0:T(8,128)S(1)} %shard_map.65.refs_3_), channel_id=1, source_target_pairs={{16,32},{32,16},{48,64},{64,48},{80,96},{96,80},{17,33},{33,17},{4... | collective-permute-start | bytes 2359304 | tf_op jit(solution)/shard_map/ppermute | solution.py:295
  104.0 2.2 %collective-permute-start.19 = (f32[48,32,128]{2,1,0:T(8,128)S(1)}, f32[48,32,128]{2,1,0:T(8,128)S(1)}, u32[]{:S(2)}, u32[]{:S(2)}) collective-permute-start(f32[48,32,128]{2,1,0:T(8,128)S(1)} %get-tuple-element.101), channel_id=1, source_target_pairs={{16,32},{32,16},{48,64},{64,48},{80,96},{96,80},{17,33},{33,17},{4... | collective-permute-start | bytes 2359304 | tf_op jit(solution)/shard_map/ppermute | solution.py:295
  106.2 7.7 %collective-permute-done.20.halo = f32[48,32,128]{2,1,0:T(8,128)S(1)} collective-permute-done((f32[48,32,128]{2,1,0:T(8,128)S(1)}, f32[48,32,128]{2,1,0:T(8,128)S(1)}, u32[]{:S(2)}, u32[]{:S(2)}) %collective-permute-start.20) | collective-permute-done | bytes 786464 | tf_op jit(solution)/shard_map/ppermute | solution.py:295
  113.9 0.2 shard_map.68.refs_3_
  114.1 8.2 %collective-permute-done.19.refs_2_ = f32[48,32,128]{2,1,0:T(8,128)S(1)} collective-permute-done((f32[48,32,128]{2,1,0:T(8,128)S(1)}, f32[48,32,128]{2,1,0:T(8,128)S(1)}, u32[]{:S(2)}, u32[]{:S(2)}) %collective-permute-start.19) | collective-permute-done | bytes 786464 | tf_op jit(solution)/shard_map/ppermute | solution.py:295
  122.3 0.4 shard_map.69
  122.7 2.7 %collective-permute-start.22 = (f32[4,96,128]{2,1,0:T(8,128)S(1)}, f32[4,96,128]{2,1,0:T(8,128)S(1)}, u32[]{:S(2)}, u32[]{:S(2)}) collective-permute-start(f32[4,96,128]{2,1,0:T(8,128)S(1)} %get-tuple-element.110), channel_id=1, source_target_pairs={{0,1},{1,0},{2,3},{3,2},{4,5},{5,4},{6,7},{7,6},{8,9},{9,8},{10,11... | collective-permute-start | bytes 589832 | tf_op jit(solution)/shard_map/ppermute | solution.py:301
  125.4 0.7 collective-permute-start.23
  126.1 0.1 collective-permute-start.24
  126.2 3.9 %collective-permute-start.25 = (f32[4,32,128]{2,1,0:T(8,128)S(1)}, f32[4,32,128]{2,1,0:T(8,128)S(1)}, u32[]{:S(2)}, u32[]{:S(2)}) collective-permute-start(f32[4,32,128]{2,1,0:T(8,128)S(1)} %get-tuple-element.113), channel_id=1, source_target_pairs={{4,8},{8,4},{5,9},{9,5},{6,10},{10,6},{7,11},{11,7},{20,24},{24,20... | collective-permute-start | bytes 196616 | tf_op jit(solution)/shard_map/ppermute | solution.py:301
  130.1 0.3 collective-permute-done.24.refs_7_
  130.4 2.1 %collective-permute-start.27 = (f32[48,32,128]{2,1,0:T(8,128)S(1)}, f32[48,32,128]{2,1,0:T(8,128)S(1)}, u32[]{:S(2)}, u32[]{:S(2)}) collective-permute-start(f32[48,32,128]{2,1,0:T(8,128)S(1)} %shard_map.68.refs_3_), channel_id=1, source_target_pairs={{16,32},{32,16},{48,64},{64,48},{80,96},{96,80},{17,33},{33,17},{4... | collective-permute-start | bytes 2359304 | tf_op jit(solution)/shard_map/ppermute | solution.py:295
  132.6 3.6 %collective-permute-start.26 = (f32[48,32,128]{2,1,0:T(8,128)S(1)}, f32[48,32,128]{2,1,0:T(8,128)S(1)}, u32[]{:S(2)}, u32[]{:S(2)}) collective-permute-start(f32[48,32,128]{2,1,0:T(8,128)S(1)} %get-tuple-element.115), channel_id=1, source_target_pairs={{16,32},{32,16},{48,64},{64,48},{80,96},{96,80},{17,33},{33,17},{4... | collective-permute-start | bytes 2359304 | tf_op jit(solution)/shard_map/ppermute | solution.py:295
  136.2 5.6 %shard_map.70 = (f32[96,32,128]{2,1,0:T(8,128)S(1)}, f32[96,32,128]{2,1,0:T(8,128)S(1)}, f32[96,32,128]{2,1,0:T(8,128)S(1)}, f32[96,32,128]{2,1,0:T(8,128)S(1)}, f32[6,32,128]{2,1,0:T(8,128)S(1)}) custom-call(f32[96,32,128]{2,1,0:T(8,128)S(1)} %get-tuple-element.106.refs_0_, f32[96,32,128]{2,1,0:T(8,128)S(1)} %get-tuple-element.107.refs_1_, ...), custom_call_target="tpu_custom_call" | custom-call | flops 20000000000 | tf_op jit(solution)/shard_map/pallas_call | solution.py:275
  141.9 2.1 %collective-permute-start.33 = (f32[6,32,128]{2,1,0:T(8,128)S(1)}, f32[6,32,128]{2,1,0:T(8,128)S(1)}, u32[]{:S(2)}, u32[]{:S(2)}) collective-permute-start(f32[6,32,128]{2,1,0:T(8,128)S(1)} %get-tuple-element.121.refs_3_), channel_id=1, source_target_pairs={{0,12},{4,8},{8,4},{12,0},{1,13},{5,9},{9,5},{13,1},{2,14},{6,10},... | collective-permute-start | bytes 294920 | tf_op jit(solution)/shard_map/ppermute | solution.py:314
  144.0 0.1 collective-permute-start.32
  144.0 2.1 %collective-permute-start.31 = (f32[6,32,128]{2,1,0:T(8,128)S(1)}, f32[6,32,128]{2,1,0:T(8,128)S(1)}, u32[]{:S(2)}, u32[]{:S(2)}) collective-permute-start(f32[6,32,128]{2,1,0:T(8,128)S(1)} %get-tuple-element.121.refs_3_), channel_id=1, source_target_pairs={{0,4},{4,0},{8,12},{12,8},{1,5},{5,1},{9,13},{13,9},{2,6},{6,2},{1... | collective-permute-start | bytes 294920 | tf_op jit(solution)/shard_map/ppermute | solution.py:314
  146.1 0.2 shard_map.71.refs_3_
  146.3 5.9 %collective-permute-done.26.refs_2_ = f32[48,32,128]{2,1,0:T(8,128)S(1)} collective-permute-done((f32[48,32,128]{2,1,0:T(8,128)S(1)}, f32[48,32,128]{2,1,0:T(8,128)S(1)}, u32[]{:S(2)}, u32[]{:S(2)}) %collective-permute-start.26) | collective-permute-done | bytes 786464 | tf_op jit(solution)/shard_map/ppermute | solution.py:295
  152.2 0.5 shard_map.72
  152.7 2.1 %collective-permute-start.30 = (f32[2,32,128]{2,1,0:T(8,128)S(1)}, f32[2,32,128]{2,1,0:T(8,128)S(1)}, u32[]{:S(2)}, u32[]{:S(2)}) collective-permute-start(f32[2,32,128]{2,1,0:T(8,128)S(1)} %get-tuple-element.117.refs_1_), channel_id=1, source_target_pairs={{0,12},{4,8},{8,4},{12,0},{1,13},{5,9},{9,5},{13,1},{2,14},{6,10},... | collective-permute-start | bytes 98312 | tf_op jit(solution)/shard_map/ppermute | solution.py:314
  154.9 2.1 %collective-permute-start.28 = (f32[2,32,128]{2,1,0:T(8,128)S(1)}, f32[2,32,128]{2,1,0:T(8,128)S(1)}, u32[]{:S(2)}, u32[]{:S(2)}) collective-permute-start(f32[2,32,128]{2,1,0:T(8,128)S(1)} %get-tuple-element.117.refs_1_), channel_id=1, source_target_pairs={{0,4},{4,0},{8,12},{12,8},{1,5},{5,1},{9,13},{13,9},{2,6},{6,2},{1... | collective-permute-start | bytes 98312 | tf_op jit(solution)/shard_map/ppermute | solution.py:314
  157.0 3.7 %shard_map.73 = (f32[4,96,32,128]{3,2,1,0:T(8,128)}, f32[4,96,32,128]{3,2,1,0:T(8,128)}) custom-call(f32[96,32,128]{2,1,0:T(8,128)S(1)} %get-tuple-element.118.refs_0_, f32[96,32,128]{2,1,0:T(8,128)S(1)} %get-tuple-element.119.refs_1_, f32[96,32,128]{2,1,0:T(8,128)S(1)} %get-tuple-element.120.refs_2_, f32[6,32,128]{2,1,0:T(8,128)S(1)} %get-tuple-element.121.refs_3_, ...), custom_call_target="tpu_custom_call" | custom-call | flops 1000000000 | tf_op jit(solution)/shard_map/pallas_call | solution.py:275
  160.7 1.7 %shard_map.74 = (f32[4,96,32,128]{3,2,1,0:T(8,128)}, f32[4,96,32,128]{3,2,1,0:T(8,128)}) custom-call(f32[96,32,128]{2,1,0:T(8,128)S(1)} %get-tuple-element.116.refs_0_, f32[2,32,128]{2,1,0:T(8,128)S(1)} %get-tuple-element.117.refs_1_, f32[2,32,128]{2,1,0:T(8,128)S(1)} %collective-permute-done.28.refs_2_, ...), custom_call_target="tpu_custom_call", output_to_operand_aliasing={{0}: (5, {}), {1}: (6, {})} | custom-call | flops 1000000000 | tf_op jit(solution)/shard_map/pallas_call | solution.py:275
  (36 shorter events, 0.1 us)
Async XLA Ops:
  0.6 13.0 %copy-start = (f32[4,96,32,128]{3,2,1,0:T(8,128)S(1)}, f32[4,96,32,128]{3,2,1,0:T(8,128)}, u32[]{:S(2)}) copy-start(f32[4,96,32,128]{3,2,1,0:T(8,128)} %refs_1_.7) | copy-start | bytes 18874372
  3.8 9.8 %collective-permute-start = (f32[96,32,128]{2,1,0:T(8,128)S(1)}, f32[96,32,128]{2,1,0:T(8,128)S(1)}, u32[]{:S(2)}, u32[]{:S(2)}) collective-permute-start(f32[96,32,128]{2,1,0:T(8,128)S(1)} %get-tuple-element.66.refs_3_), channel_id=1, source_target_pairs={{0,16},{16,0},{32,48},{48,32},{64,80},{80,64},{96,112},{112,96},{1... | collective-permute-start | bytes 4718600 | tf_op jit(solution)/shard_map/ppermute | solution.py:298
  3.9 9.7 %collective-permute-start.1 = (f32[4,96,128]{2,1,0:T(8,128)S(1)}, f32[4,96,128]{2,1,0:T(8,128)S(1)}, u32[]{:S(2)}, u32[]{:S(2)}) collective-permute-start(f32[4,96,128]{2,1,0:T(8,128)S(1)} %get-tuple-element.67), channel_id=1, source_target_pairs={{0,1},{1,0},{2,3},{3,2},{4,5},{5,4},{6,7},{7,6},{8,9},{9,8},{10,11... | collective-permute-start | bytes 589832 | tf_op jit(solution)/shard_map/ppermute | solution.py:301
  5.9 7.7 %collective-permute-start.2 = (f32[4,96,128]{2,1,0:T(8,128)S(1)}, f32[4,96,128]{2,1,0:T(8,128)S(1)}, u32[]{:S(2)}, u32[]{:S(2)}) collective-permute-start(f32[4,96,128]{2,1,0:T(8,128)S(1)} %get-tuple-element.68), channel_id=1, source_target_pairs={{1,2},{2,1},{5,6},{6,5},{9,10},{10,9},{13,14},{14,13},{17,18},{18,... | collective-permute-start | bytes 589832 | tf_op jit(solution)/shard_map/ppermute | solution.py:301
  6.6 4.8 %collective-permute-start.3 = (f32[4,32,128]{2,1,0:T(8,128)S(1)}, f32[4,32,128]{2,1,0:T(8,128)S(1)}, u32[]{:S(2)}, u32[]{:S(2)}) collective-permute-start(f32[4,32,128]{2,1,0:T(8,128)S(1)} %get-tuple-element.69), channel_id=1, source_target_pairs={{0,4},{4,0},{8,12},{12,8},{1,5},{5,1},{9,13},{13,9},{2,6},{6,2},{1... | collective-permute-start | bytes 196616 | tf_op jit(solution)/shard_map/ppermute | solution.py:301
  7.1 6.5 %collective-permute-start.4 = (f32[4,32,128]{2,1,0:T(8,128)S(1)}, f32[4,32,128]{2,1,0:T(8,128)S(1)}, u32[]{:S(2)}, u32[]{:S(2)}) collective-permute-start(f32[4,32,128]{2,1,0:T(8,128)S(1)} %get-tuple-element.70), channel_id=1, source_target_pairs={{4,8},{8,4},{5,9},{9,5},{6,10},{10,6},{7,11},{11,7},{20,24},{24,20... | collective-permute-start | bytes 196616 | tf_op jit(solution)/shard_map/ppermute | solution.py:301
  13.7 2.8 %copy-start.1 = (f32[4,96,32,128]{3,2,1,0:T(8,128)S(1)}, f32[4,96,32,128]{3,2,1,0:T(8,128)}, u32[]{:S(2)}) copy-start(f32[4,96,32,128]{3,2,1,0:T(8,128)} %refs_10_.7) | copy-start | bytes 18874372
  16.5 2.8 %copy-start.2 = (f32[4,96,32,128]{3,2,1,0:T(8,128)S(1)}, f32[4,96,32,128]{3,2,1,0:T(8,128)}, u32[]{:S(2)}) copy-start(f32[4,96,32,128]{3,2,1,0:T(8,128)} %refs_11_.7) | copy-start | bytes 18874372
  24.0 35.4 %collective-permute-start.7 = (f32[96,32,128]{2,1,0:T(8,128)S(1)}, f32[96,32,128]{2,1,0:T(8,128)S(1)}, u32[]{:S(2)}, u32[]{:S(2)}) collective-permute-start(f32[96,32,128]{2,1,0:T(8,128)S(1)} %get-tuple-element.81.refs_3_), channel_id=1, source_target_pairs={{0,16},{16,0},{32,48},{48,32},{64,80},{80,64},{96,112},{112,96},{1... | collective-permute-start | bytes 4718600 | tf_op jit(solution)/shard_map/ppermute | solution.py:298
  25.5 13.3 %collective-permute-start.6 = (f32[48,32,128]{2,1,0:T(8,128)S(1)}, f32[48,32,128]{2,1,0:T(8,128)S(1)}, u32[]{:S(2)}, u32[]{:S(2)}) collective-permute-start(f32[48,32,128]{2,1,0:T(8,128)S(1)} %get-tuple-element.73), channel_id=1, source_target_pairs={{16,32},{32,16},{48,64},{64,48},{80,96},{96,80},{17,33},{33,17},{4... | collective-permute-start | bytes 2359304 | tf_op jit(solution)/shard_map/ppermute | solution.py:295
  28.4 18.9 %collective-permute-start.5 = (f32[48,32,128]{2,1,0:T(8,128)S(1)}, f32[48,32,128]{2,1,0:T(8,128)S(1)}, u32[]{:S(2)}, u32[]{:S(2)}) collective-permute-start(f32[48,32,128]{2,1,0:T(8,128)S(1)} %get-tuple-element.72), channel_id=1, source_target_pairs={{16,32},{32,16},{48,64},{64,48},{80,96},{96,80},{17,33},{33,17},{4... | collective-permute-start | bytes 2359304 | tf_op jit(solution)/shard_map/ppermute | solution.py:295
  38.8 20.6 %slice-start = ((s8[6291456]{0:T(1024)(128)(4,1)}), s8[4194304]{0:T(1024)(128)(4,1)S(1)}, s32[]{:S(2)}) async-start(s8[6291456]{0:T(1024)(128)(4,1)} %bitcast), calls=%async_computation | async-start | bytes 8388608
  38.8 20.6 %slice-start.2 = ((s8[6291456]{0:T(1024)(128)(4,1)}), s8[4194304]{0:T(1024)(128)(4,1)S(1)}, s32[]{:S(2)}) async-start(s8[6291456]{0:T(1024)(128)(4,1)} %bitcast.2), calls=%async_computation.2 | async-start | bytes 8388608
  47.3 12.2 %slice-start.1 = ((s8[6291456]{0:T(1024)(128)(4,1)}), s8[2097152]{0:T(1024)(128)(4,1)S(1)}, s32[]{:S(2)}) async-start(s8[6291456]{0:T(1024)(128)(4,1)} %bitcast), calls=%async_computation.1 | async-start | bytes 4194304
  47.3 12.2 %slice-start.3 = ((s8[6291456]{0:T(1024)(128)(4,1)}), s8[2097152]{0:T(1024)(128)(4,1)S(1)}, s32[]{:S(2)}) async-start(s8[6291456]{0:T(1024)(128)(4,1)} %bitcast.2), calls=%async_computation.3 | async-start | bytes 4194304
  47.7 11.8 %collective-permute-start.8 = (f32[4,96,128]{2,1,0:T(8,128)S(1)}, f32[4,96,128]{2,1,0:T(8,128)S(1)}, u32[]{:S(2)}, u32[]{:S(2)}) collective-permute-start(f32[4,96,128]{2,1,0:T(8,128)S(1)} %get-tuple-element.82), channel_id=1, source_target_pairs={{0,1},{1,0},{2,3},{3,2},{4,5},{5,4},{6,7},{7,6},{8,9},{9,8},{10,11... | collective-permute-start | bytes 589832 | tf_op jit(solution)/shard_map/ppermute | solution.py:301
  52.5 6.9 %collective-permute-start.9 = (f32[4,96,128]{2,1,0:T(8,128)S(1)}, f32[4,96,128]{2,1,0:T(8,128)S(1)}, u32[]{:S(2)}, u32[]{:S(2)}) collective-permute-start(f32[4,96,128]{2,1,0:T(8,128)S(1)} %get-tuple-element.83), channel_id=1, source_target_pairs={{1,2},{2,1},{5,6},{6,5},{9,10},{10,9},{13,14},{14,13},{17,18},{18,... | collective-permute-start | bytes 589832 | tf_op jit(solution)/shard_map/ppermute | solution.py:301
  53.2 4.3 %collective-permute-start.10 = (f32[4,32,128]{2,1,0:T(8,128)S(1)}, f32[4,32,128]{2,1,0:T(8,128)S(1)}, u32[]{:S(2)}, u32[]{:S(2)}) collective-permute-start(f32[4,32,128]{2,1,0:T(8,128)S(1)} %get-tuple-element.84), channel_id=1, source_target_pairs={{0,4},{4,0},{8,12},{12,8},{1,5},{5,1},{9,13},{13,9},{2,6},{6,2},{1... | collective-permute-start | bytes 196616 | tf_op jit(solution)/shard_map/ppermute | solution.py:301
  53.3 6.2 %collective-permute-start.11 = (f32[4,32,128]{2,1,0:T(8,128)S(1)}, f32[4,32,128]{2,1,0:T(8,128)S(1)}, u32[]{:S(2)}, u32[]{:S(2)}) collective-permute-start(f32[4,32,128]{2,1,0:T(8,128)S(1)} %get-tuple-element.85), channel_id=1, source_target_pairs={{4,8},{8,4},{5,9},{9,5},{6,10},{10,6},{7,11},{11,7},{20,24},{24,20... | collective-permute-start | bytes 196616 | tf_op jit(solution)/shard_map/ppermute | solution.py:301
  64.3 31.4 %collective-permute-start.14 = (f32[96,32,128]{2,1,0:T(8,128)S(1)}, f32[96,32,128]{2,1,0:T(8,128)S(1)}, u32[]{:S(2)}, u32[]{:S(2)}) collective-permute-start(f32[96,32,128]{2,1,0:T(8,128)S(1)} %get-tuple-element.95.refs_3_), channel_id=1, source_target_pairs={{0,16},{16,0},{32,48},{48,32},{64,80},{80,64},{96,112},{112,96},{1... | collective-permute-start | bytes 4718600 | tf_op jit(solution)/shard_map/ppermute | solution.py:298
  64.4 13.3 %collective-permute-start.13 = (f32[48,32,128]{2,1,0:T(8,128)S(1)}, f32[48,32,128]{2,1,0:T(8,128)S(1)}, u32[]{:S(2)}, u32[]{:S(2)}) collective-permute-start(f32[48,32,128]{2,1,0:T(8,128)S(1)} %shard_map.62.refs_3_), channel_id=1, source_target_pairs={{16,32},{32,16},{48,64},{64,48},{80,96},{96,80},{17,33},{33,17},{4... | collective-permute-start | bytes 2359304 | tf_op jit(solution)/shard_map/ppermute | solution.py:295
  67.4 18.7 %collective-permute-start.12 = (f32[48,32,128]{2,1,0:T(8,128)S(1)}, f32[48,32,128]{2,1,0:T(8,128)S(1)}, u32[]{:S(2)}, u32[]{:S(2)}) collective-permute-start(f32[48,32,128]{2,1,0:T(8,128)S(1)} %get-tuple-element.87), channel_id=1, source_target_pairs={{16,32},{32,16},{48,64},{64,48},{80,96},{96,80},{17,33},{33,17},{4... | collective-permute-start | bytes 2359304 | tf_op jit(solution)/shard_map/ppermute | solution.py:295
  86.5 9.2 %collective-permute-start.15 = (f32[4,96,128]{2,1,0:T(8,128)S(1)}, f32[4,96,128]{2,1,0:T(8,128)S(1)}, u32[]{:S(2)}, u32[]{:S(2)}) collective-permute-start(f32[4,96,128]{2,1,0:T(8,128)S(1)} %get-tuple-element.96), channel_id=1, source_target_pairs={{0,1},{1,0},{2,3},{3,2},{4,5},{5,4},{6,7},{7,6},{8,9},{9,8},{10,11... | collective-permute-start | bytes 589832 | tf_op jit(solution)/shard_map/ppermute | solution.py:301
  88.8 6.9 %collective-permute-start.16 = (f32[4,96,128]{2,1,0:T(8,128)S(1)}, f32[4,96,128]{2,1,0:T(8,128)S(1)}, u32[]{:S(2)}, u32[]{:S(2)}) collective-permute-start(f32[4,96,128]{2,1,0:T(8,128)S(1)} %get-tuple-element.97), channel_id=1, source_target_pairs={{1,2},{2,1},{5,6},{6,5},{9,10},{10,9},{13,14},{14,13},{17,18},{18,... | collective-permute-start | bytes 589832 | tf_op jit(solution)/shard_map/ppermute | solution.py:301
  89.4 4.3 %collective-permute-start.17 = (f32[4,32,128]{2,1,0:T(8,128)S(1)}, f32[4,32,128]{2,1,0:T(8,128)S(1)}, u32[]{:S(2)}, u32[]{:S(2)}) collective-permute-start(f32[4,32,128]{2,1,0:T(8,128)S(1)} %get-tuple-element.98), channel_id=1, source_target_pairs={{0,4},{4,0},{8,12},{12,8},{1,5},{5,1},{9,13},{13,9},{2,6},{6,2},{1... | collective-permute-start | bytes 196616 | tf_op jit(solution)/shard_map/ppermute | solution.py:301
  89.5 6.2 %collective-permute-start.18 = (f32[4,32,128]{2,1,0:T(8,128)S(1)}, f32[4,32,128]{2,1,0:T(8,128)S(1)}, u32[]{:S(2)}, u32[]{:S(2)}) collective-permute-start(f32[4,32,128]{2,1,0:T(8,128)S(1)} %get-tuple-element.99), channel_id=1, source_target_pairs={{4,8},{8,4},{5,9},{9,5},{6,10},{10,6},{7,11},{11,7},{20,24},{24,20... | collective-permute-start | bytes 196616 | tf_op jit(solution)/shard_map/ppermute | solution.py:301
  100.5 35.7 %collective-permute-start.21 = (f32[96,32,128]{2,1,0:T(8,128)S(1)}, f32[96,32,128]{2,1,0:T(8,128)S(1)}, u32[]{:S(2)}, u32[]{:S(2)}) collective-permute-start(f32[96,32,128]{2,1,0:T(8,128)S(1)} %get-tuple-element.109.refs_3_), channel_id=1, source_target_pairs={{0,16},{16,0},{32,48},{48,32},{64,80},{80,64},{96,112},{112,96},{1... | collective-permute-start | bytes 4718600 | tf_op jit(solution)/shard_map/ppermute | solution.py:298
  100.6 13.3 %collective-permute-start.20 = (f32[48,32,128]{2,1,0:T(8,128)S(1)}, f32[48,32,128]{2,1,0:T(8,128)S(1)}, u32[]{:S(2)}, u32[]{:S(2)}) collective-permute-start(f32[48,32,128]{2,1,0:T(8,128)S(1)} %shard_map.65.refs_3_), channel_id=1, source_target_pairs={{16,32},{32,16},{48,64},{64,48},{80,96},{96,80},{17,33},{33,17},{4... | collective-permute-start | bytes 2359304 | tf_op jit(solution)/shard_map/ppermute | solution.py:295
  104.0 18.3 %collective-permute-start.19 = (f32[48,32,128]{2,1,0:T(8,128)S(1)}, f32[48,32,128]{2,1,0:T(8,128)S(1)}, u32[]{:S(2)}, u32[]{:S(2)}) collective-permute-start(f32[48,32,128]{2,1,0:T(8,128)S(1)} %get-tuple-element.101), channel_id=1, source_target_pairs={{16,32},{32,16},{48,64},{64,48},{80,96},{96,80},{17,33},{33,17},{4... | collective-permute-start | bytes 2359304 | tf_op jit(solution)/shard_map/ppermute | solution.py:295
  122.7 13.5 %collective-permute-start.22 = (f32[4,96,128]{2,1,0:T(8,128)S(1)}, f32[4,96,128]{2,1,0:T(8,128)S(1)}, u32[]{:S(2)}, u32[]{:S(2)}) collective-permute-start(f32[4,96,128]{2,1,0:T(8,128)S(1)} %get-tuple-element.110), channel_id=1, source_target_pairs={{0,1},{1,0},{2,3},{3,2},{4,5},{5,4},{6,7},{7,6},{8,9},{9,8},{10,11... | collective-permute-start | bytes 589832 | tf_op jit(solution)/shard_map/ppermute | solution.py:301
  125.4 10.8 %collective-permute-start.23 = (f32[4,96,128]{2,1,0:T(8,128)S(1)}, f32[4,96,128]{2,1,0:T(8,128)S(1)}, u32[]{:S(2)}, u32[]{:S(2)}) collective-permute-start(f32[4,96,128]{2,1,0:T(8,128)S(1)} %get-tuple-element.111), channel_id=1, source_target_pairs={{1,2},{2,1},{5,6},{6,5},{9,10},{10,9},{13,14},{14,13},{17,18},{18,... | collective-permute-start | bytes 589832 | tf_op jit(solution)/shard_map/ppermute | solution.py:301
  126.1 4.3 %collective-permute-start.24 = (f32[4,32,128]{2,1,0:T(8,128)S(1)}, f32[4,32,128]{2,1,0:T(8,128)S(1)}, u32[]{:S(2)}, u32[]{:S(2)}) collective-permute-start(f32[4,32,128]{2,1,0:T(8,128)S(1)} %get-tuple-element.112), channel_id=1, source_target_pairs={{0,4},{4,0},{8,12},{12,8},{1,5},{5,1},{9,13},{13,9},{2,6},{6,2},{1... | collective-permute-start | bytes 196616 | tf_op jit(solution)/shard_map/ppermute | solution.py:301
  126.2 6.4 %collective-permute-start.25 = (f32[4,32,128]{2,1,0:T(8,128)S(1)}, f32[4,32,128]{2,1,0:T(8,128)S(1)}, u32[]{:S(2)}, u32[]{:S(2)}) collective-permute-start(f32[4,32,128]{2,1,0:T(8,128)S(1)} %get-tuple-element.113), channel_id=1, source_target_pairs={{4,8},{8,4},{5,9},{9,5},{6,10},{10,6},{7,11},{11,7},{20,24},{24,20... | collective-permute-start | bytes 196616 | tf_op jit(solution)/shard_map/ppermute | solution.py:301
  130.4 15.7 %collective-permute-start.27 = (f32[48,32,128]{2,1,0:T(8,128)S(1)}, f32[48,32,128]{2,1,0:T(8,128)S(1)}, u32[]{:S(2)}, u32[]{:S(2)}) collective-permute-start(f32[48,32,128]{2,1,0:T(8,128)S(1)} %shard_map.68.refs_3_), channel_id=1, source_target_pairs={{16,32},{32,16},{48,64},{64,48},{80,96},{96,80},{17,33},{33,17},{4... | collective-permute-start | bytes 2359304 | tf_op jit(solution)/shard_map/ppermute | solution.py:295
  132.6 19.6 %collective-permute-start.26 = (f32[48,32,128]{2,1,0:T(8,128)S(1)}, f32[48,32,128]{2,1,0:T(8,128)S(1)}, u32[]{:S(2)}, u32[]{:S(2)}) collective-permute-start(f32[48,32,128]{2,1,0:T(8,128)S(1)} %get-tuple-element.115), channel_id=1, source_target_pairs={{16,32},{32,16},{48,64},{64,48},{80,96},{96,80},{17,33},{33,17},{4... | collective-permute-start | bytes 2359304 | tf_op jit(solution)/shard_map/ppermute | solution.py:295
  141.9 13.0 %collective-permute-start.33 = (f32[6,32,128]{2,1,0:T(8,128)S(1)}, f32[6,32,128]{2,1,0:T(8,128)S(1)}, u32[]{:S(2)}, u32[]{:S(2)}) collective-permute-start(f32[6,32,128]{2,1,0:T(8,128)S(1)} %get-tuple-element.121.refs_3_), channel_id=1, source_target_pairs={{0,12},{4,8},{8,4},{12,0},{1,13},{5,9},{9,5},{13,1},{2,14},{6,10},... | collective-permute-start | bytes 294920 | tf_op jit(solution)/shard_map/ppermute | solution.py:314
  144.0 13.0 %collective-permute-start.32 = (f32[6,32,128]{2,1,0:T(8,128)S(1)}, f32[6,32,128]{2,1,0:T(8,128)S(1)}, u32[]{:S(2)}, u32[]{:S(2)}) collective-permute-start(f32[6,32,128]{2,1,0:T(8,128)S(1)} %get-tuple-element.121.refs_3_), channel_id=1, source_target_pairs={{0,8},{4,12},{8,0},{12,4},{1,9},{5,13},{9,1},{13,5},{2,10},{6,14},... | collective-permute-start | bytes 294920 | tf_op jit(solution)/shard_map/ppermute | solution.py:314
  144.0 13.0 %collective-permute-start.31 = (f32[6,32,128]{2,1,0:T(8,128)S(1)}, f32[6,32,128]{2,1,0:T(8,128)S(1)}, u32[]{:S(2)}, u32[]{:S(2)}) collective-permute-start(f32[6,32,128]{2,1,0:T(8,128)S(1)} %get-tuple-element.121.refs_3_), channel_id=1, source_target_pairs={{0,4},{4,0},{8,12},{12,8},{1,5},{5,1},{9,13},{13,9},{2,6},{6,2},{1... | collective-permute-start | bytes 294920 | tf_op jit(solution)/shard_map/ppermute | solution.py:314
  152.7 8.0 %collective-permute-start.30 = (f32[2,32,128]{2,1,0:T(8,128)S(1)}, f32[2,32,128]{2,1,0:T(8,128)S(1)}, u32[]{:S(2)}, u32[]{:S(2)}) collective-permute-start(f32[2,32,128]{2,1,0:T(8,128)S(1)} %get-tuple-element.117.refs_1_), channel_id=1, source_target_pairs={{0,12},{4,8},{8,4},{12,0},{1,13},{5,9},{9,5},{13,1},{2,14},{6,10},... | collective-permute-start | bytes 98312 | tf_op jit(solution)/shard_map/ppermute | solution.py:314
  154.8 5.9 %collective-permute-start.29 = (f32[2,32,128]{2,1,0:T(8,128)S(1)}, f32[2,32,128]{2,1,0:T(8,128)S(1)}, u32[]{:S(2)}, u32[]{:S(2)}) collective-permute-start(f32[2,32,128]{2,1,0:T(8,128)S(1)} %get-tuple-element.117.refs_1_), channel_id=1, source_target_pairs={{0,8},{4,12},{8,0},{12,4},{1,9},{5,13},{9,1},{13,5},{2,10},{6,14},... | collective-permute-start | bytes 98312 | tf_op jit(solution)/shard_map/ppermute | solution.py:314
  154.9 5.8 %collective-permute-start.28 = (f32[2,32,128]{2,1,0:T(8,128)S(1)}, f32[2,32,128]{2,1,0:T(8,128)S(1)}, u32[]{:S(2)}, u32[]{:S(2)}) collective-permute-start(f32[2,32,128]{2,1,0:T(8,128)S(1)} %get-tuple-element.117.refs_1_), channel_id=1, source_target_pairs={{0,4},{4,0},{8,12},{12,8},{1,5},{5,1},{9,13},{13,9},{2,6},{6,2},{1... | collective-permute-start | bytes 98312 | tf_op jit(solution)/shard_map/ppermute | solution.py:314

commit v3 on v2

--- a/solution.py
+++ b/solution.py
@@ -12,6 +12,7 @@
 TILE = 8
 UNROLL = 19
 PIECES = 2
+FIRST = 64
 RATE = 0.05
 GRID = P("lat", "lon", "lev", None)
 
@@ -35,11 +36,13 @@
     place = here()
     pieces, sems = refs[:PIECES], refs[PIECES]
     rows, _ = roles(place[0])
-    size = pieces[0].shape[0]
-    copies = [
-        pltpu.make_async_copy(source.at[rows[0], pl.ds(size * p, size)], pieces[p], sems.at[p])
-        for p in range(PIECES)
-    ]
+    copies, at = [], 0
+    for p, piece in enumerate(pieces):
+        size = piece.shape[0]
+        copies.append(
+            pltpu.make_async_copy(source.at[rows[0], pl.ds(at, size)], piece, sems.at[p])
+        )
+        at += size
     for copy in copies:
         copy.start()
     for copy in copies:
@@ -74,18 +77,25 @@
     ends[3][k] = either(even_lon, low, high)
 
 
-def spread_step(last, *refs):
+def spread_step(first, last, *refs):
     place = here()
     for odd in (0, 1):
-        pl.when(place[0] == odd)(functools.partial(spread_rows, last, odd, place, *refs))
-
-
-def spread_rows(last, odd, place, *refs):
+        pl.when(place[0] == odd)(functools.partial(spread_rows, first, last, odd, place, *refs))
+
+
+def spread_rows(first, last, odd, place, *refs):
     state, refs = refs[:4], refs[4:]
     core_row, near_lev, far_lev, near_lon, far_lon, north, east, upward = refs[:8]
     new = refs[8:12]
     extra = refs[12:]
     rows, _ = roles(odd)
+    if first:
+        stored, (upward, sems) = upward, extra[-2:]
+        loads = [
+            pltpu.make_async_copy(stored.at[row], upward.at[row], sems.at[row]) for row in rows
+        ]
+        for load in loads:
+            load.start()
     length, levels, members = new[0].shape
     even_lev, even_lon = place[1] == 0, place[2] == 0
     parts = levels // TILE
@@ -93,6 +103,8 @@
     at_low, at_high = spot == 0, spot == TILE - 1
     for k in range(4):
         row = rows[k]
+        if first:
+            loads[k].wait()
         inward = core_row if k == 3 else state[k + 1]
         outward = None if k == 0 else state[k - 1]
 
@@ -166,12 +178,12 @@
     out[at + 1] = lax.fori_loop(0, length, body, jnp.zeros_like(mean), unroll=4)
 
 
-def add_halo(piece, place, part, north, halo, out, inner=None):
+def add_halo(offset, place, part, north, halo, out, inner=None):
     rows, sign = roles(place[0])
     size, levels, members = halo.shape
 
     def body(x, total):
-        at = size * piece + x
+        at = offset + x
         value = part[at] + (RATE + sign * north[rows[0], at]) * halo[x]
         out[x] = value
         if inner is not None:
@@ -190,7 +202,7 @@
     place = here()
     part, north, halo, done = refs[:4]
     rest = refs[4:]
-    size, levels, members = halo.shape
+    size, (levels, members) = done.shape[0], halo.shape[1:]
     if last:
         row, stats = rest
     else:
@@ -219,11 +231,11 @@
     zero = jnp.zeros((levels, members), jnp.float32)
     total = lax.fori_loop(0, size, keep, zero, unroll=4)
     if last:
-        total += add_halo(1, place, part, north, halo, row.at[pl.ds(size, size)])
+        total += add_halo(size, place, part, north, halo, row.at[pl.ds(size, halo.shape[0])])
         line_statistics(row, total, stats, 0)
     else:
-        add_halo(1, place, part, north, halo, piece, both)
-        low, high = row[0], row[2 * size - 1]
+        add_halo(size, place, part, north, halo, piece, both)
+        low, high = row[0], row[row.shape[0] - 1]
         ends[2][0] = either(even_lon, high, low)
         ends[3][0] = either(even_lon, low, high)
 
@@ -261,10 +273,15 @@
         copy.wait()
 
 
+def placed(array, space):
+    return pltpu.with_memory_space_constraint(array, space)
+
+
 def shards(initial_state, north, east, upward):
     rows_here, length, levels, members = initial_state.shape
     row_type = jax.ShapeDtypeStruct((length, levels, members), jnp.float32)
-    piece_type = jax.ShapeDtypeStruct((length // PIECES, levels, members), jnp.float32)
+    sizes = (length * FIRST // 96, length - length * FIRST // 96)
+    piece_types = [jax.ShapeDtypeStruct((n, levels, members), jnp.float32) for n in sizes]
     lev_type = jax.ShapeDtypeStruct((rows_here, length, members), jnp.float32)
     lon_type = jax.ShapeDtypeStruct((rows_here, levels, members), jnp.float32)
     whole = jax.ShapeDtypeStruct(initial_state.shape, jnp.float32)
@@ -316,15 +333,15 @@
 
     stats_type = jax.ShapeDtypeStruct((2 * rows_here - 2, levels, members), jnp.float32)
     end_types = [lev_type, lev_type, lon_type, lon_type]
-    source = pltpu.with_memory_space_constraint(initial_state, pltpu.HBM)
-    winds = [pltpu.with_memory_space_constraint(w, pltpu.VMEM) for w in (north, east, upward)]
+    source = placed(initial_state, pltpu.HBM)
+    winds = [placed(north, pltpu.VMEM), placed(east, pltpu.VMEM), placed(upward, pltpu.HBM)]
     for step in range(STEPS):
         last = step == STEPS - 1
         if step == 0:
             pieces = call(
                 take_outer,
                 [source],
-                [piece_type] * PIECES,
+                piece_types,
                 10**6,
                 in_specs=[anywhere],
                 scratch=[pltpu.SemaphoreType.DMA((PIECES,))],
@@ -342,23 +359,29 @@
             ends = ends_of(near, far, close, distant)
         else:
             (begun,) = call(
-                start_row, [part, winds[0], halos[0]], [piece_type], 10**9
+                start_row, [part, winds[0], halos[0]], piece_types[:1], 10**9
             )
             first_halo = across(begun)
             ended, outer, *sent = call(
                 functools.partial(finish_row, False),
                 [part, winds[0], halos[1], begun, *extra],
-                [piece_type, row_type, *end_types],
+                [piece_types[1], row_type, *end_types],
                 10**9,
             )
             halos = [first_halo, across(ended)]
             ends = ends_of(*sent)
         part, *made = call(
-            functools.partial(spread_step, last),
+            functools.partial(spread_step, step == 0, last),
             [outer, *inner_rows, core_row, *ends, *winds],
-            [row_type] * 4 + ([stats_type] if last else end_types),
+            [row_type] * 4
+            + ([stats_type] if last else end_types)
+            + ([whole] if step == 0 else []),
             SPREAD_FLOPS,
+            in_specs=[vmem] * 11 + [anywhere if step == 0 else vmem],
+            scratch=[pltpu.SemaphoreType.DMA((4,))] if step == 0 else [],
         )
+        if step == 0:
+            winds[2] = placed(made.pop(), pltpu.VMEM)
         inner_rows, extra = made[:3], made[3:]
         if not last:
             core_row = beside(inner_rows[2])
@@ -380,7 +403,7 @@
             room=8 * 2**20,
         )
 
-    (begun,) = call(start_row, [part, winds[0], halos[0]], [piece_type], 10**9)
+    (begun,) = call(start_row, [part, winds[0], halos[0]], piece_types[:1], 10**9)
     early = from_others(extra[0])
     outer, stats = call(
         functools.partial(finish_row, True),

time: 164 us -> 162 us (0.988)
  local copies, waits for them, and re-layouts: 5.58 us -> 2.79 us
    unnamed x14 -> x8, local copies, waits for them, and re-layouts: 5.58 us -> 2.79 us
  transfers between devices with their start and end apart: 34 -> 34, of which waited for: 13 -> 14; matrix products, arithmetic and copies ran while one was open for 0% -> 0% of each run, Pallas kernels for 8% -> 8%
where the time goes in v3:
time: 162 us; the launch traced here: 161 us
  starting transfers between devices  62.5 us (39%)
  waiting for transfers between devices  60.6 us (37%)
  Pallas kernels  33.8 us (21%)
  local copies, waits for them, and re-layouts  2.79 us (2%)
    ppermute x8, waiting for transfers between devices, across(): return lax.ppermute(array, 'lat', pairs(lats, 1))  53.5 us
    pallas_call x16, Pallas kernels, call(): pl.pallas_call(kernel, out_shape=outs, in_specs=in_specs or [vmem] * len(...  33.8 us
    ppermute x16, starting transfers between devices, swap(): return lax.ppermute(array, axis, pairs(lax.axis_size(axis), start))  31.2 us
    ppermute x8, starting transfers between devices, across(): return lax.ppermute(array, 'lat', pairs(lats, 1))  22.4 us
    ppermute x6, starting transfers between devices, from_others(): made.append(lax.ppermute(array, 'lon', [(i, i ^ d) for i in range(lons)]))  8.51 us
    ppermute x16, waiting for transfers between devices, swap(): return lax.ppermute(array, axis, pairs(lax.axis_size(axis), start))  7.03 us
  transfers between devices with their start and end apart: 34, of which 14 were waited for; matrix products, arithmetic and copies ran while one was open for 0% of the time, Pallas kernels for 8%

profile of v3, /device:TPU:14, one launch (start us, length us, event | category | flops | bytes accessed | tf_op | source)
XLA Modules:
  0.0 160.9 jit_solution(1255557062068426009)
XLA Ops:
  0.6 3.2 %shard_map.59 = (f32[96,32,128]{2,1,0:T(8,128)S(1)}, f32[96,32,128]{2,1,0:T(8,128)S(1)}, f32[96,32,128]{2,1,0:T(8,128)S(1)}, f32[96,32,128]{2,1,0:T(8,128)S(1)},...) custom-call(f32[4,96,32,128]{3,2,1,0:T(8,128)} %source.3), custom_call_target="tpu_custom_call" | custom-call | flops 1000000000 | tf_op jit(solution)/shard_map/pallas_call | solution.py:292
  3.8 0.1 collective-permute-start
  3.9 2.0 %collective-permute-start.1 = (f32[4,96,128]{2,1,0:T(8,128)S(1)}, f32[4,96,128]{2,1,0:T(8,128)S(1)}, u32[]{:S(2)}, u32[]{:S(2)}) collective-permute-start(f32[4,96,128]{2,1,0:T(8,128)S(1)} %get-tuple-element.68), channel_id=1, source_target_pairs={{0,1},{1,0},{2,3},{3,2},{4,5},{5,4},{6,7},{7,6},{8,9},{9,8},{10,11... | collective-permute-start | bytes 589832 | tf_op jit(solution)/shard_map/ppermute | solution.py:318
  5.9 0.7 collective-permute-start.2
  6.6 0.5 collective-permute-start.3
  7.1 4.3 %collective-permute-start.4 = (f32[4,32,128]{2,1,0:T(8,128)S(1)}, f32[4,32,128]{2,1,0:T(8,128)S(1)}, u32[]{:S(2)}, u32[]{:S(2)}) collective-permute-start(f32[4,32,128]{2,1,0:T(8,128)S(1)} %get-tuple-element.71), channel_id=1, source_target_pairs={{4,8},{8,4},{5,9},{9,5},{6,10},{10,6},{7,11},{11,7},{20,24},{24,20... | collective-permute-start | bytes 196616 | tf_op jit(solution)/shard_map/ppermute | solution.py:318
  11.4 2.2 %collective-permute-done.4.refs_8_ = f32[4,32,128]{2,1,0:T(8,128)S(1)} collective-permute-done((f32[4,32,128]{2,1,0:T(8,128)S(1)}, f32[4,32,128]{2,1,0:T(8,128)S(1)}, u32[]{:S(2)}, u32[]{:S(2)}) %collective-permute-start.4) | collective-permute-done | bytes 65568 | tf_op jit(solution)/shard_map/ppermute | solution.py:318
  13.7 2.8 %copy-done.1 = f32[4,96,32,128]{3,2,1,0:T(8,128)S(1)} copy-done((f32[4,96,32,128]{3,2,1,0:T(8,128)S(1)}, f32[4,96,32,128]{3,2,1,0:T(8,128)}, u32[]{:S(2)}) %copy-start.1) | copy-done | bytes 6291480
  16.5 6.2 %shard_map.60 = (f32[96,32,128]{2,1,0:T(8,128)S(1)}, f32[96,32,128]{2,1,0:T(8,128)S(1)}, f32[96,32,128]{2,1,0:T(8,128)S(1)}, f32[96,32,128]{2,1,0:T(8,128)S(1)},...) custom-call(f32[96,32,128]{2,1,0:T(8,128)S(1)} %get-tuple-element.64, ...), custom_call_target="tpu_custom_call" | custom-call | flops 20000000000 | tf_op jit(solution)/shard_map/pallas_call | solution.py:292
  22.7 0.1 collective-permute-start.7
  22.8 1.4 shard_map.61
  24.2 2.8 %collective-permute-start.6 = (f32[64,32,128]{2,1,0:T(8,128)S(1)}, f32[64,32,128]{2,1,0:T(8,128)S(1)}, u32[]{:S(2)}, u32[]{:S(2)}) collective-permute-start(f32[64,32,128]{2,1,0:T(8,128)S(1)} %get-tuple-element.74), channel_id=1, source_target_pairs={{16,32},{32,16},{48,64},{64,48},{80,96},{96,80},{17,33},{33,17},{4... | collective-permute-start | bytes 3145736 | tf_op jit(solution)/shard_map/ppermute | solution.py:312
  27.0 2.7 %collective-permute-start.5 = (f32[32,32,128]{2,1,0:T(8,128)S(1)}, f32[32,32,128]{2,1,0:T(8,128)S(1)}, u32[]{:S(2)}, u32[]{:S(2)}) collective-permute-start(f32[32,32,128]{2,1,0:T(8,128)S(1)} %get-tuple-element.73), channel_id=1, source_target_pairs={{16,32},{32,16},{48,64},{64,48},{80,96},{96,80},{17,33},{33,17},{4... | collective-permute-start | bytes 1572872 | tf_op jit(solution)/shard_map/ppermute | solution.py:312
  29.8 10.5 %collective-permute-done.6.halo = f32[64,32,128]{2,1,0:T(8,128)S(1)} collective-permute-done((f32[64,32,128]{2,1,0:T(8,128)S(1)}, f32[64,32,128]{2,1,0:T(8,128)S(1)}, u32[]{:S(2)}, u32[]{:S(2)}) %collective-permute-start.6) | collective-permute-done | bytes 1048608 | tf_op jit(solution)/shard_map/ppermute | solution.py:312
  40.3 0.2 shard_map.62.refs_3_
  40.6 5.4 %collective-permute-done.5.refs_2_ = f32[32,32,128]{2,1,0:T(8,128)S(1)} collective-permute-done((f32[32,32,128]{2,1,0:T(8,128)S(1)}, f32[32,32,128]{2,1,0:T(8,128)S(1)}, u32[]{:S(2)}, u32[]{:S(2)}) %collective-permute-start.5) | collective-permute-done | bytes 524320 | tf_op jit(solution)/shard_map/ppermute | solution.py:312
  45.9 0.3 shard_map.63
  46.3 4.9 %collective-permute-start.8 = (f32[4,96,128]{2,1,0:T(8,128)S(1)}, f32[4,96,128]{2,1,0:T(8,128)S(1)}, u32[]{:S(2)}, u32[]{:S(2)}) collective-permute-start(f32[4,96,128]{2,1,0:T(8,128)S(1)} %get-tuple-element.83), channel_id=1, source_target_pairs={{0,1},{1,0},{2,3},{3,2},{4,5},{5,4},{6,7},{7,6},{8,9},{9,8},{10,11... | collective-permute-start | bytes 589832 | tf_op jit(solution)/shard_map/ppermute | solution.py:318
  51.1 0.7 collective-permute-start.9
  51.8 0.1 collective-permute-start.10
  51.9 3.9 %collective-permute-start.11 = (f32[4,32,128]{2,1,0:T(8,128)S(1)}, f32[4,32,128]{2,1,0:T(8,128)S(1)}, u32[]{:S(2)}, u32[]{:S(2)}) collective-permute-start(f32[4,32,128]{2,1,0:T(8,128)S(1)} %get-tuple-element.86), channel_id=1, source_target_pairs={{4,8},{8,4},{5,9},{9,5},{6,10},{10,6},{7,11},{11,7},{20,24},{24,20... | collective-permute-start | bytes 196616 | tf_op jit(solution)/shard_map/ppermute | solution.py:318
  55.8 0.3 collective-permute-done.10.refs_7_
  56.1 1.9 %collective-permute-done.11.refs_8_ = f32[4,32,128]{2,1,0:T(8,128)S(1)} collective-permute-done((f32[4,32,128]{2,1,0:T(8,128)S(1)}, f32[4,32,128]{2,1,0:T(8,128)S(1)}, u32[]{:S(2)}, u32[]{:S(2)}) %collective-permute-start.11) | collective-permute-done | bytes 65568 | tf_op jit(solution)/shard_map/ppermute | solution.py:318
  58.1 4.8 %shard_map.64 = (f32[96,32,128]{2,1,0:T(8,128)S(1)}, f32[96,32,128]{2,1,0:T(8,128)S(1)}, f32[96,32,128]{2,1,0:T(8,128)S(1)}, f32[96,32,128]{2,1,0:T(8,128)S(1)},...) custom-call(f32[96,32,128]{2,1,0:T(8,128)S(1)} %get-tuple-element.79, ...), custom_call_target="tpu_custom_call" | custom-call | flops 20000000000 | tf_op jit(solution)/shard_map/pallas_call | solution.py:292
  62.9 0.1 collective-permute-start.14
  63.0 3.0 %collective-permute-start.13 = (f32[64,32,128]{2,1,0:T(8,128)S(1)}, f32[64,32,128]{2,1,0:T(8,128)S(1)}, u32[]{:S(2)}, u32[]{:S(2)}) collective-permute-start(f32[64,32,128]{2,1,0:T(8,128)S(1)} %shard_map.62.refs_3_), channel_id=1, source_target_pairs={{16,32},{32,16},{48,64},{64,48},{80,96},{96,80},{17,33},{33,17},{4... | collective-permute-start | bytes 3145736 | tf_op jit(solution)/shard_map/ppermute | solution.py:312
  66.0 2.5 %collective-permute-start.12 = (f32[32,32,128]{2,1,0:T(8,128)S(1)}, f32[32,32,128]{2,1,0:T(8,128)S(1)}, u32[]{:S(2)}, u32[]{:S(2)}) collective-permute-start(f32[32,32,128]{2,1,0:T(8,128)S(1)} %get-tuple-element.89), channel_id=1, source_target_pairs={{16,32},{32,16},{48,64},{64,48},{80,96},{96,80},{17,33},{33,17},{4... | collective-permute-start | bytes 1572872 | tf_op jit(solution)/shard_map/ppermute | solution.py:312
  68.6 10.5 %collective-permute-done.13.halo = f32[64,32,128]{2,1,0:T(8,128)S(1)} collective-permute-done((f32[64,32,128]{2,1,0:T(8,128)S(1)}, f32[64,32,128]{2,1,0:T(8,128)S(1)}, u32[]{:S(2)}, u32[]{:S(2)}) %collective-permute-start.13) | collective-permute-done | bytes 1048608 | tf_op jit(solution)/shard_map/ppermute | solution.py:312
  79.1 0.2 shard_map.65.refs_3_
  79.3 5.4 %collective-permute-done.12.refs_2_ = f32[32,32,128]{2,1,0:T(8,128)S(1)} collective-permute-done((f32[32,32,128]{2,1,0:T(8,128)S(1)}, f32[32,32,128]{2,1,0:T(8,128)S(1)}, u32[]{:S(2)}, u32[]{:S(2)}) %collective-permute-start.12) | collective-permute-done | bytes 524320 | tf_op jit(solution)/shard_map/ppermute | solution.py:312
  84.7 0.3 shard_map.66
  85.1 2.1 %collective-permute-start.15 = (f32[4,96,128]{2,1,0:T(8,128)S(1)}, f32[4,96,128]{2,1,0:T(8,128)S(1)}, u32[]{:S(2)}, u32[]{:S(2)}) collective-permute-start(f32[4,96,128]{2,1,0:T(8,128)S(1)} %get-tuple-element.98), channel_id=1, source_target_pairs={{0,1},{1,0},{2,3},{3,2},{4,5},{5,4},{6,7},{7,6},{8,9},{9,8},{10,11... | collective-permute-start | bytes 589832 | tf_op jit(solution)/shard_map/ppermute | solution.py:318
  87.2 0.7 collective-permute-start.16
  87.9 0.1 collective-permute-start.17
  87.9 3.9 %collective-permute-start.18 = (f32[4,32,128]{2,1,0:T(8,128)S(1)}, f32[4,32,128]{2,1,0:T(8,128)S(1)}, u32[]{:S(2)}, u32[]{:S(2)}) collective-permute-start(f32[4,32,128]{2,1,0:T(8,128)S(1)} %get-tuple-element.101), channel_id=1, source_target_pairs={{4,8},{8,4},{5,9},{9,5},{6,10},{10,6},{7,11},{11,7},{20,24},{24,20... | collective-permute-start | bytes 196616 | tf_op jit(solution)/shard_map/ppermute | solution.py:318
  91.9 0.3 collective-permute-done.17.refs_7_
  92.2 1.9 %collective-permute-done.18.refs_8_ = f32[4,32,128]{2,1,0:T(8,128)S(1)} collective-permute-done((f32[4,32,128]{2,1,0:T(8,128)S(1)}, f32[4,32,128]{2,1,0:T(8,128)S(1)}, u32[]{:S(2)}, u32[]{:S(2)}) %collective-permute-start.18) | collective-permute-done | bytes 65568 | tf_op jit(solution)/shard_map/ppermute | solution.py:318
  94.1 4.8 %shard_map.67 = (f32[96,32,128]{2,1,0:T(8,128)S(1)}, f32[96,32,128]{2,1,0:T(8,128)S(1)}, f32[96,32,128]{2,1,0:T(8,128)S(1)}, f32[96,32,128]{2,1,0:T(8,128)S(1)},...) custom-call(f32[96,32,128]{2,1,0:T(8,128)S(1)} %get-tuple-element.94, ...), custom_call_target="tpu_custom_call" | custom-call | flops 20000000000 | tf_op jit(solution)/shard_map/pallas_call | solution.py:292
  98.9 0.1 collective-permute-start.21
  99.0 3.4 %collective-permute-start.20 = (f32[64,32,128]{2,1,0:T(8,128)S(1)}, f32[64,32,128]{2,1,0:T(8,128)S(1)}, u32[]{:S(2)}, u32[]{:S(2)}) collective-permute-start(f32[64,32,128]{2,1,0:T(8,128)S(1)} %shard_map.65.refs_3_), channel_id=1, source_target_pairs={{16,32},{32,16},{48,64},{64,48},{80,96},{96,80},{17,33},{33,17},{4... | collective-permute-start | bytes 3145736 | tf_op jit(solution)/shard_map/ppermute | solution.py:312
  102.4 2.2 %collective-permute-start.19 = (f32[32,32,128]{2,1,0:T(8,128)S(1)}, f32[32,32,128]{2,1,0:T(8,128)S(1)}, u32[]{:S(2)}, u32[]{:S(2)}) collective-permute-start(f32[32,32,128]{2,1,0:T(8,128)S(1)} %get-tuple-element.103), channel_id=1, source_target_pairs={{16,32},{32,16},{48,64},{64,48},{80,96},{96,80},{17,33},{33,17},{4... | collective-permute-start | bytes 1572872 | tf_op jit(solution)/shard_map/ppermute | solution.py:312
  104.6 10.5 %collective-permute-done.20.halo = f32[64,32,128]{2,1,0:T(8,128)S(1)} collective-permute-done((f32[64,32,128]{2,1,0:T(8,128)S(1)}, f32[64,32,128]{2,1,0:T(8,128)S(1)}, u32[]{:S(2)}, u32[]{:S(2)}) %collective-permute-start.20) | collective-permute-done | bytes 1048608 | tf_op jit(solution)/shard_map/ppermute | solution.py:312
  115.1 0.2 shard_map.68.refs_3_
  115.4 5.4 %collective-permute-done.19.refs_2_ = f32[32,32,128]{2,1,0:T(8,128)S(1)} collective-permute-done((f32[32,32,128]{2,1,0:T(8,128)S(1)}, f32[32,32,128]{2,1,0:T(8,128)S(1)}, u32[]{:S(2)}, u32[]{:S(2)}) %collective-permute-start.19) | collective-permute-done | bytes 524320 | tf_op jit(solution)/shard_map/ppermute | solution.py:312
  120.7 0.3 shard_map.69
  121.1 2.7 %collective-permute-start.22 = (f32[4,96,128]{2,1,0:T(8,128)S(1)}, f32[4,96,128]{2,1,0:T(8,128)S(1)}, u32[]{:S(2)}, u32[]{:S(2)}) collective-permute-start(f32[4,96,128]{2,1,0:T(8,128)S(1)} %get-tuple-element.112), channel_id=1, source_target_pairs={{0,1},{1,0},{2,3},{3,2},{4,5},{5,4},{6,7},{7,6},{8,9},{9,8},{10,11... | collective-permute-start | bytes 589832 | tf_op jit(solution)/shard_map/ppermute | solution.py:318
  123.8 0.7 collective-permute-start.23
  124.5 0.1 collective-permute-start.24
  124.6 3.9 %collective-permute-start.25 = (f32[4,32,128]{2,1,0:T(8,128)S(1)}, f32[4,32,128]{2,1,0:T(8,128)S(1)}, u32[]{:S(2)}, u32[]{:S(2)}) collective-permute-start(f32[4,32,128]{2,1,0:T(8,128)S(1)} %get-tuple-element.115), channel_id=1, source_target_pairs={{4,8},{8,4},{5,9},{9,5},{6,10},{10,6},{7,11},{11,7},{20,24},{24,20... | collective-permute-start | bytes 196616 | tf_op jit(solution)/shard_map/ppermute | solution.py:318
  128.5 0.3 collective-permute-done.24.refs_7_
  128.8 2.1 %collective-permute-start.27 = (f32[64,32,128]{2,1,0:T(8,128)S(1)}, f32[64,32,128]{2,1,0:T(8,128)S(1)}, u32[]{:S(2)}, u32[]{:S(2)}) collective-permute-start(f32[64,32,128]{2,1,0:T(8,128)S(1)} %shard_map.68.refs_3_), channel_id=1, source_target_pairs={{16,32},{32,16},{48,64},{64,48},{80,96},{96,80},{17,33},{33,17},{4... | collective-permute-start | bytes 3145736 | tf_op jit(solution)/shard_map/ppermute | solution.py:312
  131.0 3.6 %collective-permute-start.26 = (f32[32,32,128]{2,1,0:T(8,128)S(1)}, f32[32,32,128]{2,1,0:T(8,128)S(1)}, u32[]{:S(2)}, u32[]{:S(2)}) collective-permute-start(f32[32,32,128]{2,1,0:T(8,128)S(1)} %get-tuple-element.117), channel_id=1, source_target_pairs={{16,32},{32,16},{48,64},{64,48},{80,96},{96,80},{17,33},{33,17},{4... | collective-permute-start | bytes 1572872 | tf_op jit(solution)/shard_map/ppermute | solution.py:312
  134.6 5.6 %shard_map.70 = (f32[96,32,128]{2,1,0:T(8,128)S(1)}, f32[96,32,128]{2,1,0:T(8,128)S(1)}, f32[96,32,128]{2,1,0:T(8,128)S(1)}, f32[96,32,128]{2,1,0:T(8,128)S(1)}, f32[6,32,128]{2,1,0:T(8,128)S(1)}) custom-call(f32[96,32,128]{2,1,0:T(8,128)S(1)} %get-tuple-element.108.refs_0_, f32[96,32,128]{2,1,0:T(8,128)S(1)} %get-tuple-element.109.refs_1_, ...), custom_call_target="tpu_custom_call" | custom-call | flops 20000000000 | tf_op jit(solution)/shard_map/pallas_call | solution.py:292
  140.2 2.1 %collective-permute-start.33 = (f32[6,32,128]{2,1,0:T(8,128)S(1)}, f32[6,32,128]{2,1,0:T(8,128)S(1)}, u32[]{:S(2)}, u32[]{:S(2)}) collective-permute-start(f32[6,32,128]{2,1,0:T(8,128)S(1)} %get-tuple-element.123.refs_3_), channel_id=1, source_target_pairs={{0,12},{4,8},{8,4},{12,0},{1,13},{5,9},{9,5},{13,1},{2,14},{6,10},... | collective-permute-start | bytes 294920 | tf_op jit(solution)/shard_map/ppermute | solution.py:331
  142.3 0.1 collective-permute-start.32
  142.4 2.1 %collective-permute-start.31 = (f32[6,32,128]{2,1,0:T(8,128)S(1)}, f32[6,32,128]{2,1,0:T(8,128)S(1)}, u32[]{:S(2)}, u32[]{:S(2)}) collective-permute-start(f32[6,32,128]{2,1,0:T(8,128)S(1)} %get-tuple-element.123.refs_3_), channel_id=1, source_target_pairs={{0,4},{4,0},{8,12},{12,8},{1,5},{5,1},{9,13},{13,9},{2,6},{6,2},{1... | collective-permute-start | bytes 294920 | tf_op jit(solution)/shard_map/ppermute | solution.py:331
  144.5 0.4 collective-permute-done.27.halo
  144.9 0.2 shard_map.71.refs_3_
  145.2 5.4 %collective-permute-done.26.refs_2_ = f32[32,32,128]{2,1,0:T(8,128)S(1)} collective-permute-done((f32[32,32,128]{2,1,0:T(8,128)S(1)}, f32[32,32,128]{2,1,0:T(8,128)S(1)}, u32[]{:S(2)}, u32[]{:S(2)}) %collective-permute-start.26) | collective-permute-done | bytes 524320 | tf_op jit(solution)/shard_map/ppermute | solution.py:312
  150.5 0.5 shard_map.72
  151.0 2.1 %collective-permute-start.30 = (f32[2,32,128]{2,1,0:T(8,128)S(1)}, f32[2,32,128]{2,1,0:T(8,128)S(1)}, u32[]{:S(2)}, u32[]{:S(2)}) collective-permute-start(f32[2,32,128]{2,1,0:T(8,128)S(1)} %get-tuple-element.119.refs_1_), channel_id=1, source_target_pairs={{0,12},{4,8},{8,4},{12,0},{1,13},{5,9},{9,5},{13,1},{2,14},{6,10},... | collective-permute-start | bytes 98312 | tf_op jit(solution)/shard_map/ppermute | solution.py:331
  153.2 2.1 %collective-permute-start.28 = (f32[2,32,128]{2,1,0:T(8,128)S(1)}, f32[2,32,128]{2,1,0:T(8,128)S(1)}, u32[]{:S(2)}, u32[]{:S(2)}) collective-permute-start(f32[2,32,128]{2,1,0:T(8,128)S(1)} %get-tuple-element.119.refs_1_), channel_id=1, source_target_pairs={{0,4},{4,0},{8,12},{12,8},{1,5},{5,1},{9,13},{13,9},{2,6},{6,2},{1... | collective-permute-start | bytes 98312 | tf_op jit(solution)/shard_map/ppermute | solution.py:331
  155.3 3.7 %shard_map.73 = (f32[4,96,32,128]{3,2,1,0:T(8,128)}, f32[4,96,32,128]{3,2,1,0:T(8,128)}) custom-call(f32[96,32,128]{2,1,0:T(8,128)S(1)} %get-tuple-element.120.refs_0_, f32[96,32,128]{2,1,0:T(8,128)S(1)} %get-tuple-element.121.refs_1_, f32[96,32,128]{2,1,0:T(8,128)S(1)} %get-tuple-element.122.refs_2_, f32[6,32,128]{2,1,0:T(8,128)S(1)} %get-tuple-element.123.refs_3_, ...), custom_call_target="tpu_custom_call" | custom-call | flops 1000000000 | tf_op jit(solution)/shard_map/pallas_call | solution.py:292
  159.1 1.7 %shard_map.74 = (f32[4,96,32,128]{3,2,1,0:T(8,128)}, f32[4,96,32,128]{3,2,1,0:T(8,128)}) custom-call(f32[96,32,128]{2,1,0:T(8,128)S(1)} %get-tuple-element.118.refs_0_, f32[2,32,128]{2,1,0:T(8,128)S(1)} %get-tuple-element.119.refs_1_, f32[2,32,128]{2,1,0:T(8,128)S(1)} %collective-permute-done.28.refs_2_, ...), custom_call_target="tpu_custom_call", output_to_operand_aliasing={{0}: (5, {}), {1}: (6, {})} | custom-call | flops 1000000000 | tf_op jit(solution)/shard_map/pallas_call | solution.py:292
  (29 shorter events, 0.1 us)
Async XLA Ops:
  0.6 13.0 %copy-start = (f32[4,96,32,128]{3,2,1,0:T(8,128)S(1)}, f32[4,96,32,128]{3,2,1,0:T(8,128)}, u32[]{:S(2)}) copy-start(f32[4,96,32,128]{3,2,1,0:T(8,128)} %refs_1_.7) | copy-start | bytes 18874372
  3.8 9.8 %collective-permute-start = (f32[96,32,128]{2,1,0:T(8,128)S(1)}, f32[96,32,128]{2,1,0:T(8,128)S(1)}, u32[]{:S(2)}, u32[]{:S(2)}) collective-permute-start(f32[96,32,128]{2,1,0:T(8,128)S(1)} %get-tuple-element.67.refs_3_), channel_id=1, source_target_pairs={{0,16},{16,0},{32,48},{48,32},{64,80},{80,64},{96,112},{112,96},{1... | collective-permute-start | bytes 4718600 | tf_op jit(solution)/shard_map/ppermute | solution.py:315
  3.9 9.7 %collective-permute-start.1 = (f32[4,96,128]{2,1,0:T(8,128)S(1)}, f32[4,96,128]{2,1,0:T(8,128)S(1)}, u32[]{:S(2)}, u32[]{:S(2)}) collective-permute-start(f32[4,96,128]{2,1,0:T(8,128)S(1)} %get-tuple-element.68), channel_id=1, source_target_pairs={{0,1},{1,0},{2,3},{3,2},{4,5},{5,4},{6,7},{7,6},{8,9},{9,8},{10,11... | collective-permute-start | bytes 589832 | tf_op jit(solution)/shard_map/ppermute | solution.py:318
  5.9 7.7 %collective-permute-start.2 = (f32[4,96,128]{2,1,0:T(8,128)S(1)}, f32[4,96,128]{2,1,0:T(8,128)S(1)}, u32[]{:S(2)}, u32[]{:S(2)}) collective-permute-start(f32[4,96,128]{2,1,0:T(8,128)S(1)} %get-tuple-element.69), channel_id=1, source_target_pairs={{1,2},{2,1},{5,6},{6,5},{9,10},{10,9},{13,14},{14,13},{17,18},{18,... | collective-permute-start | bytes 589832 | tf_op jit(solution)/shard_map/ppermute | solution.py:318
  6.6 4.8 %collective-permute-start.3 = (f32[4,32,128]{2,1,0:T(8,128)S(1)}, f32[4,32,128]{2,1,0:T(8,128)S(1)}, u32[]{:S(2)}, u32[]{:S(2)}) collective-permute-start(f32[4,32,128]{2,1,0:T(8,128)S(1)} %get-tuple-element.70), channel_id=1, source_target_pairs={{0,4},{4,0},{8,12},{12,8},{1,5},{5,1},{9,13},{13,9},{2,6},{6,2},{1... | collective-permute-start | bytes 196616 | tf_op jit(solution)/shard_map/ppermute | solution.py:318
  7.1 6.5 %collective-permute-start.4 = (f32[4,32,128]{2,1,0:T(8,128)S(1)}, f32[4,32,128]{2,1,0:T(8,128)S(1)}, u32[]{:S(2)}, u32[]{:S(2)}) collective-permute-start(f32[4,32,128]{2,1,0:T(8,128)S(1)} %get-tuple-element.71), channel_id=1, source_target_pairs={{4,8},{8,4},{5,9},{9,5},{6,10},{10,6},{7,11},{11,7},{20,24},{24,20... | collective-permute-start | bytes 196616 | tf_op jit(solution)/shard_map/ppermute | solution.py:318
  13.7 2.8 %copy-start.1 = (f32[4,96,32,128]{3,2,1,0:T(8,128)S(1)}, f32[4,96,32,128]{3,2,1,0:T(8,128)}, u32[]{:S(2)}) copy-start(f32[4,96,32,128]{3,2,1,0:T(8,128)} %refs_10_.7) | copy-start | bytes 18874372
  22.7 35.3 %collective-permute-start.7 = (f32[96,32,128]{2,1,0:T(8,128)S(1)}, f32[96,32,128]{2,1,0:T(8,128)S(1)}, u32[]{:S(2)}, u32[]{:S(2)}) collective-permute-start(f32[96,32,128]{2,1,0:T(8,128)S(1)} %get-tuple-element.82.refs_3_), channel_id=1, source_target_pairs={{0,16},{16,0},{32,48},{48,32},{64,80},{80,64},{96,112},{112,96},{1... | collective-permute-start | bytes 4718600 | tf_op jit(solution)/shard_map/ppermute | solution.py:315
  24.2 16.1 %collective-permute-start.6 = (f32[64,32,128]{2,1,0:T(8,128)S(1)}, f32[64,32,128]{2,1,0:T(8,128)S(1)}, u32[]{:S(2)}, u32[]{:S(2)}) collective-permute-start(f32[64,32,128]{2,1,0:T(8,128)S(1)} %get-tuple-element.74), channel_id=1, source_target_pairs={{16,32},{32,16},{48,64},{64,48},{80,96},{96,80},{17,33},{33,17},{4... | collective-permute-start | bytes 3145736 | tf_op jit(solution)/shard_map/ppermute | solution.py:312
  27.0 18.9 %collective-permute-start.5 = (f32[32,32,128]{2,1,0:T(8,128)S(1)}, f32[32,32,128]{2,1,0:T(8,128)S(1)}, u32[]{:S(2)}, u32[]{:S(2)}) collective-permute-start(f32[32,32,128]{2,1,0:T(8,128)S(1)} %get-tuple-element.73), channel_id=1, source_target_pairs={{16,32},{32,16},{48,64},{64,48},{80,96},{96,80},{17,33},{33,17},{4... | collective-permute-start | bytes 1572872 | tf_op jit(solution)/shard_map/ppermute | solution.py:312
  40.3 17.7 %slice-start = ((s8[6291456]{0:T(1024)(128)(4,1)}), s8[4194304]{0:T(1024)(128)(4,1)S(1)}, s32[]{:S(2)}) async-start(s8[6291456]{0:T(1024)(128)(4,1)} %bitcast), calls=%async_computation | async-start | bytes 8388608
  45.9 12.1 %slice-start.1 = ((s8[6291456]{0:T(1024)(128)(4,1)}), s8[2097152]{0:T(1024)(128)(4,1)S(1)}, s32[]{:S(2)}) async-start(s8[6291456]{0:T(1024)(128)(4,1)} %bitcast), calls=%async_computation.1 | async-start | bytes 4194304
  46.3 11.8 %collective-permute-start.8 = (f32[4,96,128]{2,1,0:T(8,128)S(1)}, f32[4,96,128]{2,1,0:T(8,128)S(1)}, u32[]{:S(2)}, u32[]{:S(2)}) collective-permute-start(f32[4,96,128]{2,1,0:T(8,128)S(1)} %get-tuple-element.83), channel_id=1, source_target_pairs={{0,1},{1,0},{2,3},{3,2},{4,5},{5,4},{6,7},{7,6},{8,9},{9,8},{10,11... | collective-permute-start | bytes 589832 | tf_op jit(solution)/shard_map/ppermute | solution.py:318
  51.1 6.9 %collective-permute-start.9 = (f32[4,96,128]{2,1,0:T(8,128)S(1)}, f32[4,96,128]{2,1,0:T(8,128)S(1)}, u32[]{:S(2)}, u32[]{:S(2)}) collective-permute-start(f32[4,96,128]{2,1,0:T(8,128)S(1)} %get-tuple-element.84), channel_id=1, source_target_pairs={{1,2},{2,1},{5,6},{6,5},{9,10},{10,9},{13,14},{14,13},{17,18},{18,... | collective-permute-start | bytes 589832 | tf_op jit(solution)/shard_map/ppermute | solution.py:318
  51.8 4.3 %collective-permute-start.10 = (f32[4,32,128]{2,1,0:T(8,128)S(1)}, f32[4,32,128]{2,1,0:T(8,128)S(1)}, u32[]{:S(2)}, u32[]{:S(2)}) collective-permute-start(f32[4,32,128]{2,1,0:T(8,128)S(1)} %get-tuple-element.85), channel_id=1, source_target_pairs={{0,4},{4,0},{8,12},{12,8},{1,5},{5,1},{9,13},{13,9},{2,6},{6,2},{1... | collective-permute-start | bytes 196616 | tf_op jit(solution)/shard_map/ppermute | solution.py:318
  51.9 6.2 %collective-permute-start.11 = (f32[4,32,128]{2,1,0:T(8,128)S(1)}, f32[4,32,128]{2,1,0:T(8,128)S(1)}, u32[]{:S(2)}, u32[]{:S(2)}) collective-permute-start(f32[4,32,128]{2,1,0:T(8,128)S(1)} %get-tuple-element.86), channel_id=1, source_target_pairs={{4,8},{8,4},{5,9},{9,5},{6,10},{10,6},{7,11},{11,7},{20,24},{24,20... | collective-permute-start | bytes 196616 | tf_op jit(solution)/shard_map/ppermute | solution.py:318
  62.9 31.2 %collective-permute-start.14 = (f32[96,32,128]{2,1,0:T(8,128)S(1)}, f32[96,32,128]{2,1,0:T(8,128)S(1)}, u32[]{:S(2)}, u32[]{:S(2)}) collective-permute-start(f32[96,32,128]{2,1,0:T(8,128)S(1)} %get-tuple-element.97.refs_3_), channel_id=1, source_target_pairs={{0,16},{16,0},{32,48},{48,32},{64,80},{80,64},{96,112},{112,96},{1... | collective-permute-start | bytes 4718600 | tf_op jit(solution)/shard_map/ppermute | solution.py:315
  63.0 16.1 %collective-permute-start.13 = (f32[64,32,128]{2,1,0:T(8,128)S(1)}, f32[64,32,128]{2,1,0:T(8,128)S(1)}, u32[]{:S(2)}, u32[]{:S(2)}) collective-permute-start(f32[64,32,128]{2,1,0:T(8,128)S(1)} %shard_map.62.refs_3_), channel_id=1, source_target_pairs={{16,32},{32,16},{48,64},{64,48},{80,96},{96,80},{17,33},{33,17},{4... | collective-permute-start | bytes 3145736 | tf_op jit(solution)/shard_map/ppermute | solution.py:312
  66.0 18.7 %collective-permute-start.12 = (f32[32,32,128]{2,1,0:T(8,128)S(1)}, f32[32,32,128]{2,1,0:T(8,128)S(1)}, u32[]{:S(2)}, u32[]{:S(2)}) collective-permute-start(f32[32,32,128]{2,1,0:T(8,128)S(1)} %get-tuple-element.89), channel_id=1, source_target_pairs={{16,32},{32,16},{48,64},{64,48},{80,96},{96,80},{17,33},{33,17},{4... | collective-permute-start | bytes 1572872 | tf_op jit(solution)/shard_map/ppermute | solution.py:312
  85.1 9.0 %collective-permute-start.15 = (f32[4,96,128]{2,1,0:T(8,128)S(1)}, f32[4,96,128]{2,1,0:T(8,128)S(1)}, u32[]{:S(2)}, u32[]{:S(2)}) collective-permute-start(f32[4,96,128]{2,1,0:T(8,128)S(1)} %get-tuple-element.98), channel_id=1, source_target_pairs={{0,1},{1,0},{2,3},{3,2},{4,5},{5,4},{6,7},{7,6},{8,9},{9,8},{10,11... | collective-permute-start | bytes 589832 | tf_op jit(solution)/shard_map/ppermute | solution.py:318
  87.2 6.9 %collective-permute-start.16 = (f32[4,96,128]{2,1,0:T(8,128)S(1)}, f32[4,96,128]{2,1,0:T(8,128)S(1)}, u32[]{:S(2)}, u32[]{:S(2)}) collective-permute-start(f32[4,96,128]{2,1,0:T(8,128)S(1)} %get-tuple-element.99), channel_id=1, source_target_pairs={{1,2},{2,1},{5,6},{6,5},{9,10},{10,9},{13,14},{14,13},{17,18},{18,... | collective-permute-start | bytes 589832 | tf_op jit(solution)/shard_map/ppermute | solution.py:318
  87.9 4.3 %collective-permute-start.17 = (f32[4,32,128]{2,1,0:T(8,128)S(1)}, f32[4,32,128]{2,1,0:T(8,128)S(1)}, u32[]{:S(2)}, u32[]{:S(2)}) collective-permute-start(f32[4,32,128]{2,1,0:T(8,128)S(1)} %get-tuple-element.100), channel_id=1, source_target_pairs={{0,4},{4,0},{8,12},{12,8},{1,5},{5,1},{9,13},{13,9},{2,6},{6,2},{1... | collective-permute-start | bytes 196616 | tf_op jit(solution)/shard_map/ppermute | solution.py:318
  87.9 6.2 %collective-permute-start.18 = (f32[4,32,128]{2,1,0:T(8,128)S(1)}, f32[4,32,128]{2,1,0:T(8,128)S(1)}, u32[]{:S(2)}, u32[]{:S(2)}) collective-permute-start(f32[4,32,128]{2,1,0:T(8,128)S(1)} %get-tuple-element.101), channel_id=1, source_target_pairs={{4,8},{8,4},{5,9},{9,5},{6,10},{10,6},{7,11},{11,7},{20,24},{24,20... | collective-permute-start | bytes 196616 | tf_op jit(solution)/shard_map/ppermute | solution.py:318
  98.9 35.7 %collective-permute-start.21 = (f32[96,32,128]{2,1,0:T(8,128)S(1)}, f32[96,32,128]{2,1,0:T(8,128)S(1)}, u32[]{:S(2)}, u32[]{:S(2)}) collective-permute-start(f32[96,32,128]{2,1,0:T(8,128)S(1)} %get-tuple-element.111.refs_3_), channel_id=1, source_target_pairs={{0,16},{16,0},{32,48},{48,32},{64,80},{80,64},{96,112},{112,96},{1... | collective-permute-start | bytes 4718600 | tf_op jit(solution)/shard_map/ppermute | solution.py:315
  99.0 16.1 %collective-permute-start.20 = (f32[64,32,128]{2,1,0:T(8,128)S(1)}, f32[64,32,128]{2,1,0:T(8,128)S(1)}, u32[]{:S(2)}, u32[]{:S(2)}) collective-permute-start(f32[64,32,128]{2,1,0:T(8,128)S(1)} %shard_map.65.refs_3_), channel_id=1, source_target_pairs={{16,32},{32,16},{48,64},{64,48},{80,96},{96,80},{17,33},{33,17},{4... | collective-permute-start | bytes 3145736 | tf_op jit(solution)/shard_map/ppermute | solution.py:312
  102.4 18.3 %collective-permute-start.19 = (f32[32,32,128]{2,1,0:T(8,128)S(1)}, f32[32,32,128]{2,1,0:T(8,128)S(1)}, u32[]{:S(2)}, u32[]{:S(2)}) collective-permute-start(f32[32,32,128]{2,1,0:T(8,128)S(1)} %get-tuple-element.103), channel_id=1, source_target_pairs={{16,32},{32,16},{48,64},{64,48},{80,96},{96,80},{17,33},{33,17},{4... | collective-permute-start | bytes 1572872 | tf_op jit(solution)/shard_map/ppermute | solution.py:312
  121.1 13.5 %collective-permute-start.22 = (f32[4,96,128]{2,1,0:T(8,128)S(1)}, f32[4,96,128]{2,1,0:T(8,128)S(1)}, u32[]{:S(2)}, u32[]{:S(2)}) collective-permute-start(f32[4,96,128]{2,1,0:T(8,128)S(1)} %get-tuple-element.112), channel_id=1, source_target_pairs={{0,1},{1,0},{2,3},{3,2},{4,5},{5,4},{6,7},{7,6},{8,9},{9,8},{10,11... | collective-permute-start | bytes 589832 | tf_op jit(solution)/shard_map/ppermute | solution.py:318
  123.8 10.8 %collective-permute-start.23 = (f32[4,96,128]{2,1,0:T(8,128)S(1)}, f32[4,96,128]{2,1,0:T(8,128)S(1)}, u32[]{:S(2)}, u32[]{:S(2)}) collective-permute-start(f32[4,96,128]{2,1,0:T(8,128)S(1)} %get-tuple-element.113), channel_id=1, source_target_pairs={{1,2},{2,1},{5,6},{6,5},{9,10},{10,9},{13,14},{14,13},{17,18},{18,... | collective-permute-start | bytes 589832 | tf_op jit(solution)/shard_map/ppermute | solution.py:318
  124.5 4.3 %collective-permute-start.24 = (f32[4,32,128]{2,1,0:T(8,128)S(1)}, f32[4,32,128]{2,1,0:T(8,128)S(1)}, u32[]{:S(2)}, u32[]{:S(2)}) collective-permute-start(f32[4,32,128]{2,1,0:T(8,128)S(1)} %get-tuple-element.114), channel_id=1, source_target_pairs={{0,4},{4,0},{8,12},{12,8},{1,5},{5,1},{9,13},{13,9},{2,6},{6,2},{1... | collective-permute-start | bytes 196616 | tf_op jit(solution)/shard_map/ppermute | solution.py:318
  124.6 6.4 %collective-permute-start.25 = (f32[4,32,128]{2,1,0:T(8,128)S(1)}, f32[4,32,128]{2,1,0:T(8,128)S(1)}, u32[]{:S(2)}, u32[]{:S(2)}) collective-permute-start(f32[4,32,128]{2,1,0:T(8,128)S(1)} %get-tuple-element.115), channel_id=1, source_target_pairs={{4,8},{8,4},{5,9},{9,5},{6,10},{10,6},{7,11},{11,7},{20,24},{24,20... | collective-permute-start | bytes 196616 | tf_op jit(solution)/shard_map/ppermute | solution.py:318
  128.8 16.1 %collective-permute-start.27 = (f32[64,32,128]{2,1,0:T(8,128)S(1)}, f32[64,32,128]{2,1,0:T(8,128)S(1)}, u32[]{:S(2)}, u32[]{:S(2)}) collective-permute-start(f32[64,32,128]{2,1,0:T(8,128)S(1)} %shard_map.68.refs_3_), channel_id=1, source_target_pairs={{16,32},{32,16},{48,64},{64,48},{80,96},{96,80},{17,33},{33,17},{4... | collective-permute-start | bytes 3145736 | tf_op jit(solution)/shard_map/ppermute | solution.py:312
  131.0 19.6 %collective-permute-start.26 = (f32[32,32,128]{2,1,0:T(8,128)S(1)}, f32[32,32,128]{2,1,0:T(8,128)S(1)}, u32[]{:S(2)}, u32[]{:S(2)}) collective-permute-start(f32[32,32,128]{2,1,0:T(8,128)S(1)} %get-tuple-element.117), channel_id=1, source_target_pairs={{16,32},{32,16},{48,64},{64,48},{80,96},{96,80},{17,33},{33,17},{4... | collective-permute-start | bytes 1572872 | tf_op jit(solution)/shard_map/ppermute | solution.py:312
  140.2 13.0 %collective-permute-start.33 = (f32[6,32,128]{2,1,0:T(8,128)S(1)}, f32[6,32,128]{2,1,0:T(8,128)S(1)}, u32[]{:S(2)}, u32[]{:S(2)}) collective-permute-start(f32[6,32,128]{2,1,0:T(8,128)S(1)} %get-tuple-element.123.refs_3_), channel_id=1, source_target_pairs={{0,12},{4,8},{8,4},{12,0},{1,13},{5,9},{9,5},{13,1},{2,14},{6,10},... | collective-permute-start | bytes 294920 | tf_op jit(solution)/shard_map/ppermute | solution.py:331
  142.3 13.0 %collective-permute-start.32 = (f32[6,32,128]{2,1,0:T(8,128)S(1)}, f32[6,32,128]{2,1,0:T(8,128)S(1)}, u32[]{:S(2)}, u32[]{:S(2)}) collective-permute-start(f32[6,32,128]{2,1,0:T(8,128)S(1)} %get-tuple-element.123.refs_3_), channel_id=1, source_target_pairs={{0,8},{4,12},{8,0},{12,4},{1,9},{5,13},{9,1},{13,5},{2,10},{6,14},... | collective-permute-start | bytes 294920 | tf_op jit(solution)/shard_map/ppermute | solution.py:331
  142.4 12.9 %collective-permute-start.31 = (f32[6,32,128]{2,1,0:T(8,128)S(1)}, f32[6,32,128]{2,1,0:T(8,128)S(1)}, u32[]{:S(2)}, u32[]{:S(2)}) collective-permute-start(f32[6,32,128]{2,1,0:T(8,128)S(1)} %get-tuple-element.123.refs_3_), channel_id=1, source_target_pairs={{0,4},{4,0},{8,12},{12,8},{1,5},{5,1},{9,13},{13,9},{2,6},{6,2},{1... | collective-permute-start | bytes 294920 | tf_op jit(solution)/shard_map/ppermute | solution.py:331
  151.0 8.0 %collective-permute-start.30 = (f32[2,32,128]{2,1,0:T(8,128)S(1)}, f32[2,32,128]{2,1,0:T(8,128)S(1)}, u32[]{:S(2)}, u32[]{:S(2)}) collective-permute-start(f32[2,32,128]{2,1,0:T(8,128)S(1)} %get-tuple-element.119.refs_1_), channel_id=1, source_target_pairs={{0,12},{4,8},{8,4},{12,0},{1,13},{5,9},{9,5},{13,1},{2,14},{6,10},... | collective-permute-start | bytes 98312 | tf_op jit(solution)/shard_map/ppermute | solution.py:331
  153.1 5.9 %collective-permute-start.29 = (f32[2,32,128]{2,1,0:T(8,128)S(1)}, f32[2,32,128]{2,1,0:T(8,128)S(1)}, u32[]{:S(2)}, u32[]{:S(2)}) collective-permute-start(f32[2,32,128]{2,1,0:T(8,128)S(1)} %get-tuple-element.119.refs_1_), channel_id=1, source_target_pairs={{0,8},{4,12},{8,0},{12,4},{1,9},{5,13},{9,1},{13,5},{2,10},{6,14},... | collective-permute-start | bytes 98312 | tf_op jit(solution)/shard_map/ppermute | solution.py:331
  153.2 5.8 %collective-permute-start.28 = (f32[2,32,128]{2,1,0:T(8,128)S(1)}, f32[2,32,128]{2,1,0:T(8,128)S(1)}, u32[]{:S(2)}, u32[]{:S(2)}) collective-permute-start(f32[2,32,128]{2,1,0:T(8,128)S(1)} %get-tuple-element.119.refs_1_), channel_id=1, source_target_pairs={{0,4},{4,0},{8,12},{12,8},{1,5},{5,1},{9,13},{13,9},{2,6},{6,2},{1... | collective-permute-start | bytes 98312 | tf_op jit(solution)/shard_map/ppermute | solution.py:331

commit v4 on v3

--- a/solution.py
+++ b/solution.py
@@ -12,7 +12,7 @@
 TILE = 8
 UNROLL = 19
 PIECES = 2
-FIRST = 64
+FIRST = 72
 RATE = 0.05
 GRID = P("lat", "lon", "lev", None)
 
@@ -96,12 +96,17 @@
         ]
         for load in loads:
             load.start()
+    if last:
+        end, sems = extra[1:]
+        writes = [
+            pltpu.make_async_copy(new[k], end.at[rows[k]], sems.at[k - 1]) for k in (1, 2, 3)
+        ]
     length, levels, members = new[0].shape
     even_lev, even_lon = place[1] == 0, place[2] == 0
     parts = levels // TILE
     spot = lax.broadcasted_iota(jnp.int32, (TILE, members), 0)
     at_low, at_high = spot == 0, spot == TILE - 1
-    for k in range(4):
+    for k in (1, 2, 3, 0) if last else range(4):
         row = rows[k]
         if first:
             loads[k].wait()
@@ -163,7 +168,11 @@
             extra[2][k] = either(even_lon, high, low)
             extra[3][k] = either(even_lon, low, high)
         if last and k > 0:
+            writes[k - 1].start()
             line_statistics(new[k], total + value, extra[0], 2 * (k - 1))
+    if last:
+        for write in writes:
+            write.wait()
 
 
 def line_statistics(row, total, out, at):
@@ -242,15 +251,18 @@
 
 def normalise(count, *refs):
     state, stats = refs[:count], refs[count : count + 4]
-    out, end, work, sems = refs[-4:]
     rows, _ = roles(here()[0])
-    offset = 0 if count == 1 else 1
+    copies = []
+    if count == 1:
+        out, end, work, sems = refs[-4:]
+        copies.append(pltpu.make_async_copy(state[0], end.at[rows[0]], sems.at[0]))
+        copies[0].start()
+        rows = rows[:1]
+    else:
+        out, work, sems = refs[-3:]
+        rows = rows[1:]
     length = state[0].shape[0]
-    copies = [
-        pltpu.make_async_copy(state[k], end.at[rows[k + offset]], sems.at[k]) for k in range(count)
-    ]
-    for copy in copies:
-        copy.start()
+    half = length // 2
     for k in range(count):
         means = [s[2 * k] for s in stats]
         mean = 0.25 * ((means[0] + means[1]) + (means[2] + means[3]))
@@ -265,10 +277,15 @@
             work[k, x] = (state[k][x] - mean) * scale
             return carry
 
-        lax.fori_loop(0, length, body, 0, unroll=4)
-        copy = pltpu.make_async_copy(work.at[k], out.at[rows[k + offset]], sems.at[count + k])
-        copy.start()
-        copies.append(copy)
+        for h in range(2):
+            lax.fori_loop(half * h, half * (h + 1), body, 0, unroll=4)
+            cut = pl.ds(half * h, half)
+            copies.append(
+                pltpu.make_async_copy(
+                    work.at[k, cut], out.at[rows[k], cut], sems.at[1 + 2 * k + h]
+                )
+            )
+            copies[-1].start()
     for copy in copies:
         copy.wait()
 
@@ -374,14 +391,17 @@
             functools.partial(spread_step, step == 0, last),
             [outer, *inner_rows, core_row, *ends, *winds],
             [row_type] * 4
-            + ([stats_type] if last else end_types)
+            + ([stats_type, whole] if last else end_types)
             + ([whole] if step == 0 else []),
             SPREAD_FLOPS,
             in_specs=[vmem] * 11 + [anywhere if step == 0 else vmem],
-            scratch=[pltpu.SemaphoreType.DMA((4,))] if step == 0 else [],
+            out_specs=[vmem] * 5 + [anywhere] if last else None,
+            scratch=[pltpu.SemaphoreType.DMA((4,))] if step == 0 or last else [],
         )
         if step == 0:
             winds[2] = placed(made.pop(), pltpu.VMEM)
+        if last:
+            end = made.pop()
         inner_rows, extra = made[:3], made[3:]
         if not last:
             core_row = beside(inner_rows[2])
@@ -391,14 +411,14 @@
         return call(
             functools.partial(normalise, count),
             [*rows_of, stats, *others, *results],
-            [whole, whole],
+            [whole] * max(1, len(results)),
             10**9,
             aliases={count + 4 + i: i for i in range(len(results))},
             in_specs=[vmem] * (count + 4) + [anywhere] * len(results),
-            out_specs=[anywhere, anywhere],
+            out_specs=[anywhere] * max(1, len(results)),
             scratch=[
                 pltpu.VMEM((count, length, levels, members), jnp.float32),
-                pltpu.SemaphoreType.DMA((2 * count,)),
+                pltpu.SemaphoreType.DMA((1 + 2 * count,)),
             ],
             room=8 * 2**20,
         )
@@ -413,7 +433,7 @@
     )
     late = from_others(stats)
     results = normalised(inner_rows, extra[0], early)
-    return tuple(normalised([outer], stats, late, *results))
+    return tuple(normalised([outer], stats, late, *results, end))
 
 
 SPREAD_FLOPS = 2 * 10**10

time: 162 us -> 162 us (level)
  transfers between devices with their start and end apart: 34 -> 34, of which waited for: 14 -> 15; matrix products, arithmetic and copies ran while one was open for 0% -> 0% of each run, Pallas kernels for 8% -> 7%
where the time goes in v4:
time: 162 us; the launch traced here: 160 us
  starting transfers between devices  62.5 us (39%)
  waiting for transfers between devices  61.3 us (38%)
  Pallas kernels  32.7 us (20%)
  local copies, waits for them, and re-layouts  2.8 us (2%)
    ppermute x8, waiting for transfers between devices, across(): return lax.ppermute(array, 'lat', pairs(lats, 1))  53.4 us
    pallas_call x16, Pallas kernels, call(): pl.pallas_call(kernel, out_shape=outs, in_specs=in_specs or [vmem] * len(...  32.7 us
    ppermute x16, starting transfers between devices, swap(): return lax.ppermute(array, axis, pairs(lax.axis_size(axis), start))  31.1 us
    ppermute x8, starting transfers between devices, across(): return lax.ppermute(array, 'lat', pairs(lats, 1))  22.6 us
    ppermute x6, starting transfers between devices, from_others(): made.append(lax.ppermute(array, 'lon', [(i, i ^ d) for i in range(lons)]))  8.51 us
    ppermute x16, waiting for transfers between devices, swap(): return lax.ppermute(array, axis, pairs(lax.axis_size(axis), start))  7.03 us
  transfers between devices with their start and end apart: 34, of which 15 were waited for; matrix products, arithmetic and copies ran while one was open for 0% of the time, Pallas kernels for 7%

profile of v4, /device:TPU:14, one launch (start us, length us, event | category | flops | bytes accessed | tf_op | source)
XLA Modules:
  0.0 160.5 jit_solution(11671017084940104627)
XLA Ops:
  0.6 3.2 %shard_map.59 = (f32[96,32,128]{2,1,0:T(8,128)S(1)}, f32[96,32,128]{2,1,0:T(8,128)S(1)}, f32[96,32,128]{2,1,0:T(8,128)S(1)}, f32[96,32,128]{2,1,0:T(8,128)S(1)},...) custom-call(f32[4,96,32,128]{3,2,1,0:T(8,128)} %source.3), custom_call_target="tpu_custom_call" | custom-call | flops 1000000000 | tf_op jit(solution)/shard_map/pallas_call | solution.py:309
  3.8 0.1 collective-permute-start
  3.9 2.0 %collective-permute-start.1 = (f32[4,96,128]{2,1,0:T(8,128)S(1)}, f32[4,96,128]{2,1,0:T(8,128)S(1)}, u32[]{:S(2)}, u32[]{:S(2)}) collective-permute-start(f32[4,96,128]{2,1,0:T(8,128)S(1)} %get-tuple-element.67), channel_id=1, source_target_pairs={{0,1},{1,0},{2,3},{3,2},{4,5},{5,4},{6,7},{7,6},{8,9},{9,8},{10,11... | collective-permute-start | bytes 589832 | tf_op jit(solution)/shard_map/ppermute | solution.py:335
  5.9 0.7 collective-permute-start.2
  6.6 0.5 collective-permute-start.3
  7.1 4.3 %collective-permute-start.4 = (f32[4,32,128]{2,1,0:T(8,128)S(1)}, f32[4,32,128]{2,1,0:T(8,128)S(1)}, u32[]{:S(2)}, u32[]{:S(2)}) collective-permute-start(f32[4,32,128]{2,1,0:T(8,128)S(1)} %get-tuple-element.70), channel_id=1, source_target_pairs={{4,8},{8,4},{5,9},{9,5},{6,10},{10,6},{7,11},{11,7},{20,24},{24,20... | collective-permute-start | bytes 196616 | tf_op jit(solution)/shard_map/ppermute | solution.py:335
  11.4 2.2 %collective-permute-done.4.refs_8_ = f32[4,32,128]{2,1,0:T(8,128)S(1)} collective-permute-done((f32[4,32,128]{2,1,0:T(8,128)S(1)}, f32[4,32,128]{2,1,0:T(8,128)S(1)}, u32[]{:S(2)}, u32[]{:S(2)}) %collective-permute-start.4) | collective-permute-done | bytes 65568 | tf_op jit(solution)/shard_map/ppermute | solution.py:335
  13.7 2.8 %copy-done.1 = f32[4,96,32,128]{3,2,1,0:T(8,128)S(1)} copy-done((f32[4,96,32,128]{3,2,1,0:T(8,128)S(1)}, f32[4,96,32,128]{3,2,1,0:T(8,128)}, u32[]{:S(2)}) %copy-start.1) | copy-done | bytes 6291480
  16.5 6.2 %shard_map.60 = (f32[96,32,128]{2,1,0:T(8,128)S(1)}, f32[96,32,128]{2,1,0:T(8,128)S(1)}, f32[96,32,128]{2,1,0:T(8,128)S(1)}, f32[96,32,128]{2,1,0:T(8,128)S(1)},...) custom-call(f32[96,32,128]{2,1,0:T(8,128)S(1)} %get-tuple-element.63, ...), custom_call_target="tpu_custom_call" | custom-call | flops 20000000000 | tf_op jit(solution)/shard_map/pallas_call | solution.py:309
  22.7 0.1 collective-permute-start.7
  22.8 1.5 shard_map.61
  24.4 2.9 %collective-permute-start.6 = (f32[72,32,128]{2,1,0:T(8,128)S(1)}, f32[72,32,128]{2,1,0:T(8,128)S(1)}, u32[]{:S(2)}, u32[]{:S(2)}) collective-permute-start(f32[72,32,128]{2,1,0:T(8,128)S(1)} %get-tuple-element.73), channel_id=1, source_target_pairs={{16,32},{32,16},{48,64},{64,48},{80,96},{96,80},{17,33},{33,17},{4... | collective-permute-start | bytes 3538952 | tf_op jit(solution)/shard_map/ppermute | solution.py:329
  27.3 2.8 %collective-permute-start.5 = (f32[24,32,128]{2,1,0:T(8,128)S(1)}, f32[24,32,128]{2,1,0:T(8,128)S(1)}, u32[]{:S(2)}, u32[]{:S(2)}) collective-permute-start(f32[24,32,128]{2,1,0:T(8,128)S(1)} %get-tuple-element.72), channel_id=1, source_target_pairs={{16,32},{32,16},{48,64},{64,48},{80,96},{96,80},{17,33},{33,17},{4... | collective-permute-start | bytes 1179656 | tf_op jit(solution)/shard_map/ppermute | solution.py:329
  30.1 11.9 %collective-permute-done.6.halo = f32[72,32,128]{2,1,0:T(8,128)S(1)} collective-permute-done((f32[72,32,128]{2,1,0:T(8,128)S(1)}, f32[72,32,128]{2,1,0:T(8,128)S(1)}, u32[]{:S(2)}, u32[]{:S(2)}) %collective-permute-start.6) | collective-permute-done | bytes 1179680 | tf_op jit(solution)/shard_map/ppermute | solution.py:329
  42.0 0.3 shard_map.62.refs_3_
  42.3 3.9 %collective-permute-done.5.refs_2_ = f32[24,32,128]{2,1,0:T(8,128)S(1)} collective-permute-done((f32[24,32,128]{2,1,0:T(8,128)S(1)}, f32[24,32,128]{2,1,0:T(8,128)S(1)}, u32[]{:S(2)}, u32[]{:S(2)}) %collective-permute-start.5) | collective-permute-done | bytes 393248 | tf_op jit(solution)/shard_map/ppermute | solution.py:329
  46.2 0.3 shard_map.63
  46.5 4.9 %collective-permute-start.8 = (f32[4,96,128]{2,1,0:T(8,128)S(1)}, f32[4,96,128]{2,1,0:T(8,128)S(1)}, u32[]{:S(2)}, u32[]{:S(2)}) collective-permute-start(f32[4,96,128]{2,1,0:T(8,128)S(1)} %get-tuple-element.82), channel_id=1, source_target_pairs={{0,1},{1,0},{2,3},{3,2},{4,5},{5,4},{6,7},{7,6},{8,9},{9,8},{10,11... | collective-permute-start | bytes 589832 | tf_op jit(solution)/shard_map/ppermute | solution.py:335
  51.4 0.7 collective-permute-start.9
  52.1 0.1 collective-permute-start.10
  52.2 3.9 %collective-permute-start.11 = (f32[4,32,128]{2,1,0:T(8,128)S(1)}, f32[4,32,128]{2,1,0:T(8,128)S(1)}, u32[]{:S(2)}, u32[]{:S(2)}) collective-permute-start(f32[4,32,128]{2,1,0:T(8,128)S(1)} %get-tuple-element.85), channel_id=1, source_target_pairs={{4,8},{8,4},{5,9},{9,5},{6,10},{10,6},{7,11},{11,7},{20,24},{24,20... | collective-permute-start | bytes 196616 | tf_op jit(solution)/shard_map/ppermute | solution.py:335
  56.1 0.3 collective-permute-done.10.refs_7_
  56.4 1.9 %collective-permute-done.11.refs_8_ = f32[4,32,128]{2,1,0:T(8,128)S(1)} collective-permute-done((f32[4,32,128]{2,1,0:T(8,128)S(1)}, f32[4,32,128]{2,1,0:T(8,128)S(1)}, u32[]{:S(2)}, u32[]{:S(2)}) %collective-permute-start.11) | collective-permute-done | bytes 65568 | tf_op jit(solution)/shard_map/ppermute | solution.py:335
  58.4 4.8 %shard_map.64 = (f32[96,32,128]{2,1,0:T(8,128)S(1)}, f32[96,32,128]{2,1,0:T(8,128)S(1)}, f32[96,32,128]{2,1,0:T(8,128)S(1)}, f32[96,32,128]{2,1,0:T(8,128)S(1)},...) custom-call(f32[96,32,128]{2,1,0:T(8,128)S(1)} %get-tuple-element.78, ...), custom_call_target="tpu_custom_call" | custom-call | flops 20000000000 | tf_op jit(solution)/shard_map/pallas_call | solution.py:309
  63.2 0.1 collective-permute-start.14
  63.3 3.0 %collective-permute-start.13 = (f32[72,32,128]{2,1,0:T(8,128)S(1)}, f32[72,32,128]{2,1,0:T(8,128)S(1)}, u32[]{:S(2)}, u32[]{:S(2)}) collective-permute-start(f32[72,32,128]{2,1,0:T(8,128)S(1)} %shard_map.62.refs_3_), channel_id=1, source_target_pairs={{16,32},{32,16},{48,64},{64,48},{80,96},{96,80},{17,33},{33,17},{4... | collective-permute-start | bytes 3538952 | tf_op jit(solution)/shard_map/ppermute | solution.py:329
  66.3 2.5 %collective-permute-start.12 = (f32[24,32,128]{2,1,0:T(8,128)S(1)}, f32[24,32,128]{2,1,0:T(8,128)S(1)}, u32[]{:S(2)}, u32[]{:S(2)}) collective-permute-start(f32[24,32,128]{2,1,0:T(8,128)S(1)} %get-tuple-element.88), channel_id=1, source_target_pairs={{16,32},{32,16},{48,64},{64,48},{80,96},{96,80},{17,33},{33,17},{4... | collective-permute-start | bytes 1179656 | tf_op jit(solution)/shard_map/ppermute | solution.py:329
  68.8 11.9 %collective-permute-done.13.halo = f32[72,32,128]{2,1,0:T(8,128)S(1)} collective-permute-done((f32[72,32,128]{2,1,0:T(8,128)S(1)}, f32[72,32,128]{2,1,0:T(8,128)S(1)}, u32[]{:S(2)}, u32[]{:S(2)}) %collective-permute-start.13) | collective-permute-done | bytes 1179680 | tf_op jit(solution)/shard_map/ppermute | solution.py:329
  80.8 0.3 shard_map.65.refs_3_
  81.0 3.9 %collective-permute-done.12.refs_2_ = f32[24,32,128]{2,1,0:T(8,128)S(1)} collective-permute-done((f32[24,32,128]{2,1,0:T(8,128)S(1)}, f32[24,32,128]{2,1,0:T(8,128)S(1)}, u32[]{:S(2)}, u32[]{:S(2)}) %collective-permute-start.12) | collective-permute-done | bytes 393248 | tf_op jit(solution)/shard_map/ppermute | solution.py:329
  85.0 0.3 shard_map.66
  85.3 2.0 %collective-permute-start.15 = (f32[4,96,128]{2,1,0:T(8,128)S(1)}, f32[4,96,128]{2,1,0:T(8,128)S(1)}, u32[]{:S(2)}, u32[]{:S(2)}) collective-permute-start(f32[4,96,128]{2,1,0:T(8,128)S(1)} %get-tuple-element.97), channel_id=1, source_target_pairs={{0,1},{1,0},{2,3},{3,2},{4,5},{5,4},{6,7},{7,6},{8,9},{9,8},{10,11... | collective-permute-start | bytes 589832 | tf_op jit(solution)/shard_map/ppermute | solution.py:335
  87.3 0.7 collective-permute-start.16
  88.0 0.1 collective-permute-start.17
  88.1 3.9 %collective-permute-start.18 = (f32[4,32,128]{2,1,0:T(8,128)S(1)}, f32[4,32,128]{2,1,0:T(8,128)S(1)}, u32[]{:S(2)}, u32[]{:S(2)}) collective-permute-start(f32[4,32,128]{2,1,0:T(8,128)S(1)} %get-tuple-element.100), channel_id=1, source_target_pairs={{4,8},{8,4},{5,9},{9,5},{6,10},{10,6},{7,11},{11,7},{20,24},{24,20... | collective-permute-start | bytes 196616 | tf_op jit(solution)/shard_map/ppermute | solution.py:335
  92.0 0.3 collective-permute-done.17.refs_7_
  92.3 1.9 %collective-permute-done.18.refs_8_ = f32[4,32,128]{2,1,0:T(8,128)S(1)} collective-permute-done((f32[4,32,128]{2,1,0:T(8,128)S(1)}, f32[4,32,128]{2,1,0:T(8,128)S(1)}, u32[]{:S(2)}, u32[]{:S(2)}) %collective-permute-start.18) | collective-permute-done | bytes 65568 | tf_op jit(solution)/shard_map/ppermute | solution.py:335
  94.2 4.8 %shard_map.67 = (f32[96,32,128]{2,1,0:T(8,128)S(1)}, f32[96,32,128]{2,1,0:T(8,128)S(1)}, f32[96,32,128]{2,1,0:T(8,128)S(1)}, f32[96,32,128]{2,1,0:T(8,128)S(1)},...) custom-call(f32[96,32,128]{2,1,0:T(8,128)S(1)} %get-tuple-element.93, ...), custom_call_target="tpu_custom_call" | custom-call | flops 20000000000 | tf_op jit(solution)/shard_map/pallas_call | solution.py:309
  99.0 0.1 collective-permute-start.21
  99.1 3.4 %collective-permute-start.20 = (f32[72,32,128]{2,1,0:T(8,128)S(1)}, f32[72,32,128]{2,1,0:T(8,128)S(1)}, u32[]{:S(2)}, u32[]{:S(2)}) collective-permute-start(f32[72,32,128]{2,1,0:T(8,128)S(1)} %shard_map.65.refs_3_), channel_id=1, source_target_pairs={{16,32},{32,16},{48,64},{64,48},{80,96},{96,80},{17,33},{33,17},{4... | collective-permute-start | bytes 3538952 | tf_op jit(solution)/shard_map/ppermute | solution.py:329
  102.5 2.2 %collective-permute-start.19 = (f32[24,32,128]{2,1,0:T(8,128)S(1)}, f32[24,32,128]{2,1,0:T(8,128)S(1)}, u32[]{:S(2)}, u32[]{:S(2)}) collective-permute-start(f32[24,32,128]{2,1,0:T(8,128)S(1)} %get-tuple-element.102), channel_id=1, source_target_pairs={{16,32},{32,16},{48,64},{64,48},{80,96},{96,80},{17,33},{33,17},{4... | collective-permute-start | bytes 1179656 | tf_op jit(solution)/shard_map/ppermute | solution.py:329
  104.7 11.9 %collective-permute-done.20.halo = f32[72,32,128]{2,1,0:T(8,128)S(1)} collective-permute-done((f32[72,32,128]{2,1,0:T(8,128)S(1)}, f32[72,32,128]{2,1,0:T(8,128)S(1)}, u32[]{:S(2)}, u32[]{:S(2)}) %collective-permute-start.20) | collective-permute-done | bytes 1179680 | tf_op jit(solution)/shard_map/ppermute | solution.py:329
  116.6 0.3 shard_map.68.refs_3_
  116.9 3.9 %collective-permute-done.19.refs_2_ = f32[24,32,128]{2,1,0:T(8,128)S(1)} collective-permute-done((f32[24,32,128]{2,1,0:T(8,128)S(1)}, f32[24,32,128]{2,1,0:T(8,128)S(1)}, u32[]{:S(2)}, u32[]{:S(2)}) %collective-permute-start.19) | collective-permute-done | bytes 393248 | tf_op jit(solution)/shard_map/ppermute | solution.py:329
  120.9 0.3 shard_map.69
  121.2 2.7 %collective-permute-start.22 = (f32[4,96,128]{2,1,0:T(8,128)S(1)}, f32[4,96,128]{2,1,0:T(8,128)S(1)}, u32[]{:S(2)}, u32[]{:S(2)}) collective-permute-start(f32[4,96,128]{2,1,0:T(8,128)S(1)} %get-tuple-element.111), channel_id=1, source_target_pairs={{0,1},{1,0},{2,3},{3,2},{4,5},{5,4},{6,7},{7,6},{8,9},{9,8},{10,11... | collective-permute-start | bytes 589832 | tf_op jit(solution)/shard_map/ppermute | solution.py:335
  123.9 0.7 collective-permute-start.23
  124.5 0.1 collective-permute-start.24
  124.6 3.9 %collective-permute-start.25 = (f32[4,32,128]{2,1,0:T(8,128)S(1)}, f32[4,32,128]{2,1,0:T(8,128)S(1)}, u32[]{:S(2)}, u32[]{:S(2)}) collective-permute-start(f32[4,32,128]{2,1,0:T(8,128)S(1)} %get-tuple-element.114), channel_id=1, source_target_pairs={{4,8},{8,4},{5,9},{9,5},{6,10},{10,6},{7,11},{11,7},{20,24},{24,20... | collective-permute-start | bytes 196616 | tf_op jit(solution)/shard_map/ppermute | solution.py:335
  128.6 0.3 collective-permute-done.24.refs_7_
  128.9 2.1 %collective-permute-start.27 = (f32[72,32,128]{2,1,0:T(8,128)S(1)}, f32[72,32,128]{2,1,0:T(8,128)S(1)}, u32[]{:S(2)}, u32[]{:S(2)}) collective-permute-start(f32[72,32,128]{2,1,0:T(8,128)S(1)} %shard_map.68.refs_3_), channel_id=1, source_target_pairs={{16,32},{32,16},{48,64},{64,48},{80,96},{96,80},{17,33},{33,17},{4... | collective-permute-start | bytes 3538952 | tf_op jit(solution)/shard_map/ppermute | solution.py:329
  131.0 3.6 %collective-permute-start.26 = (f32[24,32,128]{2,1,0:T(8,128)S(1)}, f32[24,32,128]{2,1,0:T(8,128)S(1)}, u32[]{:S(2)}, u32[]{:S(2)}) collective-permute-start(f32[24,32,128]{2,1,0:T(8,128)S(1)} %get-tuple-element.116), channel_id=1, source_target_pairs={{16,32},{32,16},{48,64},{64,48},{80,96},{96,80},{17,33},{33,17},{4... | collective-permute-start | bytes 1179656 | tf_op jit(solution)/shard_map/ppermute | solution.py:329
  134.7 5.7 %shard_map.70 = (f32[96,32,128]{2,1,0:T(8,128)S(1)}, f32[96,32,128]{2,1,0:T(8,128)S(1)}, f32[96,32,128]{2,1,0:T(8,128)S(1)}, f32[96,32,128]{2,1,0:T(8,128)S(1)},...) custom-call(f32[96,32,128]{2,1,0:T(8,128)S(1)} %get-tuple-element.107.refs_0_, ...), custom_call_target="tpu_custom_call" | custom-call | flops 20000000000 | tf_op jit(solution)/shard_map/pallas_call | solution.py:309
  140.4 2.1 %collective-permute-start.33 = (f32[6,32,128]{2,1,0:T(8,128)S(1)}, f32[6,32,128]{2,1,0:T(8,128)S(1)}, u32[]{:S(2)}, u32[]{:S(2)}) collective-permute-start(f32[6,32,128]{2,1,0:T(8,128)S(1)} %get-tuple-element.122.refs_3_), channel_id=1, source_target_pairs={{0,12},{4,8},{8,4},{12,0},{1,13},{5,9},{9,5},{13,1},{2,14},{6,10},... | collective-permute-start | bytes 294920 | tf_op jit(solution)/shard_map/ppermute | solution.py:348
  142.5 2.1 %collective-permute-start.31 = (f32[6,32,128]{2,1,0:T(8,128)S(1)}, f32[6,32,128]{2,1,0:T(8,128)S(1)}, u32[]{:S(2)}, u32[]{:S(2)}) collective-permute-start(f32[6,32,128]{2,1,0:T(8,128)S(1)} %get-tuple-element.122.refs_3_), channel_id=1, source_target_pairs={{0,4},{4,0},{8,12},{12,8},{1,5},{5,1},{9,13},{13,9},{2,6},{6,2},{1... | collective-permute-start | bytes 294920 | tf_op jit(solution)/shard_map/ppermute | solution.py:348
  144.6 1.8 %collective-permute-done.27.halo = f32[72,32,128]{2,1,0:T(8,128)S(1)} collective-permute-done((f32[72,32,128]{2,1,0:T(8,128)S(1)}, f32[72,32,128]{2,1,0:T(8,128)S(1)}, u32[]{:S(2)}, u32[]{:S(2)}) %collective-permute-start.27) | collective-permute-done | bytes 1179680 | tf_op jit(solution)/shard_map/ppermute | solution.py:329
  146.4 0.3 shard_map.71.refs_3_
  146.7 3.9 %collective-permute-done.26.refs_2_ = f32[24,32,128]{2,1,0:T(8,128)S(1)} collective-permute-done((f32[24,32,128]{2,1,0:T(8,128)S(1)}, f32[24,32,128]{2,1,0:T(8,128)S(1)}, u32[]{:S(2)}, u32[]{:S(2)}) %collective-permute-start.26) | collective-permute-done | bytes 393248 | tf_op jit(solution)/shard_map/ppermute | solution.py:329
  150.6 0.5 shard_map.72
  151.1 2.1 %collective-permute-start.30 = (f32[2,32,128]{2,1,0:T(8,128)S(1)}, f32[2,32,128]{2,1,0:T(8,128)S(1)}, u32[]{:S(2)}, u32[]{:S(2)}) collective-permute-start(f32[2,32,128]{2,1,0:T(8,128)S(1)} %get-tuple-element.118.refs_1_), channel_id=1, source_target_pairs={{0,12},{4,8},{8,4},{12,0},{1,13},{5,9},{9,5},{13,1},{2,14},{6,10},... | collective-permute-start | bytes 98312 | tf_op jit(solution)/shard_map/ppermute | solution.py:348
  153.3 2.1 %collective-permute-start.28 = (f32[2,32,128]{2,1,0:T(8,128)S(1)}, f32[2,32,128]{2,1,0:T(8,128)S(1)}, u32[]{:S(2)}, u32[]{:S(2)}) collective-permute-start(f32[2,32,128]{2,1,0:T(8,128)S(1)} %get-tuple-element.118.refs_1_), channel_id=1, source_target_pairs={{0,4},{4,0},{8,12},{12,8},{1,5},{5,1},{9,13},{13,9},{2,6},{6,2},{1... | collective-permute-start | bytes 98312 | tf_op jit(solution)/shard_map/ppermute | solution.py:348
  155.4 2.4 %shard_map.73.refs_5_ = f32[4,96,32,128]{3,2,1,0:T(8,128)} custom-call(f32[96,32,128]{2,1,0:T(8,128)S(1)} %get-tuple-element.119.refs_0_, f32[96,32,128]{2,1,0:T(8,128)S(1)} %get-tuple-element.120.refs_1_, f32[96,32,128]{2,1,0:T(8,128)S(1)} %get-tuple-element.121.refs_2_, f32[6,32,128]{2,1,0:T(8,128)S(1)} %get-tuple-element.122.refs_3_, ...), custom_call_target="tpu_custom_call" | custom-call | flops 1000000000 | tf_op jit(solution)/shard_map/pallas_call | solution.py:309
  157.8 0.9 collective-permute-done.29.refs_3_
  158.6 1.7 %shard_map.74 = (f32[4,96,32,128]{3,2,1,0:T(8,128)}, f32[4,96,32,128]{3,2,1,0:T(8,128)}) custom-call(f32[96,32,128]{2,1,0:T(8,128)S(1)} %get-tuple-element.117.refs_0_, f32[2,32,128]{2,1,0:T(8,128)S(1)} %get-tuple-element.118.refs_1_, f32[2,32,128]{2,1,0:T(8,128)S(1)} %collective-permute-done.28.refs_2_, ...), custom_call_target="tpu_custom_call", output_to_operand_aliasing={{0}: (5, {}), {1}: (6, {})} | custom-call | flops 1000000000 | tf_op jit(solution)/shard_map/pallas_call | solution.py:309
  (29 shorter events, 0.2 us)
Async XLA Ops:
  0.6 13.0 %copy-start = (f32[4,96,32,128]{3,2,1,0:T(8,128)S(1)}, f32[4,96,32,128]{3,2,1,0:T(8,128)}, u32[]{:S(2)}) copy-start(f32[4,96,32,128]{3,2,1,0:T(8,128)} %refs_1_.7) | copy-start | bytes 18874372
  3.8 9.8 %collective-permute-start = (f32[96,32,128]{2,1,0:T(8,128)S(1)}, f32[96,32,128]{2,1,0:T(8,128)S(1)}, u32[]{:S(2)}, u32[]{:S(2)}) collective-permute-start(f32[96,32,128]{2,1,0:T(8,128)S(1)} %get-tuple-element.66.refs_3_), channel_id=1, source_target_pairs={{0,16},{16,0},{32,48},{48,32},{64,80},{80,64},{96,112},{112,96},{1... | collective-permute-start | bytes 4718600 | tf_op jit(solution)/shard_map/ppermute | solution.py:332
  3.9 9.7 %collective-permute-start.1 = (f32[4,96,128]{2,1,0:T(8,128)S(1)}, f32[4,96,128]{2,1,0:T(8,128)S(1)}, u32[]{:S(2)}, u32[]{:S(2)}) collective-permute-start(f32[4,96,128]{2,1,0:T(8,128)S(1)} %get-tuple-element.67), channel_id=1, source_target_pairs={{0,1},{1,0},{2,3},{3,2},{4,5},{5,4},{6,7},{7,6},{8,9},{9,8},{10,11... | collective-permute-start | bytes 589832 | tf_op jit(solution)/shard_map/ppermute | solution.py:335
  5.9 7.7 %collective-permute-start.2 = (f32[4,96,128]{2,1,0:T(8,128)S(1)}, f32[4,96,128]{2,1,0:T(8,128)S(1)}, u32[]{:S(2)}, u32[]{:S(2)}) collective-permute-start(f32[4,96,128]{2,1,0:T(8,128)S(1)} %get-tuple-element.68), channel_id=1, source_target_pairs={{1,2},{2,1},{5,6},{6,5},{9,10},{10,9},{13,14},{14,13},{17,18},{18,... | collective-permute-start | bytes 589832 | tf_op jit(solution)/shard_map/ppermute | solution.py:335
  6.6 4.8 %collective-permute-start.3 = (f32[4,32,128]{2,1,0:T(8,128)S(1)}, f32[4,32,128]{2,1,0:T(8,128)S(1)}, u32[]{:S(2)}, u32[]{:S(2)}) collective-permute-start(f32[4,32,128]{2,1,0:T(8,128)S(1)} %get-tuple-element.69), channel_id=1, source_target_pairs={{0,4},{4,0},{8,12},{12,8},{1,5},{5,1},{9,13},{13,9},{2,6},{6,2},{1... | collective-permute-start | bytes 196616 | tf_op jit(solution)/shard_map/ppermute | solution.py:335
  7.1 6.5 %collective-permute-start.4 = (f32[4,32,128]{2,1,0:T(8,128)S(1)}, f32[4,32,128]{2,1,0:T(8,128)S(1)}, u32[]{:S(2)}, u32[]{:S(2)}) collective-permute-start(f32[4,32,128]{2,1,0:T(8,128)S(1)} %get-tuple-element.70), channel_id=1, source_target_pairs={{4,8},{8,4},{5,9},{9,5},{6,10},{10,6},{7,11},{11,7},{20,24},{24,20... | collective-permute-start | bytes 196616 | tf_op jit(solution)/shard_map/ppermute | solution.py:335
  13.7 2.8 %copy-start.1 = (f32[4,96,32,128]{3,2,1,0:T(8,128)S(1)}, f32[4,96,32,128]{3,2,1,0:T(8,128)}, u32[]{:S(2)}) copy-start(f32[4,96,32,128]{3,2,1,0:T(8,128)} %refs_10_.7) | copy-start | bytes 18874372
  22.7 35.6 %collective-permute-start.7 = (f32[96,32,128]{2,1,0:T(8,128)S(1)}, f32[96,32,128]{2,1,0:T(8,128)S(1)}, u32[]{:S(2)}, u32[]{:S(2)}) collective-permute-start(f32[96,32,128]{2,1,0:T(8,128)S(1)} %get-tuple-element.81.refs_3_), channel_id=1, source_target_pairs={{0,16},{16,0},{32,48},{48,32},{64,80},{80,64},{96,112},{112,96},{1... | collective-permute-start | bytes 4718600 | tf_op jit(solution)/shard_map/ppermute | solution.py:332
  22.8 35.5 %slice-start = ((s8[6291456]{0:T(1024)(128)(4,1)}), s8[4194304]{0:T(1024)(128)(4,1)S(1)}, s32[]{:S(2)}) async-start(s8[6291456]{0:T(1024)(128)(4,1)} %bitcast), calls=%async_computation | async-start | bytes 8388608
  24.4 17.7 %collective-permute-start.6 = (f32[72,32,128]{2,1,0:T(8,128)S(1)}, f32[72,32,128]{2,1,0:T(8,128)S(1)}, u32[]{:S(2)}, u32[]{:S(2)}) collective-permute-start(f32[72,32,128]{2,1,0:T(8,128)S(1)} %get-tuple-element.73), channel_id=1, source_target_pairs={{16,32},{32,16},{48,64},{64,48},{80,96},{96,80},{17,33},{33,17},{4... | collective-permute-start | bytes 3538952 | tf_op jit(solution)/shard_map/ppermute | solution.py:329
  27.3 18.9 %collective-permute-start.5 = (f32[24,32,128]{2,1,0:T(8,128)S(1)}, f32[24,32,128]{2,1,0:T(8,128)S(1)}, u32[]{:S(2)}, u32[]{:S(2)}) collective-permute-start(f32[24,32,128]{2,1,0:T(8,128)S(1)} %get-tuple-element.72), channel_id=1, source_target_pairs={{16,32},{32,16},{48,64},{64,48},{80,96},{96,80},{17,33},{33,17},{4... | collective-permute-start | bytes 1179656 | tf_op jit(solution)/shard_map/ppermute | solution.py:329
  42.0 16.3 %slice-start.1 = ((s8[6291456]{0:T(1024)(128)(4,1)}), s8[2097152]{0:T(1024)(128)(4,1)S(1)}, s32[]{:S(2)}) async-start(s8[6291456]{0:T(1024)(128)(4,1)} %bitcast), calls=%async_computation.1 | async-start | bytes 4194304
  46.5 11.8 %collective-permute-start.8 = (f32[4,96,128]{2,1,0:T(8,128)S(1)}, f32[4,96,128]{2,1,0:T(8,128)S(1)}, u32[]{:S(2)}, u32[]{:S(2)}) collective-permute-start(f32[4,96,128]{2,1,0:T(8,128)S(1)} %get-tuple-element.82), channel_id=1, source_target_pairs={{0,1},{1,0},{2,3},{3,2},{4,5},{5,4},{6,7},{7,6},{8,9},{9,8},{10,11... | collective-permute-start | bytes 589832 | tf_op jit(solution)/shard_map/ppermute | solution.py:335
  51.4 6.9 %collective-permute-start.9 = (f32[4,96,128]{2,1,0:T(8,128)S(1)}, f32[4,96,128]{2,1,0:T(8,128)S(1)}, u32[]{:S(2)}, u32[]{:S(2)}) collective-permute-start(f32[4,96,128]{2,1,0:T(8,128)S(1)} %get-tuple-element.83), channel_id=1, source_target_pairs={{1,2},{2,1},{5,6},{6,5},{9,10},{10,9},{13,14},{14,13},{17,18},{18,... | collective-permute-start | bytes 589832 | tf_op jit(solution)/shard_map/ppermute | solution.py:335
  52.1 4.3 %collective-permute-start.10 = (f32[4,32,128]{2,1,0:T(8,128)S(1)}, f32[4,32,128]{2,1,0:T(8,128)S(1)}, u32[]{:S(2)}, u32[]{:S(2)}) collective-permute-start(f32[4,32,128]{2,1,0:T(8,128)S(1)} %get-tuple-element.84), channel_id=1, source_target_pairs={{0,4},{4,0},{8,12},{12,8},{1,5},{5,1},{9,13},{13,9},{2,6},{6,2},{1... | collective-permute-start | bytes 196616 | tf_op jit(solution)/shard_map/ppermute | solution.py:335
  52.2 6.2 %collective-permute-start.11 = (f32[4,32,128]{2,1,0:T(8,128)S(1)}, f32[4,32,128]{2,1,0:T(8,128)S(1)}, u32[]{:S(2)}, u32[]{:S(2)}) collective-permute-start(f32[4,32,128]{2,1,0:T(8,128)S(1)} %get-tuple-element.85), channel_id=1, source_target_pairs={{4,8},{8,4},{5,9},{9,5},{6,10},{10,6},{7,11},{11,7},{20,24},{24,20... | collective-permute-start | bytes 196616 | tf_op jit(solution)/shard_map/ppermute | solution.py:335
  63.2 31.1 %collective-permute-start.14 = (f32[96,32,128]{2,1,0:T(8,128)S(1)}, f32[96,32,128]{2,1,0:T(8,128)S(1)}, u32[]{:S(2)}, u32[]{:S(2)}) collective-permute-start(f32[96,32,128]{2,1,0:T(8,128)S(1)} %get-tuple-element.96.refs_3_), channel_id=1, source_target_pairs={{0,16},{16,0},{32,48},{48,32},{64,80},{80,64},{96,112},{112,96},{1... | collective-permute-start | bytes 4718600 | tf_op jit(solution)/shard_map/ppermute | solution.py:332
  63.3 17.5 %collective-permute-start.13 = (f32[72,32,128]{2,1,0:T(8,128)S(1)}, f32[72,32,128]{2,1,0:T(8,128)S(1)}, u32[]{:S(2)}, u32[]{:S(2)}) collective-permute-start(f32[72,32,128]{2,1,0:T(8,128)S(1)} %shard_map.62.refs_3_), channel_id=1, source_target_pairs={{16,32},{32,16},{48,64},{64,48},{80,96},{96,80},{17,33},{33,17},{4... | collective-permute-start | bytes 3538952 | tf_op jit(solution)/shard_map/ppermute | solution.py:329
  66.3 18.7 %collective-permute-start.12 = (f32[24,32,128]{2,1,0:T(8,128)S(1)}, f32[24,32,128]{2,1,0:T(8,128)S(1)}, u32[]{:S(2)}, u32[]{:S(2)}) collective-permute-start(f32[24,32,128]{2,1,0:T(8,128)S(1)} %get-tuple-element.88), channel_id=1, source_target_pairs={{16,32},{32,16},{48,64},{64,48},{80,96},{96,80},{17,33},{33,17},{4... | collective-permute-start | bytes 1179656 | tf_op jit(solution)/shard_map/ppermute | solution.py:329
  85.3 8.9 %collective-permute-start.15 = (f32[4,96,128]{2,1,0:T(8,128)S(1)}, f32[4,96,128]{2,1,0:T(8,128)S(1)}, u32[]{:S(2)}, u32[]{:S(2)}) collective-permute-start(f32[4,96,128]{2,1,0:T(8,128)S(1)} %get-tuple-element.97), channel_id=1, source_target_pairs={{0,1},{1,0},{2,3},{3,2},{4,5},{5,4},{6,7},{7,6},{8,9},{9,8},{10,11... | collective-permute-start | bytes 589832 | tf_op jit(solution)/shard_map/ppermute | solution.py:335
  87.3 6.9 %collective-permute-start.16 = (f32[4,96,128]{2,1,0:T(8,128)S(1)}, f32[4,96,128]{2,1,0:T(8,128)S(1)}, u32[]{:S(2)}, u32[]{:S(2)}) collective-permute-start(f32[4,96,128]{2,1,0:T(8,128)S(1)} %get-tuple-element.98), channel_id=1, source_target_pairs={{1,2},{2,1},{5,6},{6,5},{9,10},{10,9},{13,14},{14,13},{17,18},{18,... | collective-permute-start | bytes 589832 | tf_op jit(solution)/shard_map/ppermute | solution.py:335
  88.0 4.3 %collective-permute-start.17 = (f32[4,32,128]{2,1,0:T(8,128)S(1)}, f32[4,32,128]{2,1,0:T(8,128)S(1)}, u32[]{:S(2)}, u32[]{:S(2)}) collective-permute-start(f32[4,32,128]{2,1,0:T(8,128)S(1)} %get-tuple-element.99), channel_id=1, source_target_pairs={{0,4},{4,0},{8,12},{12,8},{1,5},{5,1},{9,13},{13,9},{2,6},{6,2},{1... | collective-permute-start | bytes 196616 | tf_op jit(solution)/shard_map/ppermute | solution.py:335
  88.1 6.2 %collective-permute-start.18 = (f32[4,32,128]{2,1,0:T(8,128)S(1)}, f32[4,32,128]{2,1,0:T(8,128)S(1)}, u32[]{:S(2)}, u32[]{:S(2)}) collective-permute-start(f32[4,32,128]{2,1,0:T(8,128)S(1)} %get-tuple-element.100), channel_id=1, source_target_pairs={{4,8},{8,4},{5,9},{9,5},{6,10},{10,6},{7,11},{11,7},{20,24},{24,20... | collective-permute-start | bytes 196616 | tf_op jit(solution)/shard_map/ppermute | solution.py:335
  99.0 35.6 %collective-permute-start.21 = (f32[96,32,128]{2,1,0:T(8,128)S(1)}, f32[96,32,128]{2,1,0:T(8,128)S(1)}, u32[]{:S(2)}, u32[]{:S(2)}) collective-permute-start(f32[96,32,128]{2,1,0:T(8,128)S(1)} %get-tuple-element.110.refs_3_), channel_id=1, source_target_pairs={{0,16},{16,0},{32,48},{48,32},{64,80},{80,64},{96,112},{112,96},{1... | collective-permute-start | bytes 4718600 | tf_op jit(solution)/shard_map/ppermute | solution.py:332
  99.1 17.5 %collective-permute-start.20 = (f32[72,32,128]{2,1,0:T(8,128)S(1)}, f32[72,32,128]{2,1,0:T(8,128)S(1)}, u32[]{:S(2)}, u32[]{:S(2)}) collective-permute-start(f32[72,32,128]{2,1,0:T(8,128)S(1)} %shard_map.65.refs_3_), channel_id=1, source_target_pairs={{16,32},{32,16},{48,64},{64,48},{80,96},{96,80},{17,33},{33,17},{4... | collective-permute-start | bytes 3538952 | tf_op jit(solution)/shard_map/ppermute | solution.py:329
  102.5 18.4 %collective-permute-start.19 = (f32[24,32,128]{2,1,0:T(8,128)S(1)}, f32[24,32,128]{2,1,0:T(8,128)S(1)}, u32[]{:S(2)}, u32[]{:S(2)}) collective-permute-start(f32[24,32,128]{2,1,0:T(8,128)S(1)} %get-tuple-element.102), channel_id=1, source_target_pairs={{16,32},{32,16},{48,64},{64,48},{80,96},{96,80},{17,33},{33,17},{4... | collective-permute-start | bytes 1179656 | tf_op jit(solution)/shard_map/ppermute | solution.py:329
  121.2 13.5 %collective-permute-start.22 = (f32[4,96,128]{2,1,0:T(8,128)S(1)}, f32[4,96,128]{2,1,0:T(8,128)S(1)}, u32[]{:S(2)}, u32[]{:S(2)}) collective-permute-start(f32[4,96,128]{2,1,0:T(8,128)S(1)} %get-tuple-element.111), channel_id=1, source_target_pairs={{0,1},{1,0},{2,3},{3,2},{4,5},{5,4},{6,7},{7,6},{8,9},{9,8},{10,11... | collective-permute-start | bytes 589832 | tf_op jit(solution)/shard_map/ppermute | solution.py:335
  123.9 10.8 %collective-permute-start.23 = (f32[4,96,128]{2,1,0:T(8,128)S(1)}, f32[4,96,128]{2,1,0:T(8,128)S(1)}, u32[]{:S(2)}, u32[]{:S(2)}) collective-permute-start(f32[4,96,128]{2,1,0:T(8,128)S(1)} %get-tuple-element.112), channel_id=1, source_target_pairs={{1,2},{2,1},{5,6},{6,5},{9,10},{10,9},{13,14},{14,13},{17,18},{18,... | collective-permute-start | bytes 589832 | tf_op jit(solution)/shard_map/ppermute | solution.py:335
  124.5 4.3 %collective-permute-start.24 = (f32[4,32,128]{2,1,0:T(8,128)S(1)}, f32[4,32,128]{2,1,0:T(8,128)S(1)}, u32[]{:S(2)}, u32[]{:S(2)}) collective-permute-start(f32[4,32,128]{2,1,0:T(8,128)S(1)} %get-tuple-element.113), channel_id=1, source_target_pairs={{0,4},{4,0},{8,12},{12,8},{1,5},{5,1},{9,13},{13,9},{2,6},{6,2},{1... | collective-permute-start | bytes 196616 | tf_op jit(solution)/shard_map/ppermute | solution.py:335
  124.6 6.4 %collective-permute-start.25 = (f32[4,32,128]{2,1,0:T(8,128)S(1)}, f32[4,32,128]{2,1,0:T(8,128)S(1)}, u32[]{:S(2)}, u32[]{:S(2)}) collective-permute-start(f32[4,32,128]{2,1,0:T(8,128)S(1)} %get-tuple-element.114), channel_id=1, source_target_pairs={{4,8},{8,4},{5,9},{9,5},{6,10},{10,6},{7,11},{11,7},{20,24},{24,20... | collective-permute-start | bytes 196616 | tf_op jit(solution)/shard_map/ppermute | solution.py:335
  128.9 17.5 %collective-permute-start.27 = (f32[72,32,128]{2,1,0:T(8,128)S(1)}, f32[72,32,128]{2,1,0:T(8,128)S(1)}, u32[]{:S(2)}, u32[]{:S(2)}) collective-permute-start(f32[72,32,128]{2,1,0:T(8,128)S(1)} %shard_map.68.refs_3_), channel_id=1, source_target_pairs={{16,32},{32,16},{48,64},{64,48},{80,96},{96,80},{17,33},{33,17},{4... | collective-permute-start | bytes 3538952 | tf_op jit(solution)/shard_map/ppermute | solution.py:329
  131.0 19.6 %collective-permute-start.26 = (f32[24,32,128]{2,1,0:T(8,128)S(1)}, f32[24,32,128]{2,1,0:T(8,128)S(1)}, u32[]{:S(2)}, u32[]{:S(2)}) collective-permute-start(f32[24,32,128]{2,1,0:T(8,128)S(1)} %get-tuple-element.116), channel_id=1, source_target_pairs={{16,32},{32,16},{48,64},{64,48},{80,96},{96,80},{17,33},{33,17},{4... | collective-permute-start | bytes 1179656 | tf_op jit(solution)/shard_map/ppermute | solution.py:329
  140.4 12.9 %collective-permute-start.33 = (f32[6,32,128]{2,1,0:T(8,128)S(1)}, f32[6,32,128]{2,1,0:T(8,128)S(1)}, u32[]{:S(2)}, u32[]{:S(2)}) collective-permute-start(f32[6,32,128]{2,1,0:T(8,128)S(1)} %get-tuple-element.122.refs_3_), channel_id=1, source_target_pairs={{0,12},{4,8},{8,4},{12,0},{1,13},{5,9},{9,5},{13,1},{2,14},{6,10},... | collective-permute-start | bytes 294920 | tf_op jit(solution)/shard_map/ppermute | solution.py:348
  142.5 12.9 %collective-permute-start.32 = (f32[6,32,128]{2,1,0:T(8,128)S(1)}, f32[6,32,128]{2,1,0:T(8,128)S(1)}, u32[]{:S(2)}, u32[]{:S(2)}) collective-permute-start(f32[6,32,128]{2,1,0:T(8,128)S(1)} %get-tuple-element.122.refs_3_), channel_id=1, source_target_pairs={{0,8},{4,12},{8,0},{12,4},{1,9},{5,13},{9,1},{13,5},{2,10},{6,14},... | collective-permute-start | bytes 294920 | tf_op jit(solution)/shard_map/ppermute | solution.py:348
  142.5 12.9 %collective-permute-start.31 = (f32[6,32,128]{2,1,0:T(8,128)S(1)}, f32[6,32,128]{2,1,0:T(8,128)S(1)}, u32[]{:S(2)}, u32[]{:S(2)}) collective-permute-start(f32[6,32,128]{2,1,0:T(8,128)S(1)} %get-tuple-element.122.refs_3_), channel_id=1, source_target_pairs={{0,4},{4,0},{8,12},{12,8},{1,5},{5,1},{9,13},{13,9},{2,6},{6,2},{1... | collective-permute-start | bytes 294920 | tf_op jit(solution)/shard_map/ppermute | solution.py:348
  151.1 6.6 %collective-permute-start.30 = (f32[2,32,128]{2,1,0:T(8,128)S(1)}, f32[2,32,128]{2,1,0:T(8,128)S(1)}, u32[]{:S(2)}, u32[]{:S(2)}) collective-permute-start(f32[2,32,128]{2,1,0:T(8,128)S(1)} %get-tuple-element.118.refs_1_), channel_id=1, source_target_pairs={{0,12},{4,8},{8,4},{12,0},{1,13},{5,9},{9,5},{13,1},{2,14},{6,10},... | collective-permute-start | bytes 98312 | tf_op jit(solution)/shard_map/ppermute | solution.py:348
  153.2 5.4 %collective-permute-start.29 = (f32[2,32,128]{2,1,0:T(8,128)S(1)}, f32[2,32,128]{2,1,0:T(8,128)S(1)}, u32[]{:S(2)}, u32[]{:S(2)}) collective-permute-start(f32[2,32,128]{2,1,0:T(8,128)S(1)} %get-tuple-element.118.refs_1_), channel_id=1, source_target_pairs={{0,8},{4,12},{8,0},{12,4},{1,9},{5,13},{9,1},{13,5},{2,10},{6,14},... | collective-permute-start | bytes 98312 | tf_op jit(solution)/shard_map/ppermute | solution.py:348
  153.3 5.4 %collective-permute-start.28 = (f32[2,32,128]{2,1,0:T(8,128)S(1)}, f32[2,32,128]{2,1,0:T(8,128)S(1)}, u32[]{:S(2)}, u32[]{:S(2)}) collective-permute-start(f32[2,32,128]{2,1,0:T(8,128)S(1)} %get-tuple-element.118.refs_1_), channel_id=1, source_target_pairs={{0,4},{4,0},{8,12},{12,8},{1,5},{5,1},{9,13},{13,9},{2,6},{6,2},{1... | collective-permute-start | bytes 98312 | tf_op jit(solution)/shard_map/ppermute | solution.py:348
